TPU v7x, 8 devices: a whole 2x2x1 slice. The times are simulated.
8 devices in a mesh: tp: 4 (over z, y, x), cp: 2 (over core).
Axes of the slice: x: 2, y: 2, z: 1, core: 2. Of those that a mesh axis runs over, the one named last changes fastest.
Arguments:
- x_in: bfloat16 [32, 256, 4096], P(None, 'cp')
- grad_z: bfloat16 [32, 256, 4096], P(None, 'cp')
- seg_pos: int32 [32, 256], P(None, 'cp')
- norm_scale: bfloat16 [4096], replicated
- w_x: bfloat16 [4096, 4096], P(None, 'tp')
- b_x: bfloat16 [4096], P('tp')
- w_y: bfloat16 [4096, 4096], P(None, 'tp')
- b_y: bfloat16 [4096], P('tp')
- conv_w: bfloat16 [4, 4096], P(None, 'tp')
- conv_b: bfloat16 [4096], P('tp')
- w_a: bfloat16 [32, 128, 128], P('tp')
- b_a: bfloat16 [4096], P('tp')
- w_i: bfloat16 [32, 128, 128], P('tp')
- b_i: bfloat16 [4096], P('tp')
- a_param: float32 [4096], P('tp')
- w_out: bfloat16 [4096, 4096], P('tp')
- b_out: bfloat16 [4096], replicated
Outputs:
- output 1: bfloat16 [32, 256, 4096], P(None, 'cp')
- output 2: bfloat16 [32, 256, 4096], P(None, 'cp')
- output 3: float32 [4096], replicated
- output 4: float32 [4096, 4096], P(None, 'tp')
- output 5: float32 [4096], P('tp')
- output 6: float32 [4096, 4096], P(None, 'tp')
- output 7: float32 [4096], P('tp')
- output 8: float32 [4, 4096], P(None, 'tp')
- output 9: float32 [4096], P('tp')
- output 10: float32 [32, 128, 128], P('tp')
- output 11: float32 [4096], P('tp')
- output 12: float32 [32, 128, 128], P('tp')
- output 13: float32 [4096], P('tp')
- output 14: float32 [4096], P('tp')
- output 15: float32 [4096, 4096], P('tp')
- output 16: float32 [4096], replicated
All inputs are finite; a program needn't handle non-finite values.
Results may differ from a plain program's by a relative error of at most 0.00859572.
Values sent between devices are 32-bit elements.
A program may use at most 1 GiB of HBM per device.

v0:
```python
import functools
import jax
import jax.numpy as jnp
from jax import lax
from jax.sharding import PartitionSpec as P

NORM_EPS = 1e-6
CONV_WIDTH = 4
BORROW_ROWS = CONV_WIDTH - 1
IN_SPECS = (P(None, "cp", None), P(None, "cp", None), P(None, "cp"), P(), P(None, "tp"), P("tp"), P(None, "tp"), P("tp"), P(None, "tp"), P("tp"), P("tp", None, None), P("tp"), P("tp", None, None), P("tp"), P("tp"), P("tp", None), P())
OUT_SPECS = (P(None, "cp", None), P(None, "cp", None), P(), P(None, "tp"), P("tp"), P(None, "tp"), P("tp"), P(None, "tp"), P("tp"), P("tp", None, None), P("tp"), P("tp", None, None), P("tp"), P("tp"), P("tp", None), P())


def norm_apply(x_f, scale_f):
    mean_sq = jnp.mean(x_f * x_f, axis=-1, keepdims=True)
    return x_f * lax.rsqrt(mean_sq + NORM_EPS) * (1.0 + scale_f)


def gelu_tanh(pre_y):
    return jax.nn.gelu(pre_y, approximate=True)


def gate_math(pre_a, pre_i, conv_f, a_param, reset_mask):
    log_a = -8.0 * jax.nn.sigmoid(pre_a) * jax.nn.softplus(a_param)
    decays = jnp.where(reset_mask, 0.0, jnp.exp(log_a))
    multiplier = jnp.where(reset_mask, 1.0, jnp.sqrt(-jnp.expm1(2.0 * log_a)))
    return decays, multiplier * jax.nn.sigmoid(pre_i) * conv_f


def conv_apply(xb_ext, conv_w, conv_b, pos_t):
    n_rows = pos_t.shape[0]
    conv_wf = conv_w.astype(jnp.float32)
    conv_sum = conv_b.astype(jnp.float32)
    for tap_k in range(CONV_WIDTH):
        start_row = BORROW_ROWS - tap_k
        keep_mask = (pos_t >= tap_k)[:, :, None]
        conv_sum = conv_sum + jnp.where(keep_mask, xb_ext[start_row:start_row + n_rows], 0.0) * conv_wf[tap_k]
    return conv_sum


def conv_back(grad_conv, xb_ext, conv_w, pos_t):
    n_rows = pos_t.shape[0]
    conv_wf = conv_w.astype(jnp.float32)
    grad_ext = 0.0
    tap_grads = []
    for tap_k in range(CONV_WIDTH):
        start_row = BORROW_ROWS - tap_k
        masked = jnp.where((pos_t >= tap_k)[:, :, None], grad_conv, 0.0)
        tap_grads.append(jnp.sum(masked * xb_ext[start_row:start_row + n_rows], axis=(0, 1)))
        grad_ext = grad_ext + jnp.pad(masked * conv_wf[tap_k], ((start_row, tap_k), (0, 0), (0, 0)))
    return grad_ext, jnp.stack(tap_grads), jnp.sum(grad_conv, axis=(0, 1))


def local_scan(decays, drives):
    def scan_step(carry_in, inputs_t):
        state_h, prod_a = carry_in
        state_h = inputs_t[0] * state_h + inputs_t[1]
        prod_a = inputs_t[0] * prod_a
        return (state_h, prod_a), (state_h, prod_a)
    zeros_h = jnp.zeros(decays.shape[1:], jnp.float32)
    _, (states, run_prods) = lax.scan(scan_step, (zeros_h, jnp.ones_like(zeros_h)), (decays, drives))
    return states, run_prods


def local_scan_back(decays, grad_out):
    def scan_step(carry_in, inputs_t):
        next_grad, prod_a = carry_in
        grad_h = inputs_t[1] + next_grad
        return (inputs_t[0] * grad_h, inputs_t[0] * prod_a), (grad_h, prod_a)
    zeros_h = jnp.zeros(decays.shape[1:], jnp.float32)
    (head_grad, total_prod), (grad_loc, suffix_prods) = lax.scan(scan_step, (zeros_h, jnp.ones_like(zeros_h)), (decays, grad_out), reverse=True)
    return grad_loc, suffix_prods, head_grad, total_prod


def carry_in_forward(end_info, cp_index):
    def compose(carry_in, piece_info):
        return piece_info[0] * carry_in + piece_info[1], carry_in
    _, entering = lax.scan(compose, jnp.zeros_like(end_info[0, 0]), end_info)
    return lax.dynamic_index_in_dim(entering, cp_index, 0, keepdims=False)


def carry_in_backward(head_info, cp_index):
    def compose(carry_in, piece_info):
        return piece_info[0] * carry_in + piece_info[1], carry_in
    _, entering = lax.scan(compose, jnp.zeros_like(head_info[0, 0]), head_info, reverse=True)
    return lax.dynamic_index_in_dim(entering, cp_index, 0, keepdims=False)


def shard_body(x_in, grad_z, seg_pos, norm_scale, w_x, b_x, w_y, b_y, conv_w, conv_b, w_a, b_a, w_i, b_i, a_param, w_out, b_out, fwd_perm, back_perm):
    cp_index = lax.axis_index("cp")
    n_tok = x_in.shape[1]
    n_blocks, blk_width = w_a.shape[0], w_a.shape[1]
    x_f = x_in.astype(jnp.float32)
    normed_f, norm_pull = jax.vjp(norm_apply, x_f, norm_scale.astype(jnp.float32))
    normed = normed_f.astype(jnp.bfloat16)
    pre_y = jnp.einsum("btd,dl->tbl", normed, w_y, preferred_element_type=jnp.float32) + b_y
    y_act, gelu_pull = jax.vjp(gelu_tanh, pre_y)
    x_branch = (jnp.einsum("btd,dl->tbl", normed, w_x, preferred_element_type=jnp.float32) + b_x).astype(jnp.bfloat16).astype(jnp.float32)
    borrowed = lax.ppermute(x_branch[n_tok - BORROW_ROWS:], "cp", fwd_perm)
    xb_ext = jnp.concatenate([borrowed, x_branch], axis=0)
    pos_t = seg_pos.T
    conv_out = conv_apply(xb_ext, conv_w, conv_b, pos_t).astype(jnp.bfloat16)
    blocks = conv_out.reshape(conv_out.shape[0], conv_out.shape[1], n_blocks, blk_width)
    pre_a = jnp.einsum("tbhk,hkj->tbhj", blocks, w_a, preferred_element_type=jnp.float32).reshape(conv_out.shape) + b_a
    pre_i = jnp.einsum("tbhk,hkj->tbhj", blocks, w_i, preferred_element_type=jnp.float32).reshape(conv_out.shape) + b_i
    gate_fn = functools.partial(gate_math, reset_mask=(pos_t == 0)[:, :, None])
    (decays, drives), gate_pull = jax.vjp(gate_fn, pre_a, pre_i, conv_out.astype(jnp.float32), a_param)
    states, run_prods = local_scan(decays, drives)
    end_info = lax.all_gather(jnp.stack([run_prods[-1], states[-1]]), "cp")
    state_in = carry_in_forward(end_info, cp_index)
    hidden = states + run_prods * state_in
    prev_hidden = jnp.concatenate([state_in[None], hidden[:-1]], axis=0)
    mixed_v = (hidden * y_act).astype(jnp.bfloat16)
    out_part = jnp.einsum("tbl,ld->btd", mixed_v, w_out, preferred_element_type=jnp.float32)
    out_proj = lax.psum(out_part, "tp") + b_out
    z_out = (x_f + out_proj).astype(jnp.bfloat16)

    d_mixed = jnp.einsum("btd,ld->tbl", grad_z, w_out, preferred_element_type=jnp.float32)
    g_w_out = jnp.einsum("tbl,btd->ld", mixed_v, grad_z, preferred_element_type=jnp.float32)
    g_b_out = jnp.sum(grad_z, axis=(0, 1), dtype=jnp.float32)
    d_pre_y = gelu_pull(d_mixed * hidden)[0]
    grad_loc, suffix_prods, head_grad, total_prod = local_scan_back(decays, d_mixed * y_act)
    head_info = lax.all_gather(jnp.stack([total_prod, head_grad]), "cp")
    grad_in = carry_in_backward(head_info, cp_index)
    d_hidden = grad_loc + suffix_prods * grad_in
    d_pre_a, d_pre_i, d_conv_f, g_a_param = gate_pull((d_hidden * prev_hidden, d_hidden))
    d_pre_a16 = d_pre_a.astype(jnp.bfloat16).reshape(blocks.shape)
    d_pre_i16 = d_pre_i.astype(jnp.bfloat16).reshape(blocks.shape)
    g_w_a = jnp.einsum("tbhk,tbhj->hkj", blocks, d_pre_a16, preferred_element_type=jnp.float32)
    g_w_i = jnp.einsum("tbhk,tbhj->hkj", blocks, d_pre_i16, preferred_element_type=jnp.float32)
    d_gate_in = jnp.einsum("tbhj,hkj->tbhk", d_pre_a16, w_a, preferred_element_type=jnp.float32) + jnp.einsum("tbhj,hkj->tbhk", d_pre_i16, w_i, preferred_element_type=jnp.float32)
    d_conv = d_conv_f + d_gate_in.reshape(conv_out.shape)
    grad_ext, g_conv_w, g_conv_b = conv_back(d_conv, xb_ext, conv_w, pos_t)
    returned = lax.ppermute(grad_ext[:BORROW_ROWS], "cp", back_perm)
    d_branch = jnp.concatenate([grad_ext[BORROW_ROWS:n_tok], grad_ext[n_tok:] + returned], axis=0)
    d_branch16 = d_branch.astype(jnp.bfloat16)
    d_pre_y16 = d_pre_y.astype(jnp.bfloat16)
    g_w_x = jnp.einsum("btd,tbl->dl", normed, d_branch16, preferred_element_type=jnp.float32)
    g_w_y = jnp.einsum("btd,tbl->dl", normed, d_pre_y16, preferred_element_type=jnp.float32)
    d_norm_part = jnp.einsum("tbl,dl->btd", d_branch16, w_x, preferred_element_type=jnp.float32) + jnp.einsum("tbl,dl->btd", d_pre_y16, w_y, preferred_element_type=jnp.float32)
    d_normed = lax.psum(d_norm_part, "tp")
    d_x_norm, g_scale = norm_pull(d_normed)
    grad_x = (grad_z.astype(jnp.float32) + d_x_norm).astype(jnp.bfloat16)
    grad_sums = lax.psum((g_scale, g_w_x, jnp.sum(d_branch, axis=(0, 1)), g_w_y, jnp.sum(d_pre_y, axis=(0, 1)), g_conv_w, g_conv_b, g_w_a, jnp.sum(d_pre_a, axis=(0, 1)), g_w_i, jnp.sum(d_pre_i, axis=(0, 1)), g_a_param, g_w_out, g_b_out), "cp")
    return (z_out, grad_x) + tuple(grad_sums)


def solution(mesh):
    cp_size = mesh.shape["cp"]
    fwd_perm = [(dev_j, dev_j + 1) for dev_j in range(cp_size - 1)]
    back_perm = [(dev_j + 1, dev_j) for dev_j in range(cp_size - 1)]
    per_device = functools.partial(shard_body, fwd_perm=fwd_perm, back_perm=back_perm)
    return jax.shard_map(per_device, mesh=mesh, in_specs=IN_SPECS, out_specs=OUT_SPECS, check_vma=False)
```

profile of v0, /device:TPU:0, one launch (start us, length us, event | category | flops | bytes accessed | tf_op | source)
XLA Modules:
  0.0 4902.1 jit_solution(3739890068777665958)
XLA Ops:
  7.3 11.3 fusion.12
  19.3 42.7 add_convert_fusion.1
  62.0 11.4 convert_bitcast_fusion
  78.6 43.3 fusion.36
  122.5 49.1 %bitcast_multiply_fusion.5 = (f32[128,32,1024]{2,0,1:T(8,128)}, f32[1024,32,128]{0,2,1:T(8,128)}) fusion(f32[32,128,1024]{2,1,0:T(8,128)} %fusion.36, f32[1024]{0:T(1024)S(1)} %convert_element_type.91, bf16[32,128,4096]{2,1,0:T(8,128)(2,1)} %param.26, bf16[1024,4096]{1,0:T(8,128)(2,1)} %param.40), kind=kOutput, calls=%fused_computation.69 | convolution fusion | flops 34401681408 | bytes 92278784 | tf_op jit(solution)/shard_map/btd,ld->tbl/dot_general | solution.py:118
  172.3 34.9 add_convert_fusion
  207.3 8.9 copy.134
  216.2 12.4 copy.86
  228.6 11.5 convolution_bitcast_fusion.3
  240.1 17.5 copy.64
  257.6 18.0 reshape.98
  275.6 9.5 exponential_select_fusion
  285.1 19.5 copy.70
  304.6 8.0 broadcast.107
  312.6 7.9 broadcast.107.clone.1
  320.5 1278.5 %while.70 = (s32[]{:T(128)}, f32[32,1024]{1,0:T(8,128)S(1)}, f32[32,1024]{1,0:T(8,128)S(1)}, f32[128,32,1024]{2,0,1:T(8,128)}, f32[128,32,1024]{2,0,1:T(8,128)},...) while((s32[]{:T(128)}, f32[32,1024]{1,0:T(8,128)S(1)}, ...), condition=%wide.region_7.8_spmd.clone, body=%wide.region_6.7_spmd.clone.sunk | while | flops 163844 | bytes 2359435 | solution.py:71
  806.1 3.7 dynamic_update_slice.54
  816.2 3.7 dynamic_update_slice.54
  826.3 3.7 dynamic_update_slice.54
  836.4 3.7 dynamic_update_slice.54
  846.5 3.7 dynamic_update_slice.54
  963.2 3.8 dynamic_update_slice.55
  973.3 3.8 dynamic_update_slice.55
  983.4 3.8 dynamic_update_slice.55
  993.5 3.8 dynamic_update_slice.55
  1003.6 3.8 dynamic_update_slice.55
  1013.7 3.8 dynamic_update_slice.55
  1023.8 3.8 dynamic_update_slice.55
  1033.9 3.8 dynamic_update_slice.55
  1601.5 11.9 convolution_bitcast_fusion.2
  1613.4 17.5 copy.67
  1630.9 18.0 reshape.99
  1649.0 44.4 fusion.85
  1693.3 393.1 %while.68 = (s32[]{:T(128)}, f32[32,1024]{1,0:T(8,128)S(1)}, f32[32,1024]{1,0:T(8,128)S(1)}, f32[128,32,1024]{2,1,0:T(8,128)}, f32[128,32,1024]{2,1,0:T(8,128)},...) while((s32[]{:T(128)}, f32[32,1024]{1,0:T(8,128)S(1)}, ...), condition=%wide.region_2.3_spmd.clone, body=%wide.region_1.2_spmd.clone.sunk | while | flops 163843 | bytes 1311339 | solution.py:61
  2093.3 43.0 fusion.88
  2136.3 39.2 multiply_reduce_fusion
  2175.5 15.4 convert_bitcast_fusion.2
  2190.9 11.9 fusion.50
  2202.8 16.0 add_bitcast_fusion.1
  2218.7 17.5 copy.83
  2236.2 18.0 reshape.102
  2254.3 51.1 %fusion.83 = (f32[1024]{0:T(1024)}, f32[1024]{0:T(1024)}, f32[1024]{0:T(1024)}, f32[1024]{0:T(1024)}, f32[1024]{0:T(1024)}, /*index=5*/f32[128,32,1024]{2,0,1:T(8,128)}) fusion(bf16[32,128,1024]{2,1,0:T(8,128)(2,1)} %add_convert_fusion.1, pred[128,32]{0,1:T(8,128)(4,1)S(1)} %copy-done.27, f32[128,32,1024]{2,0,1:T(8,128)} %convert_bitcast_fusion, ...), kind=kLoop, calls=%fused_computation.165 | loop fusion | flops 134212608 | bytes 109498368 | tf_op jit(solution)/shard_map/reduce_sum | solution.py:51
  2305.4 27.0 select_multiply_fusion.3
  2336.0 45.8 fusion.55
  2381.7 30.0 pad_add_fusion
  2411.7 10.3 slice.136
  2424.9 61.1 %add_bitcast_fusion = f32[32,128,4096]{2,1,0:T(8,128)} fusion(f32[128,32,4096]{2,0,1:T(8,128)} %fusion.55, bf16[4096,1024]{1,0:T(8,128)(2,1)} %param.29, bf16[3,32,1024]{2,0,1:T(4,128)(2,1)S(1)} %get-tuple-element.501, bf16[125,32,1024]{2,0,1:T(8,128)(2,1)} %slice.136), kind=kOutput, calls=%fused_computation.40 | convolution fusion | flops 34393292800 | bytes 150994944 | tf_op jit(solution)/shard_map/tbl,dl->btd/dot_general | solution.py:140
  2486.7 15.4 multiply_convert_fusion
  2502.1 45.4 convolution_bitcast_fusion
  2547.8 9.2 fusion.70
  2557.0 9.5 fusion.67
  2566.5 42.5 convolution_bitcast_fusion.1
  2609.1 43.9 fusion.42
  2653.0 45.1 fusion.39
  2700.1 7.9 slice_reduce_fusion
  2708.6 885.4 %all-reduce.13.cloned.1.call-done = f32[32,128,4096]{2,1,0:T(8,128)} async-done(((f32[32,128,4096]{2,1,0:T(8,128)}), f32[32,128,4096]{2,1,0:T(8,128)}) %all-reduce.13.cloned.1.call-update) | async-done | bytes 67108880 | tf_op jit(solution)/shard_map/psum | solution.py:141
  3594.0 32.4 fusion.10
  3626.4 1077.7 %all-reduce.11.cloned.1.call-done = f32[32,128,4096]{2,1,0:T(8,128)} async-done(((f32[32,128,4096]{2,1,0:T(8,128)}), f32[32,128,4096]{2,1,0:T(8,128)}) %all-reduce.11.cloned.1.call-update) | async-done | bytes 67108880 | tf_op jit(solution)/shard_map/psum | solution.py:115
  4704.1 85.4 %convert_reduce_fusion = (f32[4096]{0:T(1024)}, bf16[32,128,4096]{2,1,0:T(8,128)(2,1)}, bf16[32,128,4096]{2,1,0:T(8,128)(2,1)}) fusion(bf16[32,128,4096]{2,1,0:T(8,128)(2,1)} %param.26, f32[32,128]{1,0:T(8,128)S(1)} %multiply_multiply_fusion.2, bf16[32,128,4096]{2,1,0:T(8,128)(2,1)} %param.25, f32[32,128]{1,0:T(8,128)S(1)} %copy-done.21, ...), kind=kLoop, calls=%fused_computation.30 | loop fusion | flops 218099712 | bytes 268517376 | tf_op jit(solution)/shard_map/reduce_sum | solution.py:120
  4789.5 48.9 all-reduce.17.cloned.1.call-done
  4838.4 18.7 all-reduce.15.cloned.1.call-done
  4858.4 13.7 copy.251
  4874.9 8.5 copy.253
  4888.6 6.2 copy.262
  (1237 shorter events, 1657.1 us)
Async XLA Ops:
  7.2 221.4 %copy-start = (bf16[8,128,128]{2,1,0:T(8,128)(2,1)S(1)}, bf16[8,128,128]{2,1,0:T(8,128)(2,1)}, u32[]{:S(2)}) copy-start(bf16[8,128,128]{2,1,0:T(8,128)(2,1)} %param.35) | copy-start | bytes 786436
  7.2 12.0 copy-start.57
  7.2 12.1 copy-start.65
  7.2 3586.8 %all-reduce.13.cloned.1.call-start = ((), (), s32[]{:S(2)}) async-start(), calls=%async_computation.1 | async-start | bytes 134217728 | tf_op jit(solution)/shard_map/psum | solution.py:141
  19.2 59.3 %copy-start.20 = (f32[32,128]{1,0:T(8,128)}, f32[32,128]{1,0:T(8,128)S(1)}, u32[]{:S(2)}) copy-start(f32[32,128]{1,0:T(8,128)S(1)} %fusion.77) | copy-start | bytes 49156
  19.3 59.3 %copy-start.22 = (f32[4096]{0:T(1024)}, f32[4096]{0:T(1024)S(1)}, u32[]{:S(2)}) copy-start(f32[4096]{0:T(1024)S(1)} %convert_add_fusion.2) | copy-start | bytes 49156
  62.0 15.9 copy-start.45
  62.0 15.9 copy-start.66
  62.0 16.0 copy-start.67
  74.8 97.5 %collective-permute-start = (f32[3,32,1024]{2,0,1:T(4,128)S(1)}, f32[3,32,1024]{2,0,1:T(4,128)S(1)}, u32[]{:S(2)}, u32[]{:S(2)}) collective-permute-start(f32[3,32,1024]{2,0,1:T(4,128)S(1)} %slice.96), channel_id=1, source_target_pairs={{0,1},{2,3},{4,5},{6,7}} | collective-permute-start | bytes 1179656 | tf_op jit(solution)/shard_map/ppermute | solution.py:99
  77.9 94.4 %copy-start.35 = (f32[1,1024]{1,0:T(1,128)}, f32[1,1024]{1,0:T(1,128)S(1)}, u32[]{:S(2)}) copy-start(f32[1,1024]{1,0:T(1,128)S(1)} %get-tuple-element.523) | copy-start | bytes 12292
  77.9 94.4 %copy-start.37 = (f32[1,1024]{1,0:T(1,128)}, f32[1,1024]{1,0:T(1,128)S(1)}, u32[]{:S(2)}) copy-start(f32[1,1024]{1,0:T(1,128)S(1)} %get-tuple-element.524) | copy-start | bytes 12292
  77.9 94.4 %copy-start.39 = (f32[1,1024]{1,0:T(1,128)}, f32[1,1024]{1,0:T(1,128)S(1)}, u32[]{:S(2)}) copy-start(f32[1,1024]{1,0:T(1,128)S(1)} %get-tuple-element.525) | copy-start | bytes 12292
  77.9 94.4 %copy-start.41 = (f32[1,1024]{1,0:T(1,128)}, f32[1,1024]{1,0:T(1,128)S(1)}, u32[]{:S(2)}) copy-start(f32[1,1024]{1,0:T(1,128)S(1)} %get-tuple-element.526) | copy-start | bytes 12292
  78.5 43.3 copy-start.68
  78.6 43.3 copy-start.69
  121.9 1971.4 %copy-start.43 = (f32[1024]{0:T(1024)}, f32[1024]{0:T(1024)S(1)}, u32[]{:S(2)}) copy-start(f32[1024]{0:T(1024)S(1)} %convert_element_type.91) | copy-start | bytes 12292
  122.5 49.1 %copy-start.52 = (f32[1024]{0:T(1024)S(1)}, f32[1024]{0:T(1024)}, u32[]{:S(2)}) copy-start(f32[1024]{0:T(1024)} %param.39) | copy-start | bytes 12292
  122.5 49.7 %copy-start.54 = (s32[32,128]{1,0:T(8,128)S(1)}, s32[32,128]{1,0:T(8,128)}, u32[]{:S(2)}) copy-start(s32[32,128]{1,0:T(8,128)} %param.27) | copy-start | bytes 49156
  172.2 43.9 copy-start.26
  172.2 43.9 copy-start.28
  172.2 43.9 copy-start.30
  172.2 43.9 copy-start.32
  172.3 43.9 copy-start.10
  257.6 18.0 copy-start.17
  304.6 15.9 copy-start.5
  304.6 15.9 copy-start.6
  312.6 1288.7 %copy-start.3 = (f32[32,1024]{1,0:T(8,128)S(1)}, f32[32,1024]{1,0:T(8,128)}, u32[]{:S(2)}) copy-start(f32[32,1024]{1,0:T(8,128)} %custom-call.5) | copy-start | bytes 393220
  312.6 1288.9 %copy-start.12 = (bf16[8,128,128]{2,1,0:T(8,128)(2,1)S(1)}, bf16[8,128,128]{2,1,0:T(8,128)(2,1)}, u32[]{:S(2)}) copy-start(bf16[8,128,128]{2,1,0:T(8,128)(2,1)} %param.37) | copy-start | bytes 786436
  1630.9 18.0 copy-start.24
  1648.9 44.4 copy-start.7
  1648.9 44.4 copy-start.8
  1648.9 441.6 %copy-start.9 = (f32[32,1024]{1,0:T(8,128)S(1)}, f32[32,1024]{1,0:T(8,128)}, u32[]{:S(2)}) copy-start(f32[32,1024]{1,0:T(8,128)} %custom-call.2) | copy-start | bytes 393220
  1648.9 441.6 %copy-start.25 = (f32[2,32,1024]{2,0,1:T(2,128)S(1)}, f32[2,32,1024]{2,0,1:T(2,128)}, u32[]{:S(2)}) copy-start(f32[2,32,1024]{2,0,1:T(2,128)} %custom-call.8) | copy-start | bytes 786436
  2093.3 43.0 copy-start.34
  2236.2 18.1 copy-start.11
  2236.2 18.1 copy-start.27
  2236.2 18.1 copy-start.29
  2236.2 18.1 copy-start.31
  2236.2 18.1 copy-start.33
  2254.3 51.1 %copy-start.36 = (f32[1,1024]{1,0:T(1,128)S(1)}, f32[1,1024]{1,0:T(1,128)}, u32[]{:S(2)}) copy-start(f32[1,1024]{1,0:T(1,128)} %copy-done.35) | copy-start | bytes 12292
  2254.3 51.1 %copy-start.38 = (f32[1,1024]{1,0:T(1,128)S(1)}, f32[1,1024]{1,0:T(1,128)}, u32[]{:S(2)}) copy-start(f32[1,1024]{1,0:T(1,128)} %copy-done.37) | copy-start | bytes 12292
  2254.3 51.1 %copy-start.40 = (f32[1,1024]{1,0:T(1,128)S(1)}, f32[1,1024]{1,0:T(1,128)}, u32[]{:S(2)}) copy-start(f32[1,1024]{1,0:T(1,128)} %copy-done.39) | copy-start | bytes 12292
  2254.3 51.1 %copy-start.42 = (f32[1,1024]{1,0:T(1,128)S(1)}, f32[1,1024]{1,0:T(1,128)}, u32[]{:S(2)}) copy-start(f32[1,1024]{1,0:T(1,128)} %copy-done.41) | copy-start | bytes 12292
  2334.7 87.4 %collective-permute-start.1 = (f32[3,32,1024]{2,0,1:T(4,128)S(1)}, f32[3,32,1024]{2,0,1:T(4,128)S(1)}, u32[]{:S(2)}, u32[]{:S(2)}) collective-permute-start(f32[3,32,1024]{2,0,1:T(4,128)S(1)} %pad_add_fusion.1), channel_id=1, source_target_pairs={{1,0},{3,2},{5,4},{7,6}} | collective-permute-start | bytes 1179656 | tf_op jit(solution)/shard_map/ppermute | solution.py:134
  2424.9 61.1 %copy-start.15 = (bf16[3,32,1024]{2,0,1:T(4,128)(2,1)}, bf16[3,32,1024]{2,0,1:T(4,128)(2,1)S(1)}, u32[]{:S(2)}) copy-start(bf16[3,32,1024]{2,0,1:T(4,128)(2,1)S(1)} %get-tuple-element.501) | copy-start | bytes 589828
  2486.0 2218.0 %all-reduce.11.cloned.1.call-start = ((), (), s32[]{:S(2)}) async-start(), calls=%async_computation | async-start | bytes 134217728 | tf_op jit(solution)/shard_map/psum | solution.py:115
  2547.6 2290.8 %all-reduce.17.cloned.1.call-start = ((), (), s32[]{:S(2)}) async-start(), calls=%async_computation.3 | async-start | bytes 102760448 | tf_op jit(solution)/shard_map/psum | solution.py:144
  2557.0 52.0 %slice-start.4 = ((s8[8388608]{0:T(1024)(128)(4,1)}), s8[4194304]{0:T(1024)(128)(4,1)S(1)}, s32[]{:S(2)}) async-start(s8[8388608]{0:T(1024)(128)(4,1)} %bitcast.244), calls=%async_computation.8 | async-start | bytes 8388608
  2566.5 42.5 slice-start.5
  2566.5 42.5 copy-start.21
  2566.5 42.5 copy-start.23
  2609.0 43.9 copy-start.16
  2698.2 2158.9 %all-reduce.15.cloned.1.call-start = ((), (), s32[]{:S(2)}) async-start(), calls=%async_computation.2 | async-start | bytes 147456 | tf_op jit(solution)/shard_map/psum | solution.py:144
  2708.6 917.7 %copy-start.19 = (f32[32,128]{1,0:T(8,128)S(1)}, f32[32,128]{1,0:T(8,128)}, u32[]{:S(2)}) copy-start(f32[32,128]{1,0:T(8,128)} %copy-done.18) | copy-start | bytes 49156
  4858.4 13.7 copy-start.64
  4858.4 16.4 copy-start.2
  4858.4 30.2 slice-start
  4858.4 30.2 slice-start.1
  4874.8 11.7 copy-start.13
  4874.8 12.5 copy-start.60
  4874.9 13.1 copy-start.59
  4874.9 13.7 slice-start.2
  4874.9 13.7 slice-start.3
  (18 other events, 89.4 us)
Sparse Core Ops, SparseCore 0:
  2486.2 1107.7 all-reduce.12
  3597.5 1106.5 all-reduce.10
  4708.2 130.1 all-reduce.16
  4842.3 14.6 all-reduce.14
where the time goes:
time: 4940 us; the launch traced here: 4900 us
  waiting for transfers between devices  2030 us (41%)
  local copies, waits for them, and re-layouts  1530 us (31%)
  other arithmetic  820 us (17%)
  matrix products  489 us (10%)
    psum x1, waiting for transfers between devices, shard_body(): out_proj = lax.psum(out_part, 'tp') + b_out  1080 us
    dynamic_update_slice x512, local copies, waits for them, and re-layouts, local_scan(): lax.scan(scan_step, (zeros_h, jnp.ones_like(zeros_h)), (decays, drives))  977 us
    psum x1, waiting for transfers between devices, shard_body(): d_normed = lax.psum(d_norm_part, 'tp')  885 us
    dynamic_slice x256, local copies, waits for them, and re-layouts, local_scan(): lax.scan(scan_step, (zeros_h, jnp.ones_like(zeros_h)), (decays, drives))  338 us
    dynamic_update_slice x128, other arithmetic, local_scan(): lax.scan(scan_step, (zeros_h, jnp.ones_like(zeros_h)), (decays, drives))  223 us
    mul x128, other arithmetic, scan_step(): return ((inputs_t[0] * grad_h, inputs_t[0] * prod_a), (grad_h, prod_a))  129 us
  transfers between devices with their start and end apart: 6, of which 4 were waited for; matrix products, arithmetic and copies ran while one was open for 11% of the time, Pallas kernels for 0%

commit v1 on v0

v1 whole, which is shorter than its diff:
```python
import functools
import jax
import jax.numpy as jnp
from jax import lax
from jax.experimental import pallas as pl
from jax.experimental.pallas import tpu as pltpu
from jax.sharding import PartitionSpec as P

F32 = jnp.float32
BF16 = jnp.bfloat16
TAPS = 4
SUB = 8
LANES = 128
SLOTS = 3
MSG_SLOTS = 4
GELU_K0 = 0.7978845608028654
GELU_K1 = 0.7978845608028654 * 0.044715
N_SUMS = 9


def middle_kernel(n_steps, n_tiles, n_tok, grads, pos_f, pos_b, par_f, par_b, wg_f, wg_b, px, py, dm, *rest):
    if grads:
        mix_o, dpy_o, dbr_o, gw_o, sy_o, sb_o = rest[:6]
        rest = rest[6:]
    else:
        mix_o, dpy_o, dbr_o = rest[:3]
        rest = rest[3:]
    (s_g, s_a, s_h, s_k, s_ra, s_ui, s_mi, s_c16, s_r, s_xb, in_x, in_y, in_d, pre_a, pre_i, out_m, out_y, out_b, d_c, d_16, d_gate, xb_w, send, recv, send_sem, recv_sem) = rest
    pitch = n_tok + SUB
    me = lax.axis_index("cp")
    step = pl.program_id(0)
    f_step = step - me
    b_step = step - 2 + me
    f_on = jnp.logical_and(f_step >= 0, f_step < n_steps)
    b_on = jnp.logical_and(b_step >= 0, b_step < n_steps)
    f_slot = lax.rem(f_step + SLOTS, SLOTS)
    b_slot = lax.rem(b_step + SLOTS, SLOTS)
    f_msg = lax.rem(f_step + MSG_SLOTS, MSG_SLOTS)
    b_msg = lax.rem(b_step + MSG_SLOTS, MSG_SLOTS)
    n_groups = n_tok // SUB

    def message(slot):
        return pltpu.make_async_remote_copy(src_ref=send.at[slot], dst_ref=recv.at[slot], send_sem=send_sem.at[slot], recv_sem=recv_sem.at[slot], device_id={"cp": 1 - me}, device_id_type=pl.DeviceIdType.MESH)

    @pl.when(step == 0)
    def _():
        barrier = pltpu.get_barrier_semaphore()
        pl.semaphore_signal(barrier, inc=1, device_id={"cp": 1 - me}, device_id_type=pl.DeviceIdType.MESH)
        pl.semaphore_wait(barrier, 1)

    def row8(base):
        return pl.ds(pl.multiple_of(base, SUB), SUB)

    def strided(t):
        return pl.ds(t, SUB, stride=pitch)

    @pl.when(jnp.logical_and(f_on, me == 1))
    def _():
        message(f_msg).wait_recv()

    @pl.when(f_on)
    def _():
        for seq in range(SUB):
            for src, dst in ((px, in_x), (py, in_y), (dm, in_d)):
                dst[pl.ds(seq * pitch, n_tok), :] = src[pl.ds(seq * n_tok, n_tok), :]
        b_x = jnp.broadcast_to(par_f[0:1, :], (SUB, LANES))
        b_y = jnp.broadcast_to(par_f[1:2, :], (SUB, LANES))
        taps = [jnp.broadcast_to(par_f[2 + k:3 + k, :], (SUB, LANES)) for k in range(TAPS)]
        c_b = jnp.broadcast_to(par_f[6:7, :], (SUB, LANES))
        b_a = jnp.broadcast_to(par_f[7:8, :], (SUB, LANES))
        b_i = jnp.broadcast_to(par_f[8:9, :], (SUB, LANES))
        nsp = jnp.broadcast_to(par_f[9:10, :], (SUB, LANES))
        first = (me == 0)
        in_msg = recv.at[f_msg]
        halo = [jnp.where(first, 0.0, in_msg[pl.ds(SUB * (1 + j), SUB), :]) for j in range(3)]
        h_in = jnp.where(first, 0.0, in_msg[pl.ds(0, SUB), :])
        xb_r = s_xb.at[f_slot] if grads else xb_w
        if grads:
            for j in range(3):
                xb_r[pl.ds(SUB * j, SUB), :] = halo[j]
        c16_r, g_r, a_r, h_r, k_r = s_c16.at[f_slot], s_g.at[f_slot], s_a.at[f_slot], s_h.at[f_slot], s_k.at[f_slot]
        ra_r, ui_r, mi_r = s_ra.at[f_slot], s_ui.at[f_slot], s_mi.at[f_slot]
        r_r = s_r.at[f_slot] if grads else None

        def conv_body(grp, carry):
            xm3, xm2, xm1 = carry
            pend = None
            for j in range(SUB):
                t = grp * SUB + j
                x0 = (in_x[strided(t), :] + b_x).astype(BF16).astype(F32)
                pos = pos_f[row8(t * SUB), :]
                acc = c_b + x0 * taps[0]
                acc = acc + jnp.where(pos >= 1, xm1, 0.0) * taps[1]
                acc = acc + jnp.where(pos >= 2, xm2, 0.0) * taps[2]
                acc = acc + jnp.where(pos >= 3, xm3, 0.0) * taps[3]
                if grads:
                    xb_r[row8(t * SUB + 3 * SUB), :] = x0
                if pend is None:
                    pend = acc
                else:
                    both = jnp.concatenate([pend, acc], axis=0).astype(BF16)
                    c16_r[pl.ds(pl.multiple_of((t - 1) * SUB, 2 * SUB), 2 * SUB), :] = both
                    pend = None
                xm3, xm2, xm1 = xm2, xm1, x0
            return xm3, xm2, xm1

        last3 = lax.fori_loop(0, n_groups, conv_body, tuple(halo))
        pre = jnp.dot(c16_r[...], wg_f[...], preferred_element_type=F32)
        pre_a[...] = pre[:, :LANES]
        pre_i[...] = pre[:, LANES:]
        h_r[pl.ds(0, SUB), :] = h_in

        def gate_body(grp, carry):
            h, sum_y = carry
            for j in range(SUB):
                t = grp * SUB + j
                rows = row8(t * SUB)
                if j % 2 == 0:
                    c2 = c16_r[pl.ds(pl.multiple_of(t * SUB, 2 * SUB), 2 * SUB), :].astype(F32)
                c = c2[:SUB] if j % 2 == 0 else c2[SUB:]
                reset = pos_f[rows, :] == 0
                r = jax.nn.sigmoid(pre_a[rows, :] + b_a)
                i = jax.nn.sigmoid(pre_i[rows, :] + b_i)
                la = nsp * r
                a = jnp.exp(la)
                y2 = la + la
                poly = -y2 * (1.0 + y2 * (0.5 + y2 * (1.0 / 6.0 + y2 * (1.0 / 24.0))))
                q = jnp.maximum(jnp.where(y2 > -0.0625, poly, 1.0 - a * a), 1e-37)
                rm = lax.rsqrt(q)
                m = jnp.where(reset, 1.0, q * rm)
                ic = i * c
                k = a * ic * rm
                a = jnp.where(reset, 0.0, a)
                u = m * ic
                h = a * h + u
                h_r[row8(t * SUB + SUB), :] = h
                a_r[rows, :] = a
                k_r[rows, :] = k
                ra_r[rows, :] = la - la * r
                ui_r[rows, :] = u - u * i
                mi_r[rows, :] = m * i
                if grads:
                    r_r[rows, :] = r
                v = in_y[strided(t), :] + b_y
                v2 = v * v
                th = jnp.tanh(v * (GELU_K0 + GELU_K1 * v2))
                hv = 0.5 * v
                y = hv + hv * th
                dy = (0.5 + 0.5 * th) + hv * (1.0 - th * th) * (GELU_K0 + (3.0 * GELU_K1) * v2)
                d = in_d[strided(t), :]
                g_r[rows, :] = d * y
                out_m[strided(t), :] = h * y
                d_py = d * h * dy
                out_y[strided(t), :] = d_py
                if grads:
                    sum_y = sum_y + d_py
            return h, sum_y

        h_end, sum_y = lax.fori_loop(0, n_groups, gate_body, (h_in, jnp.zeros((SUB, LANES), F32)))
        if grads:
            @pl.when(lax.rem(f_step, n_tiles) == 0)
            def _():
                sy_o[...] = jnp.zeros_like(sy_o)
            sy_o[...] += sum_y

        @pl.when(me == 0)
        def _():
            out_msg = send.at[f_msg]
            out_msg[pl.ds(0, SUB), :] = h_end
            for j in range(3):
                out_msg[pl.ds(SUB * (1 + j), SUB), :] = last3[j]
        for seq in range(SUB):
            mix_o[pl.ds(seq * n_tok, n_tok), :] = out_m[pl.ds(seq * pitch, n_tok), :].astype(BF16)
            dpy_o[pl.ds(seq * n_tok, n_tok), :] = out_y[pl.ds(seq * pitch, n_tok), :].astype(BF16)

        @pl.when(me == 0)
        def _():
            message(f_msg).start()

    @pl.when(jnp.logical_and(b_on, me == 0))
    def _():
        message(b_msg).wait_recv()

    @pl.when(jnp.logical_and(jnp.logical_and(b_step >= 1, b_step <= n_steps), me == 1))
    def _():
        message(lax.rem(b_step - 1 + MSG_SLOTS, MSG_SLOTS)).wait_send()

    @pl.when(b_on)
    def _():
        taps = [jnp.broadcast_to(par_b[2 + k:3 + k, :], (SUB, LANES)) for k in range(TAPS)]
        last = (me == 1)
        in_msg = recv.at[b_msg]
        carry_in = jnp.where(last, 0.0, in_msg[pl.ds(0, SUB), :])
        tail = [jnp.where(last, 0.0, in_msg[pl.ds(SUB * (1 + j), SUB), :]) for j in range(3)]
        g_r, a_r, h_r, k_r = s_g.at[b_slot], s_a.at[b_slot], s_h.at[b_slot], s_k.at[b_slot]
        ra_r, ui_r, mi_r = s_ra.at[b_slot], s_ui.at[b_slot], s_mi.at[b_slot]
        r_r = s_r.at[b_slot] if grads else None
        xb_r = s_xb.at[b_slot] if grads else None
        zero = jnp.zeros((SUB, LANES), F32)

        def scan_body(back, carry):
            grp = n_groups - 1 - back
            adh, sum_a, sum_i, sum_p = carry
            pend = None
            for j in reversed(range(SUB)):
                t = grp * SUB + j
                rows = row8(t * SUB)
                dh = g_r[rows, :] + adh
                adh = a_r[rows, :] * dh
                dlog = adh * (h_r[rows, :] - k_r[rows, :])
                dpa = dlog * ra_r[rows, :]
                dpi = dh * ui_r[rows, :]
                d_c[rows, :] = dh * mi_r[rows, :]
                if grads:
                    sum_a = sum_a + dpa
                    sum_i = sum_i + dpi
                    sum_p = sum_p + dlog * r_r[rows, :]
                if pend is None:
                    pend = (dpa, dpi)
                else:
                    pair = pl.ds(pl.multiple_of(t * SUB, 2 * SUB), 2 * SUB)
                    d_16[pair, :LANES] = jnp.concatenate([dpa, pend[0]], axis=0).astype(BF16)
                    d_16[pair, LANES:] = jnp.concatenate([dpi, pend[1]], axis=0).astype(BF16)
                    pend = None
            return adh, sum_a, sum_i, sum_p

        adh, sum_a, sum_i, sum_p = lax.fori_loop(0, n_groups, scan_body, (carry_in, zero, zero, zero))
        d_gate[...] = lax.dot_general(d_16[...], wg_b[...], (((1,), (1,)), ((), ())), preferred_element_type=F32)

        def conv_body(grp, carry):
            e3, e2, e1 = carry[:3]
            sums = list(carry[3:])
            for j in range(SUB):
                s = grp * SUB + j
                rows = row8(s * SUB)
                pos = pos_b[rows, :]
                dc = d_c[rows, :] + d_gate[rows, :]
                m1 = jnp.where(pos >= 1, dc, 0.0)
                m2 = jnp.where(pos >= 2, dc, 0.0)
                m3 = jnp.where(pos >= 3, dc, 0.0)
                done = e3 + m3 * taps[3]
                out_b[strided(s + SUB - 3), :] = done
                e3, e2, e1 = e2 + m2 * taps[2], e1 + m1 * taps[1], dc * taps[0]
                if grads:
                    sums[0] = sums[0] + dc * xb_r[row8(s * SUB + 3 * SUB), :]
                    sums[1] = sums[1] + m1 * xb_r[row8(s * SUB + 2 * SUB), :]
                    sums[2] = sums[2] + m2 * xb_r[row8(s * SUB + SUB), :]
                    sums[3] = sums[3] + m3 * xb_r[row8(s * SUB), :]
                    sums[4] = sums[4] + dc
                    sums[5] = sums[5] + done
            return (e3, e2, e1) + tuple(sums)

        res = lax.fori_loop(0, n_groups, conv_body, (zero, zero, zero) + (zero,) * (6 if grads else 0))
        ends = [res[j] + tail[j] for j in range(3)]
        for j in range(3):
            out_b[strided(n_tok + SUB - 3 + j), :] = ends[j]
        heads = [out_b[strided(SUB - 3 + j), :] for j in range(3)]

        @pl.when(me == 1)
        def _():
            out_msg = send.at[b_msg]
            out_msg[pl.ds(0, SUB), :] = adh
            for j in range(3):
                out_msg[pl.ds(SUB * (1 + j), SUB), :] = heads[j]

        for seq in range(SUB):
            dbr_o[pl.ds(seq * n_tok, n_tok), :] = out_b[pl.ds(seq * pitch + SUB, n_tok), :].astype(BF16)
        if grads:
            sums = list(res[3:])
            sum_x = sums[5] + ends[0] + ends[1] + ends[2] - heads[0] - heads[1] - heads[2]

            @pl.when(lax.rem(b_step, n_tiles) == 0)
            def _():
                gw_o[...] = jnp.zeros_like(gw_o)
                sb_o[...] = jnp.zeros_like(sb_o)
            for n, val in enumerate((sum_x, sums[0], sums[1], sums[2], sums[3], sums[4], sum_a, sum_i, sum_p)):
                sb_o[0, pl.ds(n * SUB, SUB), :] += val
            gw_o[0] += lax.dot_general(s_c16[b_slot], d_16[...], (((0,), (0,)), ((), ())), preferred_element_type=F32)

        @pl.when(me == 1)
        def _():
            message(b_msg).start()

    @pl.when(jnp.logical_and(f_on, me == 0))
    def _():
        message(f_msg).wait_send()


def middle(px, py, dm, pos_rep, par, w_gate, grads, collective_id):
    n_rows, width = px.shape
    n_tok = pos_rep.shape[1] // SUB
    tile = SUB * n_tok
    n_tiles, n_chunks = n_rows // tile, width // LANES
    n_steps = n_tiles * n_chunks

    def f_of(s):
        return jnp.clip(s - lax.axis_index("cp"), 0, n_steps - 1)

    def b_of(s):
        return jnp.clip(s - 2 + lax.axis_index("cp"), 0, n_steps - 1)

    def spec(shape, of, index):
        def index_map(s):
            k = of(s)
            return index(k // n_tiles, k % n_tiles)
        return pl.BlockSpec(shape, index_map)

    big = lambda of: spec((tile, LANES), of, lambda c, t: (t, c))
    in_specs = [
        spec((None, tile, LANES), f_of, lambda c, t: (t, 0, 0)), spec((None, tile, LANES), b_of, lambda c, t: (t, 0, 0)),
        spec((16, LANES), f_of, lambda c, t: (0, c)), spec((16, LANES), b_of, lambda c, t: (0, c)),
        spec((None, LANES, 2 * LANES), f_of, lambda c, t: (c, 0, 0)), spec((None, LANES, 2 * LANES), b_of, lambda c, t: (c, 0, 0)),
        big(f_of), big(f_of), big(f_of)]
    out_specs = [big(f_of), big(f_of), big(b_of)]
    out_shape = [jax.ShapeDtypeStruct((n_rows, width), BF16)] * 3
    if grads:
        out_specs += [spec((1, LANES, 2 * LANES), b_of, lambda c, t: (c, 0, 0)), spec((1, SUB, LANES), f_of, lambda c, t: (c, 0, 0)), spec((1, N_SUMS * SUB, LANES), b_of, lambda c, t: (c, 0, 0))]
        out_shape += [jax.ShapeDtypeStruct((n_chunks, LANES, 2 * LANES), F32), jax.ShapeDtypeStruct((n_chunks, SUB, LANES), F32), jax.ShapeDtypeStruct((n_chunks, N_SUMS * SUB, LANES), F32)]
    pitched = pltpu.VMEM((SUB * (n_tok + SUB), LANES), F32)
    flat = pltpu.VMEM((tile, LANES), F32)
    slots = pltpu.VMEM((SLOTS, tile, LANES), F32)
    small = pltpu.VMEM((SLOTS if grads else 1, tile if grads else SUB, LANES), F32)
    scratch = [
        slots, slots, pltpu.VMEM((SLOTS, tile + SUB, LANES), F32), slots, slots, slots, slots, pltpu.VMEM((SLOTS, tile, LANES), BF16), small,
        pltpu.VMEM((SLOTS if grads else 1, tile + 3 * SUB if grads else SUB, LANES), F32),
        pitched, pitched, pitched, flat, flat, pitched, pitched, pltpu.VMEM((SUB * (n_tok + SUB) + SUB, LANES), F32), flat, pltpu.VMEM((tile, 2 * LANES), BF16), flat,
        pltpu.VMEM((SUB, LANES), F32),
        pltpu.VMEM((MSG_SLOTS, 4 * SUB, LANES), F32), pltpu.VMEM((MSG_SLOTS, 4 * SUB, LANES), F32), pltpu.SemaphoreType.DMA((MSG_SLOTS,)), pltpu.SemaphoreType.DMA((MSG_SLOTS,))]
    return pl.pallas_call(
        functools.partial(middle_kernel, n_steps, n_tiles, n_tok, grads),
        grid=(n_steps + 2,), in_specs=in_specs, out_specs=out_specs, out_shape=out_shape, scratch_shapes=scratch,
        name="middle",
        cost_estimate=pl.CostEstimate(flops=n_rows * width * 1500, bytes_accessed=n_rows * width * 18, transcendentals=n_rows * width * 8),
        compiler_params=pltpu.CompilerParams(collective_id=collective_id, has_side_effects=True, vmem_limit_bytes=60 * 1024 * 1024, dimension_semantics=("arbitrary",)),
    )(pos_rep, pos_rep, par, par, w_gate, w_gate, px, py, dm)


NORM_EPS = 1e-6
IN_SPECS = (P(None, "cp", None), P(None, "cp", None), P(None, "cp"), P(), P(None, "tp"), P("tp"), P(None, "tp"), P("tp"), P(None, "tp"), P("tp"), P("tp", None, None), P("tp"), P("tp", None, None), P("tp"), P("tp"), P("tp", None), P())
OUT_SPECS = (P(None, "cp", None), P(None, "cp", None), P(), P(None, "tp"), P("tp"), P(None, "tp"), P("tp"), P(None, "tp"), P("tp"), P("tp", None, None), P("tp"), P("tp", None, None), P("tp"), P("tp"), P("tp", None), P())


def norm_apply(x_f, scale_f):
    mean_sq = jnp.mean(x_f * x_f, axis=-1, keepdims=True)
    return x_f * lax.rsqrt(mean_sq + NORM_EPS) * (1.0 + scale_f)


def spread_positions(seg_pos):
    n_seq, n_tok = seg_pos.shape
    pos = jnp.swapaxes(seg_pos.reshape(n_seq // SUB, SUB, n_tok), 1, 2).reshape(n_seq // SUB, n_tok * SUB, 1)
    return jnp.broadcast_to(pos, (n_seq // SUB, n_tok * SUB, LANES))


def stack_params(b_x, b_y, conv_w, conv_b, b_a, b_i, a_param):
    rows = [b_x, b_y, conv_w[0], conv_w[1], conv_w[2], conv_w[3], conv_b, b_a, b_i]
    rows = [row.astype(F32) for row in rows] + [-8.0 * jax.nn.softplus(a_param)]
    return jnp.concatenate([jnp.stack(rows), jnp.zeros((16 - len(rows), a_param.shape[0]), F32)], axis=0)


def shard_body(x_in, grad_z, seg_pos, norm_scale, w_x, b_x, w_y, b_y, conv_w, conv_b, w_a, b_a, w_i, b_i, a_param, w_out, b_out):
    n_seq, n_tok, d_model = x_in.shape
    x_f = x_in.reshape(n_seq * n_tok, d_model).astype(F32)
    gz = grad_z.reshape(n_seq * n_tok, d_model)
    normed_f, norm_pull = jax.vjp(norm_apply, x_f, norm_scale.astype(F32))
    normed = normed_f.astype(BF16)
    px = jnp.dot(normed, w_x, preferred_element_type=F32)
    py = jnp.dot(normed, w_y, preferred_element_type=F32)
    dm = lax.dot_general(gz, w_out, (((1,), (1,)), ((), ())), preferred_element_type=F32)
    par = stack_params(b_x, b_y, conv_w, conv_b, b_a, b_i, a_param)
    w_gate = jnp.concatenate([w_a, w_i], axis=2)
    mixed, dpy, dbr, g_gate, s_y, s_b = middle(px, py, dm, spread_positions(seg_pos), par, w_gate, True, 0)
    out_part = jnp.dot(mixed, w_out, preferred_element_type=F32)
    out_proj = lax.psum(out_part, "tp") + b_out
    z_out = (x_f + out_proj).astype(BF16).reshape(x_in.shape)
    tok = (((0,), (0,)), ((), ()))
    chan = (((1,), (1,)), ((), ()))
    g_w_out = lax.dot_general(mixed, gz, tok, preferred_element_type=F32)
    g_w_x = lax.dot_general(normed, dbr, tok, preferred_element_type=F32)
    g_w_y = lax.dot_general(normed, dpy, tok, preferred_element_type=F32)
    g_b_out = jnp.sum(grad_z, axis=(0, 1), dtype=F32)
    d_norm_part = lax.dot_general(dbr, w_x, chan, preferred_element_type=F32) + lax.dot_general(dpy, w_y, chan, preferred_element_type=F32)
    d_normed = lax.psum(d_norm_part, "tp")
    d_x_norm, g_scale = norm_pull(d_normed)
    grad_x = (gz.astype(F32) + d_x_norm).astype(BF16).reshape(x_in.shape)
    width = a_param.shape[0]
    s_y = jnp.sum(s_y, axis=1).reshape(width)
    s_b = jnp.sum(s_b.reshape(s_b.shape[0], N_SUMS, SUB, LANES), axis=2)
    s_b = jnp.swapaxes(s_b, 0, 1).reshape(N_SUMS, width)
    g_a = -8.0 * s_b[8] * jax.nn.sigmoid(a_param)
    blk = LANES
    sums = lax.psum((g_scale, g_w_x, s_b[0], g_w_y, s_y, s_b[1:5], s_b[5], g_gate[:, :, :blk], s_b[6], g_gate[:, :, blk:], s_b[7], g_a, g_w_out, g_b_out), "cp")
    return (z_out, grad_x) + tuple(sums)


def solution(mesh):
    return jax.shard_map(shard_body, mesh=mesh, in_specs=IN_SPECS, out_specs=OUT_SPECS, check_vma=False)
```

time: 4940 us -> 2860 us (0.58)
  local copies, waits for them, and re-layouts: 1530 us -> 44.8 us
  other arithmetic: 820 us -> 176 us
  Pallas kernels: 0 us -> 150 us
  matrix products: 489 us -> 409 us
    dynamic_update_slice x516 -> x0, local copies, waits for them, and re-layouts: 979 us -> none  [the longest x512 977 us: local_scan(): lax.scan(scan_step, (zeros_h, jnp.ones_like(zeros_h)), (decays, drives))]
    dynamic_slice x257 -> x0, local copies, waits for them, and re-layouts: 338 us -> none  [the longest x256 338 us: local_scan(): lax.scan(scan_step, (zeros_h, jnp.ones_like(zeros_h)), (decays, drives))]
    reduce_sum x8 -> x3, other arithmetic: 274 us -> 13.2 us  [the longest x1 12.5 us: shard_body(): g_b_out = jnp.sum(grad_z, axis=(0, 1), dtype=F32)]
    dynamic_update_slice x130 -> x0, other arithmetic: 223 us -> none  [the longest x128 223 us: local_scan(): lax.scan(scan_step, (zeros_h, jnp.ones_like(zeros_h)), (decays, drives))]
    mul x130 -> x3, other arithmetic: 157 us -> 2.53 us  [the longest x1 1.3 us: stack_params(): rows = [row.astype(F32) for row in rows] + [-8.0 * jax.nn.softplus(a_param)]]
    pallas_call x0 -> x1, Pallas kernels: none -> 150 us  [middle(): pl.pallas_call(functools.partial(middle_kernel, n_steps, n_tiles, n_tok,...]
    dot_general x15 -> x9, matrix products: 489 us -> 409 us  [the longest x1 61 us: shard_body(): lax.dot_general(dpy, w_y, chan, preferred_element_type=F32)]
    reshape x4 -> x1, local copies, waits for them, and re-layouts: 66.4 us -> 0.12 us  [spread_positions(): seg_pos.reshape(n_seq // SUB, SUB, n_tok)]
  transfers between devices with their start and end apart: 6 -> 4, of which waited for: 4 -> 4; matrix products, arithmetic and copies ran while one was open for 11% -> 11% of each run, Pallas kernels for 0% -> 0%
where the time goes in v1:
time: 2860 us
  waiting for transfers between devices  2060 us (72%)
  matrix products  409 us (14%)
  other arithmetic  176 us (6%)
  Pallas kernels  150 us (5%)
  local copies, waits for them, and re-layouts  44.8 us (2%)
    psum x1, waiting for transfers between devices, shard_body(): out_proj = lax.psum(out_part, 'tp') + b_out  1080 us
    psum x1, waiting for transfers between devices, shard_body(): d_normed = lax.psum(d_norm_part, 'tp')  915 us
    pallas_call x1, Pallas kernels, middle(): pl.pallas_call(functools.partial(middle_kernel, n_steps, n_tiles, n_tok,...  150 us
    convert_element_type x1, other arithmetic, shard_body(): grad_x = (gz.astype(F32) + d_x_norm).astype(BF16).reshape(x_in.shape)  84.9 us
    psum x2, waiting for transfers between devices, shard_body(): lax.psum((g_scale, g_w_x, s_b[0], g_w_y, s_y, s_b[1:5], s_b[5], g_gate[:,...  68.1 us
    dot_general x1, matrix products, shard_body(): lax.dot_general(dpy, w_y, chan, preferred_element_type=F32)  61 us
  transfers between devices with their start and end apart: 4, of which 4 were waited for; matrix products, arithmetic and copies ran while one was open for 11% of the time, Pallas kernels for 0%

profile of v1, /device:TPU:0, one launch (start us, length us, event | category | flops | bytes accessed | tf_op | source)
XLA Modules:
  0.0 2855.1 jit_solution(10452671019043994996)
XLA Ops:
  7.2 0.0 all-reduce.9.cloned.1.call-start
  7.2 1.5 slice_convert_fusion
  8.7 1.3 stack.48
  10.0 1.3 stack.49
  11.2 1.3 stack.50
  12.5 1.3 stack.51
  13.8 1.3 stack.52
  15.1 1.3 fusion.12
  16.4 11.3 fusion.6
  27.7 0.0 copy-start.11
  27.7 0.6 copy-done.11
  28.3 0.0 copy-start.7
  28.3 22.7 fusion.4
  51.1 43.0 %fusion.14.px = f32[4096,1024]{1,0:T(8,128)} fusion(bf16[4096,4096]{1,0:T(8,128)(2,1)} %fusion.4, bf16[4096,1024]{1,0:T(8,128)(2,1)} %param.21), kind=kOutput, calls=%fused_computation.36 | convolution fusion | flops 34359738368 | bytes 58720256 | tf_op jit(solution)/shard_map/dot_general | solution.py:366
  94.1 43.2 %fusion.15.py = f32[4096,1024]{1,0:T(8,128)} fusion(bf16[4096,4096]{1,0:T(8,128)(2,1)} %fusion.4, bf16[4096,1024]{1,0:T(8,128)(2,1)} %param.23), kind=kOutput, calls=%fused_computation.37 | convolution fusion | flops 34359738368 | bytes 58720256 | tf_op jit(solution)/shard_map/dot_general | solution.py:367
  137.3 0.1 copy.35
  137.4 0.2 broadcast_in_dim.16
  137.7 43.4 %fusion.16.dm = f32[4096,1024]{1,0:T(8,128)} fusion(bf16[4096,4096]{1,0:T(8,128)(2,1)} %bitcast.71, bf16[1024,4096]{1,0:T(8,128)(2,1)} %param.32), kind=kOutput, calls=%fused_computation.38 | convolution fusion | flops 34359738368 | bytes 58720256 | tf_op jit(solution)/shard_map/dot_general | solution.py:368
  181.2 0.9 pad_maximum_fusion.wg_f.wg_b
  182.1 1.3 concatenate.6.par_f.par_b
  183.4 2.2 broadcast_in_dim.17.pos_f.pos_b
  185.6 149.6 %middle.1 = (bf16[4096,1024]{1,0:T(8,128)(2,1)}, bf16[4096,1024]{1,0:T(8,128)(2,1)}, bf16[4096,1024]{1,0:T(8,128)(2,1)}, f32[8,128,256]{2,1,0:T(8,128)}, f32[8,8,128]{2,1,0:T(8,128)}, /*index=5*/f32[8,72,128]{2,1,0:T(8,128)}) custom-call(s32[4,1024,128]{2,1,0:T(8,128)} %broadcast_in_dim.17.pos_f.pos_b, s32[4,1024,128]{2,1,0:T(8,128)} %broadcast_in_dim.17.pos_f.pos_b, ...), custom_call_target="tpu_custom_call" | custom-call | flops 6291456000 | bytes 75497472 | tf_op jit(solution)/shard_map/middle/pallas_call | solution.py:329
  335.2 44.5 %fusion.18 = f32[4096,4096]{1,0:T(8,128)} fusion(bf16[4096,1024]{1,0:T(8,128)(2,1)} %get-tuple-element.23, bf16[4096,1024]{1,0:T(8,128)(2,1)} %param.21), kind=kOutput, calls=%fused_computation.40 | convolution fusion | flops 34359738368 | bytes 83886080 | tf_op jit(solution)/shard_map/dot_general | solution.py:381
  379.6 61.0 %convolution_add_fusion = f32[4096,4096]{1,0:T(8,128)} fusion(f32[4096,4096]{1,0:T(8,128)} %fusion.18, bf16[4096,1024]{1,0:T(8,128)(2,1)} %get-tuple-element.24, bf16[4096,1024]{1,0:T(8,128)(2,1)} %param.23), kind=kOutput, calls=%fused_computation.16 | convolution fusion | flops 34376515584 | bytes 150994944 | tf_op jit(solution)/shard_map/dot_general | solution.py:381
  440.7 0.0 all-reduce.9.cloned.1.call-update
  440.7 0.0 all-reduce.7.cloned.1.call-start
  440.8 44.0 %fusion.17 = f32[4096,4096]{1,0:T(8,128)} fusion(bf16[4096,1024]{1,0:T(8,128)(2,1)} %get-tuple-element.22, bf16[1024,4096]{1,0:T(8,128)(2,1)} %param.32), kind=kOutput, calls=%fused_computation.39 | convolution fusion | flops 34359738368 | bytes 83886080 | tf_op jit(solution)/shard_map/dot_general | solution.py:372
  484.7 0.0 all-reduce.7.cloned.1.call-update
  484.8 0.0 all-reduce.13.cloned.1.call-start
  484.8 1.1 copy-done.1
  486.0 1.1 fusion.13
  487.1 43.7 %fusion.21 = f32[1024,4096]{1,0:T(8,128)} fusion(bf16[4096,1024]{1,0:T(8,128)(2,1)} %get-tuple-element.22, bf16[4096,4096]{1,0:T(8,128)(2,1)} %bitcast.72), kind=kOutput, calls=%fused_computation.43 | convolution fusion | flops 34359738368 | bytes 58720256 | tf_op jit(solution)/shard_map/dot_general | solution.py:377
  530.8 43.9 %fusion.19 = f32[4096,1024]{1,0:T(8,128)} fusion(bf16[4096,4096]{1,0:T(8,128)(2,1)} %fusion.4, bf16[4096,1024]{1,0:T(8,128)(2,1)} %get-tuple-element.23), kind=kOutput, calls=%fused_computation.41 | convolution fusion | flops 34359738368 | bytes 58720256 | tf_op jit(solution)/shard_map/dot_general | solution.py:378
  574.8 42.4 %fusion.20 = f32[4096,1024]{1,0:T(8,128)} fusion(bf16[4096,4096]{1,0:T(8,128)(2,1)} %fusion.4, bf16[4096,1024]{1,0:T(8,128)(2,1)S(1)} %bitcast.94), kind=kOutput, calls=%fused_computation.42 | convolution fusion | flops 34359738368 | bytes 58720256 | tf_op jit(solution)/shard_map/dot_general | solution.py:379
  617.2 0.0 all-reduce.13.cloned.1.call-update
  617.2 0.0 all-reduce.11.cloned.1.call-start
  617.2 0.6 copy-done.13
  617.9 0.6 reduce_sum.66
  618.5 0.1 bitcast_reduce_fusion
  618.6 0.6 slice_multiply_fusion
  619.2 0.6 divide_multiply_fusion
  619.8 0.6 slice_bitcast_fusion
  620.4 12.5 convert_reduce_fusion
  632.9 915.2 %all-reduce.9.cloned.1.call-done = f32[4096,4096]{1,0:T(8,128)} async-done(((f32[4096,4096]{1,0:T(8,128)}), f32[4096,4096]{1,0:T(8,128)}) %all-reduce.9.cloned.1.call-update) | async-done | bytes 67108880 | tf_op jit(solution)/shard_map/psum | solution.py:382
  1548.1 32.2 %fusion.5 = (f32[4096]{0:T(1024)}, f32[4096]{0:T(1024)S(1)}) fusion(f32[4096,4096]{1,0:T(8,128)} %all-reduce.9.cloned.1.call-done, bf16[32,128,4096]{2,1,0:T(8,128)(2,1)} %param.17, f32[4096]{0:T(1024)S(1)} %copy-done.8, f32[4096]{0:T(1024)S(1)} %copy-done.10), kind=kLoop, calls=%fused_computation.11 | loop fusion | flops 117432320 | bytes 100728832 | tf_op jit(solution)/shard_map/transpose(jvp())/reduce_sum | solution.py:345
  1580.3 0.0 all-reduce.11.cloned.1.call-update
  1580.4 1077.8 %all-reduce.7.cloned.1.call-done = f32[4096,4096]{1,0:T(8,128)} async-done(((f32[4096,4096]{1,0:T(8,128)}), f32[4096,4096]{1,0:T(8,128)}) %all-reduce.7.cloned.1.call-update) | async-done | bytes 67108880 | tf_op jit(solution)/shard_map/psum | solution.py:373
  2658.2 84.9 %fusion.1 = (bf16[4096,4096]{1,0:T(8,128)(2,1)}, bf16[4096,4096]{1,0:T(8,128)(2,1)}) fusion(bf16[32,128,4096]{2,1,0:T(8,128)(2,1)} %param.17, f32[4096,4096]{1,0:T(8,128)} %all-reduce.9.cloned.1.call-done, f32[4096]{0:T(1024)S(1)} %fusion.11, f32[4096]{0:T(1024)S(1)} %copy-done.10, f32[4096]{0:T(1024)S(1)} %copy-done.8, bf16[32,128,4096]{2,1,0:T(8,128)(2,1)} %param.18, ...), kind=kLoop, calls=%fused_computation.2 | loop fusion | flops 201326592 | bytes 268500992 | tf_op jit(solution)/shard_map/convert_element_type | solution.py:384
  2743.1 49.4 %all-reduce.13.cloned.1.call-done = (f32[4096,1024]{1,0:T(8,128)}, f32[4096,1024]{1,0:T(8,128)}, f32[8,128,128]{2,1,0:T(8,128)}, f32[8,128,128]{2,1,0:T(8,128)}, f32[1024,4096]{1,0:T(8,128)}) async-done(((f32[4096,1024]{1,0:T(8,128)}, f32[4096,1024]{1,0:T(8,128)}, f32[8,128,128]{2,1,0:T(8,128)}, f32[8,128,128]{2,1,0:T(8,128)}, f32[1024,4096]{1,0:T(8,128)}), (f32[4096,1024]{1,0:T(8,128)}, ...) | async-done | bytes 51380240 | tf_op jit(solution)/shard_map/psum | solution.py:391
  2792.5 18.7 all-reduce.11.cloned.1.call-done
  2811.2 1.5 copy.52
  2812.8 14.2 copy.53
  2827.0 0.6 copy.54
  2827.6 8.5 copy.55
  2836.1 0.6 copy.56
  2836.7 0.6 copy.57
  2837.3 0.6 copy.58
  2837.9 0.8 copy.59
  2838.7 0.6 copy.60
  2839.3 0.8 copy.61
  2840.1 0.6 copy.62
  2840.7 0.6 copy.63
  2841.3 6.2 copy.64
  2847.4 0.6 copy.65
  (85 shorter events, 0.2 us)
Async XLA Ops:
  7.2 21.1 copy-start.28
  7.2 1541.0 %all-reduce.9.cloned.1.call-start = ((), (), s32[]{:S(2)}) async-start(), calls=%async_computation.1 | async-start | bytes 134217728 | tf_op jit(solution)/shard_map/psum | solution.py:382
  27.7 0.6 copy-start.11
  28.3 22.7 copy-start.7
  28.3 22.7 copy-start.9
  94.1 43.2 %copy-start.14 = (s32[32,128]{1,0:T(8,128)S(1)}, s32[32,128]{1,0:T(8,128)}, u32[]{:S(2)}) copy-start(s32[32,128]{1,0:T(8,128)} %param.19) | copy-start | bytes 49156
  137.6 43.6 %copy-start.5 = (bf16[8,128,128]{2,1,0:T(8,128)(2,1)S(1)}, bf16[8,128,128]{2,1,0:T(8,128)(2,1)}, u32[]{:S(2)}) copy-start(bf16[8,128,128]{2,1,0:T(8,128)(2,1)} %param.29) | copy-start | bytes 786436
  137.6 43.6 %copy-start.6 = (bf16[8,128,128]{2,1,0:T(8,128)(2,1)S(1)}, bf16[8,128,128]{2,1,0:T(8,128)(2,1)}, u32[]{:S(2)}) copy-start(bf16[8,128,128]{2,1,0:T(8,128)(2,1)} %param.27) | copy-start | bytes 786436
  137.6 44.4 %copy-start.16 = (f32[1024]{0:T(1024)S(1)}, f32[1024]{0:T(1024)}, u32[]{:S(2)}) copy-start(f32[1024]{0:T(1024)} %stack.48) | copy-start | bytes 12292
  137.6 44.4 %copy-start.17 = (f32[1024]{0:T(1024)S(1)}, f32[1024]{0:T(1024)}, u32[]{:S(2)}) copy-start(f32[1024]{0:T(1024)} %stack.49) | copy-start | bytes 12292
  137.6 44.4 %copy-start.18 = (f32[1024]{0:T(1024)S(1)}, f32[1024]{0:T(1024)}, u32[]{:S(2)}) copy-start(f32[1024]{0:T(1024)} %stack.50) | copy-start | bytes 12292
  137.6 44.4 %copy-start.19 = (f32[1024]{0:T(1024)S(1)}, f32[1024]{0:T(1024)}, u32[]{:S(2)}) copy-start(f32[1024]{0:T(1024)} %stack.51) | copy-start | bytes 12292
  137.7 44.4 %copy-start.20 = (f32[1024]{0:T(1024)S(1)}, f32[1024]{0:T(1024)}, u32[]{:S(2)}) copy-start(f32[1024]{0:T(1024)} %stack.52) | copy-start | bytes 12292
  137.7 44.4 %copy-start.21 = (f32[1024]{0:T(1024)S(1)}, f32[1024]{0:T(1024)}, u32[]{:S(2)}) copy-start(f32[1024]{0:T(1024)} %fusion.12) | copy-start | bytes 12292
  137.7 44.4 %copy-start.24 = (f32[1,1024]{1,0:T(1,128)S(1)}, f32[1,1024]{1,0:T(1,128)}, u32[]{:S(2)}) copy-start(f32[1,1024]{1,0:T(1,128)} %get-tuple-element.53) | copy-start | bytes 12292
  137.7 44.4 %copy-start.25 = (f32[1,1024]{1,0:T(1,128)S(1)}, f32[1,1024]{1,0:T(1,128)}, u32[]{:S(2)}) copy-start(f32[1,1024]{1,0:T(1,128)} %get-tuple-element.54) | copy-start | bytes 12292
  137.7 44.4 %copy-start.26 = (f32[1,1024]{1,0:T(1,128)S(1)}, f32[1,1024]{1,0:T(1,128)}, u32[]{:S(2)}) copy-start(f32[1,1024]{1,0:T(1,128)} %get-tuple-element.55) | copy-start | bytes 12292
  137.7 44.4 %copy-start.27 = (f32[1,1024]{1,0:T(1,128)S(1)}, f32[1,1024]{1,0:T(1,128)}, u32[]{:S(2)}) copy-start(f32[1,1024]{1,0:T(1,128)} %get-tuple-element.56) | copy-start | bytes 12292
  440.7 2217.5 %all-reduce.7.cloned.1.call-start = ((), (), s32[]{:S(2)}) async-start(), calls=%async_computation | async-start | bytes 134217728 | tf_op jit(solution)/shard_map/psum | solution.py:373
  484.7 1.2 copy-start.1
  484.8 2307.8 %all-reduce.13.cloned.1.call-start = ((), (), s32[]{:S(2)}) async-start(), calls=%async_computation.3 | async-start | bytes 102760448 | tf_op jit(solution)/shard_map/psum | solution.py:391
  487.0 87.7 %slice-start.4 = ((s8[8388608]{0:T(1024)(128)(4,1)}), s8[4194304]{0:T(1024)(128)(4,1)S(1)}, s32[]{:S(2)}) async-start(s8[8388608]{0:T(1024)(128)(4,1)} %bitcast.93), calls=%async_computation.8 | async-start | bytes 8388608
  530.8 44.0 %slice-start.5 = ((s8[8388608]{0:T(1024)(128)(4,1)}), s8[4194304]{0:T(1024)(128)(4,1)S(1)}, s32[]{:S(2)}) async-start(s8[8388608]{0:T(1024)(128)(4,1)} %bitcast.93), calls=%async_computation.9 | async-start | bytes 8388608
  617.1 0.8 copy-start.13
  617.1 1.4 copy-start.29
  617.1 1.4 copy-start.4
  617.1 2.1 copy-start.15
  617.1 931.0 %copy-start.8 = (f32[4096]{0:T(1024)S(1)}, f32[4096]{0:T(1024)}, u32[]{:S(2)}) copy-start(f32[4096]{0:T(1024)} %copy-done.7) | copy-start | bytes 49156
  617.2 931.0 %copy-start.10 = (f32[4096]{0:T(1024)S(1)}, f32[4096]{0:T(1024)}, u32[]{:S(2)}) copy-start(f32[4096]{0:T(1024)} %copy-done.9) | copy-start | bytes 49156
  617.2 2194.0 %all-reduce.11.cloned.1.call-start = ((), (), s32[]{:S(2)}) async-start(), calls=%async_computation.2 | async-start | bytes 147456 | tf_op jit(solution)/shard_map/psum | solution.py:391
  632.9 947.4 %copy-start.12 = (f32[32,128]{1,0:T(8,128)S(1)}, f32[32,128]{1,0:T(8,128)}, u32[]{:S(2)}) copy-start(f32[32,128]{1,0:T(8,128)} %copy-done.11) | copy-start | bytes 49156
  2811.2 15.8 copy-start.35
  2811.2 16.4 copy-start
  2812.7 23.4 copy-start.34
  2812.7 24.0 copy-start.23
  2812.7 24.6 copy-start.33
  2812.7 25.2 copy-start.3
  2812.7 26.0 copy-start.32
  2812.7 26.6 copy-start.2
  2812.7 27.4 copy-start.31
  2812.7 27.9 copy-start.30
  2812.7 28.5 slice-start
  2812.7 28.5 slice-start.1
  2827.6 13.7 slice-start.2
  2827.6 13.7 slice-start.3
  2827.6 19.9 copy-start.22
Sparse Core Ops, SparseCore 0:
  440.8 1107.2 all-reduce.8
  1551.6 1106.5 all-reduce.6
  2662.3 130.1 all-reduce.12
  2796.5 14.6 all-reduce.10

commit v2 on v1

v2 whole, which is shorter than its diff:
```python
import functools
import jax
import jax.numpy as jnp
from jax import lax
from jax.experimental import pallas as pl
from jax.experimental.pallas import tpu as pltpu
from jax.sharding import PartitionSpec as P

F32 = jnp.float32
BF16 = jnp.bfloat16
TAPS = 4
SUB = 8
LANES = 128
SLOTS = 3
MSG_SLOTS = 4
VMEM_LIMIT = 60 << 20
ROW = (((1,), (0,)), ((), ()))
CHAN = (((1,), (1,)), ((), ()))
TOK = (((0,), (0,)), ((), ()))
GELU_K0 = 0.7978845608028654
GELU_K1 = 0.7978845608028654 * 0.044715
N_SUMS = 9
N_PAR = 10
BORROW = TAPS - 1


def param_rows(ref):
    return [jnp.broadcast_to(ref[pl.ds(k, 1), :], (SUB, LANES)) for k in range(N_PAR)]


def middle_kernel(n_steps, n_tiles, n_tok, grads, pos_f, pos_b, par_f, par_b, wg_f, wg_b, px, py, dm, *rest):
    if grads:
        mix_o, dpy_o, dbr_o, gw_o, sy_o, sb_o = rest[:6]
        rest = rest[6:]
    else:
        mix_o, dpy_o, dbr_o = rest[:3]
        rest = rest[3:]
    (s_g, s_a, s_h, s_k, s_ra, s_ui, s_mi, s_c16, s_r, s_xb, in_x, in_y, in_d, pre_a, pre_i, out_m, out_y, out_b, d_c, d_16, d_gate, send, recv, send_sem, recv_sem) = rest
    pitch = n_tok + SUB
    me = lax.axis_index("cp")
    step = pl.program_id(0)
    f_step = step - me
    b_step = step - 2 + me
    f_on = jnp.logical_and(f_step >= 0, f_step < n_steps)
    b_on = jnp.logical_and(b_step >= 0, b_step < n_steps)
    f_slot = lax.rem(f_step + SLOTS, SLOTS)
    b_slot = lax.rem(b_step + SLOTS, SLOTS)
    f_msg = lax.rem(f_step + MSG_SLOTS, MSG_SLOTS)
    b_msg = lax.rem(b_step + MSG_SLOTS, MSG_SLOTS)
    n_groups = n_tok // SUB

    def message(slot):
        return pltpu.make_async_remote_copy(src_ref=send.at[slot], dst_ref=recv.at[slot], send_sem=send_sem.at[slot], recv_sem=recv_sem.at[slot], device_id={"cp": 1 - me}, device_id_type=pl.DeviceIdType.MESH)

    @pl.when(step == 0)
    def _():
        barrier = pltpu.get_barrier_semaphore()
        pl.semaphore_signal(barrier, inc=1, device_id={"cp": 1 - me}, device_id_type=pl.DeviceIdType.MESH)
        pl.semaphore_wait(barrier, 1)

    def row8(base):
        return pl.ds(pl.multiple_of(base, SUB), SUB)

    def pair(t):
        return pl.ds(pl.multiple_of(t * SUB, 2 * SUB), 2 * SUB)

    def strided(t):
        return pl.ds(t, SUB, stride=pitch)

    @pl.when(jnp.logical_and(f_on, me == 1))
    def _():
        message(f_msg).wait_recv()

    @pl.when(f_on)
    def _():
        for seq in range(SUB):
            in_x[pl.ds(seq * pitch, n_tok), :] = px[pl.ds(seq * n_tok, n_tok), :]
        b_x, b_y, *taps, c_b, b_a, b_i, nsp = param_rows(par_f)
        h_in, *halo = [jnp.where(me == 0, 0.0, recv[f_msg, pl.ds(SUB * j, SUB), :]) for j in range(TAPS)]
        xb_r = s_xb.at[f_slot] if grads else None
        if grads:
            for j in range(BORROW):
                xb_r[pl.ds(SUB * j, SUB), :] = halo[j]
        c16_r, g_r, a_r, h_r, k_r = s_c16.at[f_slot], s_g.at[f_slot], s_a.at[f_slot], s_h.at[f_slot], s_k.at[f_slot]
        ra_r, ui_r, mi_r = s_ra.at[f_slot], s_ui.at[f_slot], s_mi.at[f_slot]
        r_r = s_r.at[f_slot] if grads else None

        def conv_body(grp, past):
            past = list(past)
            pend = None
            for j in range(SUB):
                t = grp * SUB + j
                now = (in_x[strided(t), :] + b_x).astype(BF16).astype(F32)
                pos = pos_f[row8(t * SUB), :]
                acc = c_b + now * taps[0]
                for k in range(1, TAPS):
                    acc = acc + jnp.where(pos >= k, past[-k], 0.0) * taps[k]
                if grads:
                    xb_r[row8((t + BORROW) * SUB), :] = now
                if pend is None:
                    pend = acc
                else:
                    c16_r[pair(t - 1), :] = jnp.concatenate([pend, acc]).astype(BF16)
                    pend = None
                past = past[1:] + [now]
            return tuple(past)

        last3 = lax.fori_loop(0, n_groups, conv_body, tuple(halo))
        pre = jnp.dot(c16_r[...], wg_f[...], preferred_element_type=F32)
        for seq in range(SUB):
            for src, dst in ((py, in_y), (dm, in_d)):
                dst[pl.ds(seq * pitch, n_tok), :] = src[pl.ds(seq * n_tok, n_tok), :]
        pre_a[...] = pre[:, :LANES]
        pre_i[...] = pre[:, LANES:]
        h_r[pl.ds(0, SUB), :] = h_in

        def gate_body(grp, carry):
            h, sum_y = carry
            for j in range(SUB):
                t = grp * SUB + j
                rows = row8(t * SUB)
                if j % 2:
                    c = both[SUB:]
                else:
                    both = c16_r[pair(t), :].astype(F32)
                    c = both[:SUB]
                reset = pos_f[rows, :] == 0
                r = jax.nn.sigmoid(pre_a[rows, :] + b_a)
                i = jax.nn.sigmoid(pre_i[rows, :] + b_i)
                la = nsp * r
                a = jnp.exp(la)
                y2 = la + la
                poly = -y2 * (1.0 + y2 * (0.5 + y2 * (1.0 / 6.0 + y2 * (1.0 / 24.0))))
                q = jnp.maximum(jnp.where(y2 > -0.0625, poly, 1.0 - a * a), 1e-37)
                rm = lax.rsqrt(q)
                m = jnp.where(reset, 1.0, q * rm)
                ic = i * c
                k = a * ic * rm
                a = jnp.where(reset, 0.0, a)
                u = m * ic
                h = a * h + u
                h_r[row8(t * SUB + SUB), :] = h
                a_r[rows, :] = a
                k_r[rows, :] = k
                ra_r[rows, :] = la - la * r
                ui_r[rows, :] = u - u * i
                mi_r[rows, :] = m * i
                if grads:
                    r_r[rows, :] = r
                v = in_y[strided(t), :] + b_y
                v2 = v * v
                th = jnp.tanh(v * (GELU_K0 + GELU_K1 * v2))
                hv = 0.5 * v
                y = hv + hv * th
                dy = (0.5 + 0.5 * th) + hv * (1.0 - th * th) * (GELU_K0 + (3.0 * GELU_K1) * v2)
                d = in_d[strided(t), :]
                g_r[rows, :] = d * y
                out_m[strided(t), :] = h * y
                d_py = d * h * dy
                out_y[strided(t), :] = d_py
                if grads:
                    sum_y = sum_y + d_py
            return h, sum_y

        h_end, sum_y = lax.fori_loop(0, n_groups, gate_body, (h_in, jnp.zeros((SUB, LANES), F32)))
        if grads:
            @pl.when(lax.rem(f_step, n_tiles) == 0)
            def _():
                sy_o[...] = jnp.zeros_like(sy_o)

            sy_o[...] += sum_y

        @pl.when(me == 0)
        def _():
            for j, val in enumerate((h_end,) + last3):
                send[f_msg, pl.ds(SUB * j, SUB), :] = val

        for seq in range(SUB):
            mix_o[pl.ds(seq * n_tok, n_tok), :] = out_m[pl.ds(seq * pitch, n_tok), :].astype(BF16)
            dpy_o[pl.ds(seq * n_tok, n_tok), :] = out_y[pl.ds(seq * pitch, n_tok), :].astype(BF16)

        @pl.when(me == 0)
        def _():
            message(f_msg).start()

    @pl.when(jnp.logical_and(b_on, me == 0))
    def _():
        message(b_msg).wait_recv()

    @pl.when(jnp.logical_and(jnp.logical_and(b_step >= 1, b_step <= n_steps), me == 1))
    def _():
        message(lax.rem(b_step - 1 + MSG_SLOTS, MSG_SLOTS)).wait_send()

    @pl.when(b_on)
    def _():
        _, _, *taps, _, _, _, _ = param_rows(par_b)
        carry_in, *tail = [jnp.where(me == 1, 0.0, recv[b_msg, pl.ds(SUB * j, SUB), :]) for j in range(TAPS)]
        g_r, a_r, h_r, k_r = s_g.at[b_slot], s_a.at[b_slot], s_h.at[b_slot], s_k.at[b_slot]
        ra_r, ui_r, mi_r = s_ra.at[b_slot], s_ui.at[b_slot], s_mi.at[b_slot]
        r_r = s_r.at[b_slot] if grads else None
        xb_r = s_xb.at[b_slot] if grads else None
        zero = jnp.zeros((SUB, LANES), F32)

        def scan_body(back, carry):
            grp = n_groups - 1 - back
            adh, sum_a, sum_i, sum_p = carry
            pend = None
            for j in reversed(range(SUB)):
                t = grp * SUB + j
                rows = row8(t * SUB)
                dh = g_r[rows, :] + adh
                adh = a_r[rows, :] * dh
                dlog = adh * (h_r[rows, :] - k_r[rows, :])
                dpa = dlog * ra_r[rows, :]
                dpi = dh * ui_r[rows, :]
                d_c[rows, :] = dh * mi_r[rows, :]
                if grads:
                    sum_a = sum_a + dpa
                    sum_i = sum_i + dpi
                    sum_p = sum_p + dlog * r_r[rows, :]
                if pend is None:
                    pend = (dpa, dpi)
                else:
                    d_16[pair(t), :LANES] = jnp.concatenate([dpa, pend[0]]).astype(BF16)
                    d_16[pair(t), LANES:] = jnp.concatenate([dpi, pend[1]]).astype(BF16)
                    pend = None
            return adh, sum_a, sum_i, sum_p

        adh, sum_a, sum_i, sum_p = lax.fori_loop(0, n_groups, scan_body, (carry_in, zero, zero, zero))
        d_gate[...] = lax.dot_general(d_16[...], wg_b[...], CHAN, preferred_element_type=F32)

        def conv_body(grp, carry):
            ahead, sums = list(carry[:BORROW]), list(carry[BORROW:])
            for j in range(SUB):
                s = grp * SUB + j
                rows = row8(s * SUB)
                pos = pos_b[rows, :]
                dc = d_c[rows, :] + d_gate[rows, :]
                masked = [dc] + [jnp.where(pos >= k, dc, 0.0) for k in range(1, TAPS)]
                part = [val * tap for val, tap in zip(masked, taps)]
                done = ahead[0] + part[-1]
                out_b[strided(s + SUB - BORROW), :] = done
                ahead = [ahead[k] + part[-1 - k] for k in range(1, BORROW)] + [part[0]]
                if grads:
                    for k in range(TAPS):
                        sums[k] = sums[k] + masked[k] * xb_r[row8((s + BORROW - k) * SUB), :]
                    sums[TAPS] = sums[TAPS] + dc
                    sums[-1] = sums[-1] + done
            return tuple(ahead + sums)

        res = lax.fori_loop(0, n_groups, conv_body, (zero,) * (BORROW + (TAPS + 2 if grads else 0)))
        ends = [res[j] + tail[j] for j in range(BORROW)]
        for j in range(BORROW):
            out_b[strided(n_tok + SUB - BORROW + j), :] = ends[j]
        heads = [out_b[strided(SUB - BORROW + j), :] for j in range(BORROW)]

        @pl.when(me == 1)
        def _():
            for j, val in enumerate([adh] + heads):
                send[b_msg, pl.ds(SUB * j, SUB), :] = val

        for seq in range(SUB):
            dbr_o[pl.ds(seq * n_tok, n_tok), :] = out_b[pl.ds(seq * pitch + SUB, n_tok), :].astype(BF16)
        if grads:
            *sums, sum_x = res[BORROW:]
            sum_x = sum_x + sum(ends) - sum(heads)

            @pl.when(lax.rem(b_step, n_tiles) == 0)
            def _():
                gw_o[...] = jnp.zeros_like(gw_o)
                sb_o[...] = jnp.zeros_like(sb_o)

            for n, val in enumerate([sum_x] + sums + [sum_a, sum_i, sum_p]):
                sb_o[0, pl.ds(n * SUB, SUB), :] += val
            gw_o[0] += lax.dot_general(s_c16[b_slot], d_16[...], TOK, preferred_element_type=F32)

        @pl.when(me == 1)
        def _():
            message(b_msg).start()

    @pl.when(jnp.logical_and(f_on, me == 0))
    def _():
        message(f_msg).wait_send()


def middle(px, py, dm, pos_rep, par, w_gate, grads, collective_id):
    n_rows, width = px.shape
    n_tok = pos_rep.shape[1] // SUB
    tile = SUB * n_tok
    n_tiles, n_chunks = n_rows // tile, width // LANES
    n_steps = n_tiles * n_chunks

    def f_of(s):
        return jnp.clip(s - lax.axis_index("cp"), 0, n_steps - 1)

    def b_of(s):
        return jnp.clip(s - 2 + lax.axis_index("cp"), 0, n_steps - 1)

    def spec(shape, of, index):
        def index_map(s):
            k = of(s)
            return index(k // n_tiles, k % n_tiles)

        return pl.BlockSpec(shape, index_map)

    big = lambda of: spec((tile, LANES), of, lambda c, t: (t, c))
    both = (f_of, b_of)
    per_chunk = lambda of, *shape: spec((1,) + shape, of, lambda c, t: (c, 0, 0))
    in_specs = [spec((None, tile, LANES), of, lambda c, t: (t, 0, 0)) for of in both]
    in_specs += [spec((par.shape[0], LANES), of, lambda c, t: (0, c)) for of in both]
    in_specs += [spec((None,) + w_gate.shape[1:], of, lambda c, t: (c, 0, 0)) for of in both]
    in_specs += [big(f_of)] * 3
    out_specs = [big(f_of), big(f_of), big(b_of)]
    out_shape = [jax.ShapeDtypeStruct((n_rows, width), BF16)] * 3
    if grads:
        extra = ((b_of, LANES, 2 * LANES), (f_of, SUB, LANES), (b_of, N_SUMS * SUB, LANES))
        out_specs += [per_chunk(*e) for e in extra]
        out_shape += [jax.ShapeDtypeStruct((n_chunks,) + e[1:], F32) for e in extra]
    pitched = pltpu.VMEM((SUB * (n_tok + SUB), LANES), F32)
    flat = pltpu.VMEM((tile, LANES), F32)
    slots = pltpu.VMEM((SLOTS, tile, LANES), F32)
    small = pltpu.VMEM((SLOTS if grads else 1, tile if grads else SUB, LANES), F32)
    scratch = [
        slots, slots, pltpu.VMEM((SLOTS, tile + SUB, LANES), F32), slots, slots, slots, slots, pltpu.VMEM((SLOTS, tile, LANES), BF16), small,
        pltpu.VMEM((SLOTS if grads else 1, tile + BORROW * SUB if grads else SUB, LANES), F32),
        pitched, pitched, pitched, flat, flat, pitched, pitched, pltpu.VMEM((SUB * (n_tok + SUB) + SUB, LANES), F32), flat, pltpu.VMEM((tile, 2 * LANES), BF16), flat,
        *[pltpu.VMEM((MSG_SLOTS, TAPS * SUB, LANES), F32)] * 2, *[pltpu.SemaphoreType.DMA((MSG_SLOTS,))] * 2]
    return pl.pallas_call(
        functools.partial(middle_kernel, n_steps, n_tiles, n_tok, grads),
        grid=(n_steps + 2,), in_specs=in_specs, out_specs=out_specs, out_shape=out_shape, scratch_shapes=scratch,
        name="middle",
        cost_estimate=pl.CostEstimate(flops=n_rows * width * 1500, bytes_accessed=n_rows * width * 18, transcendentals=n_rows * width * 8),
        compiler_params=pltpu.CompilerParams(collective_id=collective_id, has_side_effects=True, vmem_limit_bytes=VMEM_LIMIT, dimension_semantics=("arbitrary",)),
    )(pos_rep, pos_rep, par, par, w_gate, w_gate, px, py, dm)


NORM_EPS = 1e-6
IN_SPECS = (P(None, "cp", None), P(None, "cp", None), P(None, "cp"), P(), P(None, "tp"), P("tp"), P(None, "tp"), P("tp"), P(None, "tp"), P("tp"), P("tp", None, None), P("tp"), P("tp", None, None), P("tp"), P("tp"), P("tp", None), P())
OUT_SPECS = (P(None, "cp", None), P(None, "cp", None), P(), P(None, "tp"), P("tp"), P(None, "tp"), P("tp"), P(None, "tp"), P("tp"), P("tp", None, None), P("tp"), P("tp", None, None), P("tp"), P("tp"), P("tp", None), P())


def params_of(*semantics):
    return pltpu.CompilerParams(vmem_limit_bytes=VMEM_LIMIT, dimension_semantics=semantics)


def norm_kernel(x_ref, scale_ref, n_ref):
    x = x_ref[...].astype(F32)
    inv = lax.rsqrt(jnp.mean(x * x, axis=-1, keepdims=True) + NORM_EPS)
    n_ref[...] = (x * inv * (1.0 + scale_ref[...])).astype(BF16)


def normalize(x, scale):
    rows, width = x.shape
    tile = 256
    return pl.pallas_call(
        norm_kernel, grid=(rows // tile,), name="normalize",
        in_specs=[pl.BlockSpec((tile, width), lambda i: (i, 0)), pl.BlockSpec((1, width), lambda i: (0, 0))],
        out_specs=pl.BlockSpec((tile, width), lambda i: (i, 0)), out_shape=jax.ShapeDtypeStruct(x.shape, BF16),
        cost_estimate=pl.CostEstimate(flops=rows * width * 600, bytes_accessed=4 * rows * width, transcendentals=rows),
        compiler_params=params_of("arbitrary"),
    )(x, scale)


def plain_up_kernel(n_weights, flip, lhs, *refs):
    for w, out in zip(refs[:n_weights], refs[n_weights:]):
        out[...] = lax.dot_general(lhs[...], w[...], CHAN if flip else ROW, preferred_element_type=F32)


def plain_up(lhs, weights, flip):
    rows, depth = lhs.shape
    width = weights[0].shape[0 if flip else 1]
    n = len(weights)
    bm, bn = 1024, 512 // n
    w_spec = pl.BlockSpec((bn, depth), lambda j, i: (j, 0)) if flip else pl.BlockSpec((depth, bn), lambda j, i: (0, j))
    return pl.pallas_call(
        functools.partial(plain_up_kernel, n, flip), grid=(width // bn, rows // bm), name="plain_up",
        in_specs=[pl.BlockSpec((bm, depth), lambda j, i: (i, 0))] + [w_spec] * n,
        out_specs=[pl.BlockSpec((bm, bn), lambda j, i: (i, j))] * n, out_shape=[jax.ShapeDtypeStruct((rows, width), F32)] * n,
        cost_estimate=pl.CostEstimate(flops=2 * n * rows * width * depth, bytes_accessed=4 * rows * depth, transcendentals=0),
        compiler_params=params_of("arbitrary", "arbitrary"),
    )(lhs, *weights)


def up_kernel(n_weights, n_parts, flip, lhs, *refs):
    parts = [refs[n_parts * w:n_parts * (w + 1)] for w in range(n_weights)]
    outs, held = refs[n_parts * n_weights:-1], refs[-1]
    outs, stored = outs[:n_weights], outs[n_weights:]
    me = lax.axis_index("cp")
    j = pl.program_id(1)
    cols = outs[0].shape[1]

    @pl.when(pl.program_id(0) == 0)
    def _():
        for w, part in enumerate(parts):
            mine = pl.ds(w * cols, cols)
            for q, ref in enumerate(part):
                depth = ref.shape[1] if flip else ref.shape[0]
                place = lax.rem(me * 2 + q, n_parts)
                at = pl.ds(pl.multiple_of(place * depth, depth), depth)
                val = ref[...].astype(BF16)
                if flip:
                    held[j, mine, at] = val
                else:
                    held[j, at, mine] = val
                stored[w][(slice(None), at) if flip else (at, slice(None))] = val

    res = lax.dot_general(lhs[...], held[j], CHAN if flip else ROW, preferred_element_type=F32)
    for w, out in enumerate(outs):
        out[...] = res[:, w * cols:(w + 1) * cols]


def up(lhs, weights, flip, n_rows):
    depth = lhs.shape[1]
    n, n_parts = len(weights), len(weights[0])
    width = weights[0][0][0].shape[-2 if flip else -1]
    bm, bn = 1024, 256 // n
    steps = width // bn

    def block(size, lead, of):
        shape = (bn, size) if flip else (size, bn)
        return pl.BlockSpec((None,) * len(lead) + shape, lambda i, j: lead + ((of(i, j), 0) if flip else (0, of(i, j))))

    def once(i, j):
        return jnp.where(i == 0, j, steps - 1)

    out_specs = [pl.BlockSpec((bm, bn), lambda i, j: (i, j))] * n
    out_shape = [jax.ShapeDtypeStruct((n_rows, width), F32)] * n
    out_specs += [block(depth, (), once)] * n
    out_shape += [jax.ShapeDtypeStruct((width, depth) if flip else (depth, width), BF16)] * n
    return pl.pallas_call(
        functools.partial(up_kernel, n, n_parts, flip), grid=(n_rows // bm, steps), name="up",
        in_specs=[pl.BlockSpec((bm, depth), lambda i, j: (i, 0))] + [block(depth // n_parts, lead, once) for part in weights for _, lead in part],
        out_specs=out_specs, out_shape=out_shape,
        scratch_shapes=[pltpu.VMEM((steps, n * bn, depth) if flip else (steps, depth, n * bn), BF16)],
        cost_estimate=pl.CostEstimate(flops=2 * n * n_rows * width * depth, bytes_accessed=4 * n_rows * depth, transcendentals=0),
        compiler_params=params_of("arbitrary", "arbitrary"),
    )(lhs, *[array for part in weights for array, _ in part])


def finish_rows(rows, first, dn_ref, x_ref, gz_ref, scale_ref, grad_ref, sum_ref):
    width = x_ref.shape[1]
    tiles = [pl.ds(n * LANES, LANES) for n in range(width // LANES)]
    here = pl.ds(pl.multiple_of(first, rows), rows)
    square = cross = jnp.zeros((rows, LANES), F32)
    for cols in tiles:
        x = x_ref[here, cols].astype(F32)
        square = square + x * x
        cross = cross + x * (dn_ref[here, cols] * scale_ref[:, cols])
    inv = lax.rsqrt(jnp.sum(square, axis=-1, keepdims=True) / width + NORM_EPS)
    inv_b = jnp.broadcast_to(inv, (rows, LANES))
    pull = jnp.broadcast_to(inv * inv * inv * (jnp.sum(cross, axis=-1, keepdims=True) / width), (rows, LANES))
    for cols in tiles:
        x = x_ref[here, cols].astype(F32)
        gz = gz_ref[here, cols].astype(F32)
        dn = dn_ref[here, cols] * inv_b
        grad_ref[here, cols] = (gz + dn * scale_ref[:, cols] - x * pull).astype(BF16)
        for which, val in enumerate((dn * x, gz)):
            sum_ref[which, :, cols] += sum(val[SUB * r:SUB * (r + 1)] for r in range(rows // SUB))


def z_kernel(n_own, n_far, n_cols, *refs):
    own, far, right = refs[:n_own], refs[n_own:n_own + 2 * n_far], refs[n_own + 2 * n_far:2 * n_own + 3 * n_far]
    x_ref, bias_ref, dn_ref, x_rows, gz_rows, scale_ref = refs[2 * n_own + 3 * n_far:][:6]
    out_ref, grad_ref, sum_ref = refs[-4:-1]
    far_16 = refs[-1]
    unit = 4 * SUB
    turns = out_ref.shape[1] // n_cols
    units = dn_ref.shape[0] // unit // turns

    @pl.when(jnp.logical_and(pl.program_id(0) == 0, pl.program_id(1) == 0))
    def _():
        sum_ref[...] = jnp.zeros_like(sum_ref)
        for k, ref in enumerate(far):
            half = ref.shape[0]
            far_16[k // 2, pl.ds(k % 2 * half, half), :] = ref[...].astype(BF16)

    def column(c, _):
        cols = pl.ds(pl.multiple_of(c * n_cols, n_cols), n_cols)
        acc = x_ref[:, cols].astype(F32) + bias_ref[:, cols]
        for lhs, rhs in zip(list(own) + [far_16.at[k] for k in range(n_far)], right):
            acc = acc + jnp.dot(lhs[...], rhs[:, cols], preferred_element_type=F32)
        out_ref[:, cols] = acc.astype(BF16)
        for u in range(units):
            finish_rows(unit, (c * units + u) * unit, dn_ref, x_rows, gz_rows, scale_ref, grad_ref, sum_ref)
        return 0

    lax.fori_loop(0, turns, column, 0)


def outputs(own, far, rights, x, bias, dn, gz, scale, first_row, into):
    rows, width = dn.shape
    depth = own[0].shape[1]
    bm, bn = 1024, 512
    n_row, n_col = rows // bm, width // bn
    share = rows // (n_row * n_col)
    skip, skip_share = first_row // bm, first_row // share
    tile = pl.BlockSpec((bm, bn), lambda i, j: (i + skip, j))
    part = pl.BlockSpec((share, width), lambda i, j: (i * n_col + j, 0))
    line = pl.BlockSpec((share, width), lambda i, j: (i * n_col + j + skip_share, 0))
    args = list(own) + [v for pair in far for v in pair] + list(rights) + [x, bias, dn, x, gz, scale] + list(into)
    in_specs = [pl.BlockSpec((bm, depth), lambda i, j: (i + skip, 0))] * len(own)
    in_specs += [pl.BlockSpec((bm // 2, depth), lambda i, j: (0, 0))] * (2 * len(far))
    in_specs += [pl.BlockSpec((depth, bn), lambda i, j: (0, j))] * len(rights)
    in_specs += [tile, pl.BlockSpec((1, bn), lambda i, j: (0, j)), part, line, line, pl.BlockSpec((1, width), lambda i, j: (0, 0))]
    in_specs += [pl.BlockSpec(memory_space=pl.ANY)] * len(into)
    return pl.pallas_call(
        functools.partial(z_kernel, len(own), len(far), 256), grid=(n_row, n_col), name="outputs",
        in_specs=in_specs, out_specs=[tile, line, pl.BlockSpec((2, SUB, width), lambda i, j: (0, 0, 0))],
        out_shape=[jax.ShapeDtypeStruct(x.shape, BF16), jax.ShapeDtypeStruct(x.shape, BF16), jax.ShapeDtypeStruct((2, SUB, width), F32)],
        scratch_shapes=[pltpu.VMEM((max(len(far), 1), bm if far else 2 * SUB, depth), BF16)],
        input_output_aliases={len(args) - len(into) + k: k for k in range(len(into))},
        cost_estimate=pl.CostEstimate(flops=2 * len(rights) * rows * width * depth, bytes_accessed=rows * width * 20, transcendentals=rows),
        compiler_params=params_of("arbitrary", "arbitrary"),
    )(*args)


def dn_kernel(n_pairs, *refs):
    left, right, out_ref = refs[:n_pairs], refs[n_pairs:2 * n_pairs], refs[2 * n_pairs]

    def column(c, _):
        cols = pl.ds(pl.multiple_of(c * 256, 256), 256)
        acc = lax.dot_general(left[0][...], right[0][cols, :], CHAN, preferred_element_type=F32)
        for lhs, rhs in zip(left[1:], right[1:]):
            acc = acc + lax.dot_general(lhs[...], rhs[cols, :], CHAN, preferred_element_type=F32)
        out_ref[:, cols] = acc
        return 0

    lax.fori_loop(0, out_ref.shape[1] // 256, column, 0)


def grad_normed(lefts, rights, first_row, rows):
    depth = lefts[0].shape[1]
    width = rights[0].shape[0]
    bm, bn = 1024, 512
    skip = first_row // bm
    n = len(lefts)
    return pl.pallas_call(
        functools.partial(dn_kernel, n), grid=(rows // bm, width // bn), name="grad_normed",
        in_specs=[pl.BlockSpec((bm, depth), lambda i, j: (i + skip, 0))] * n + [pl.BlockSpec((bn, depth), lambda i, j: (j, 0))] * n,
        out_specs=pl.BlockSpec((bm, bn), lambda i, j: (i, j)), out_shape=jax.ShapeDtypeStruct((rows, width), F32),
        cost_estimate=pl.CostEstimate(flops=2 * n * rows * width * depth, bytes_accessed=450000000, transcendentals=0),
        compiler_params=params_of("arbitrary", "arbitrary"),
    )(*lefts, *rights)


def token_product(lhs, rhs):
    return lax.dot_general(lhs, rhs, TOK, preferred_element_type=F32)


def spread_positions(seg_pos):
    n_seq, n_tok = seg_pos.shape
    pos = jnp.swapaxes(seg_pos.reshape(n_seq // SUB, SUB, n_tok), 1, 2).reshape(n_seq // SUB, n_tok * SUB, 1)
    return jnp.broadcast_to(pos, (n_seq // SUB, n_tok * SUB, LANES))


def stack_params(b_x, b_y, conv_w, conv_b, b_a, b_i, a_param):
    rows = [b_x, b_y, conv_w[0], conv_w[1], conv_w[2], conv_w[3], conv_b, b_a, b_i]
    rows = [row.astype(F32) for row in rows] + [-8.0 * jax.nn.softplus(a_param)]
    return jnp.concatenate([jnp.stack(rows), jnp.zeros((16 - len(rows), a_param.shape[0]), F32)], axis=0)


def block_body(x_in, grad_z, seg_pos, norm_scale, w_x, b_x, w_y, b_y, conv_w, conv_b, w_a, b_a, w_i, b_i, a_param, w_out, b_out):
    me = lax.axis_index("cp")
    n_seq, n_tok, d_model = x_in.shape
    n_rows = n_seq * n_tok
    width = a_param.shape[0]
    x = x_in.reshape(n_rows, d_model)
    gz = grad_z.reshape(n_rows, d_model)
    scale = norm_scale.astype(F32).reshape(1, d_model)

    def swap_x(v):
        return lax.ppermute(v, "tp", [(j, j ^ 1) for j in range(4)])

    def swap_y(v):
        return lax.ppermute(v, "tp", [(j, j ^ 2) for j in range(4)])

    def swap_core(v):
        return lax.ppermute(v, "cp", [(0, 1), (1, 0)])

    tile = SUB * n_tok
    shared = n_rows - tile

    par = stack_params(b_x, b_y, conv_w, conv_b, b_a, b_i, a_param)
    w_gate = jnp.concatenate([w_a, w_i], axis=2)
    small = jnp.concatenate([par.reshape(-1), w_gate.astype(F32).reshape(-1)]).reshape(-1, LANES)
    smalls = [lax.ppermute(small, "tp", [(j, j ^ far) for j in range(4)]) for far in range(1, 4)]

    def after(values, *before):
        return lax.optimization_barrier((values, before))[0]

    def quarter(w, axis, q):
        size = d_model // 4
        return lax.dynamic_slice_in_dim(w, (me * 2 + q) * size, size, axis).astype(F32)

    def to_neighbours(weights, axis, before):
        weights = after(weights, before)
        sent = [jnp.stack([quarter(w, axis, q) for w in weights]) for q in range(2)]
        return [swap_x(v) for v in sent], [swap_y(v) for v in sent]

    def cores(values):
        return values, [swap_core(v) for v in values]

    group_a = to_neighbours((w_x, w_y), 0, small)

    def unpack(s):
        flat = s.reshape(-1)
        return flat[:par.size].reshape(par.shape), lax.optimization_barrier(flat[par.size:]).reshape(w_gate.shape).astype(BF16)

    def onward(group):
        return [swap_y(group[0][0]), swap_x(group[1][1])]

    def quarters(side, n):
        own, other = side
        return [tuple((v, (k,)) for v in list(own) + list(other)) for k in range(n)]

    normed = normalize(x, scale)
    pos_rep = spread_positions(seg_pos)
    px, py = plain_up(normed, [w_x, w_y], False)
    group_b = to_neighbours((w_out,), 1, px)
    dm, = plain_up(after(gz, px), [w_out], True)
    mixed, dpy, dbr, g_gate, s_y, s_b = middle(px, py, dm, pos_rep, par, w_gate, True, 0)
    g_w_out = token_product(mixed, gz)
    g_w_y = token_product(normed, dpy)
    group_a = after(group_a, g_w_out, g_w_y)
    side_x, side_y = [cores(values) for values in group_a]
    g_w_x = token_product(normed, after(dbr, g_w_y))
    diag_a = onward(after(group_a, g_w_x))

    px_x, py_x, wx_x, wy_x = up(after(normed, g_w_x), quarters(side_x, 2), False, shared)
    px_y, py_y, wx_y, wy_y = up(after(normed, px_x), quarters(side_y, 2), False, shared)
    group_b, smalls = after((group_b, smalls), px_y)
    out_x, out_y = [cores(values) for values in group_b]
    diag_b = onward(group_b)
    dn_tail = grad_normed(after([dbr, dpy], px_y), [w_x, w_y], shared, tile)
    dm_x, wo_x = up(after(gz, dn_tail), quarters(out_x, 1), True, shared)
    mixed_x, dpy_x, dbr_x = middle(px_x, py_x, dm_x, pos_rep, *unpack(smalls[0]), False, 1)
    dm_y, wo_y = up(after(gz, mixed_x), quarters(out_y, 1), True, shared)
    mixed_y, dpy_y, dbr_y = middle(px_y, py_y, dm_y, pos_rep, *unpack(smalls[1]), False, 1)
    diag_a, diag_b = after((diag_a, diag_b), mixed_y)
    diag_a, diag_b = cores(diag_a), cores(diag_b)
    rows_tail = [after(mixed, mixed_y)[shared + h * (tile // 2):shared + (h + 1) * (tile // 2)].astype(F32) for h in range(2)]
    tail_x, tail_y = [swap_x(v) for v in rows_tail], [swap_y(v) for v in rows_tail]
    px_d, py_d, wx_d, wy_d = up(after(normed, mixed_y), quarters(diag_a, 2), False, shared)
    dn_tail = lax.psum(after(dn_tail, px_d), "tp")
    dm_d, wo_d = up(after(gz, px_d), quarters(diag_b, 1), True, shared)
    mixed_d, dpy_d, dbr_d = middle(px_d, py_d, dm_d, pos_rep, *unpack(smalls[2]), False, 1)

    far_x, far_y = after((tail_x, tail_y), mixed_d)
    far_d = [swap_y(far_x[0]), swap_x(far_y[1])]
    s_y = jnp.sum(s_y, axis=1).reshape(1, width)
    s_b = jnp.swapaxes(jnp.sum(s_b.reshape(s_b.shape[0], N_SUMS, SUB, LANES), axis=2), 0, 1).reshape(N_SUMS, width)
    own_grads = lax.psum(after((g_w_x, g_w_y, g_w_out, g_gate, jnp.concatenate([s_y, s_b])), mixed_d), "cp")
    g_w_x, g_w_y, g_w_out, g_gate, lines = own_grads
    wx_all, wy_all, wo_all = [w_x, wx_x, wx_y, wx_d], [w_y, wy_x, wy_y, wy_d], [w_out, wo_x, wo_y, wo_d]
    dn = grad_normed([dbr, dbr_x, dbr_y, dbr_d, dpy, dpy_x, dpy_y, dpy_d], wx_all + wy_all, 0, shared)
    bias = b_out.astype(F32).reshape(1, d_model)
    z_out, grad_x, sums_x = outputs([mixed, mixed_x, mixed_y, mixed_d], [], wo_all, x, bias, dn, gz, 1.0 + scale, 0, ())
    z_out, grad_x, sums_t = outputs([mixed], [far_x, far_y, far_d], wo_all, x, bias, after(dn_tail, *own_grads), gz, 1.0 + scale, shared, (z_out, grad_x))
    z_out = z_out.reshape(x_in.shape)
    sums_x = jnp.sum(sums_x + sums_t, axis=1)

    sums_x = lax.psum(sums_x, "cp")
    s_y, s_b = lines[0], lines[1:]
    g_a = -8.0 * s_b[8] * jax.nn.sigmoid(a_param)
    return (z_out, grad_x.reshape(x_in.shape), sums_x[0], g_w_x, s_b[0], g_w_y, s_y, s_b[1:5], s_b[5], g_gate[:, :, :LANES], s_b[6], g_gate[:, :, LANES:], s_b[7], g_a, g_w_out, sums_x[1])


def solution(mesh):
    return jax.shard_map(block_body, mesh=mesh, in_specs=IN_SPECS, out_specs=OUT_SPECS, check_vma=False)
```

time: 2860 us -> 2020 us (0.71)
  waiting for transfers between devices: 2060 us -> 341 us
  Pallas kernels: 150 us -> 1410 us
  matrix products: 409 us -> 131 us
  other arithmetic: 176 us -> 25.4 us
    psum x4 -> x2, waiting for transfers between devices: 2060 us -> 0.01 us  [the longest x1 0.01 us: block_body(): dn_tail = lax.psum(after(dn_tail, px_d), 'tp')]
    pallas_call x0 -> x13, Pallas kernels: none -> 977 us  [the longest x6 340 us: up(): pl.pallas_call(functools.partial(up_kernel, n, n_parts, flip), grid=(n_ro...]
    ppermute x0 -> x33, waiting for transfers between devices: none -> 341 us  [the longest x9 170 us: swap_x(): return lax.ppermute(v, 'tp', [(j, j ^ 1) for j in range(4)])]
    pallas_call x1 -> x4, Pallas kernels: 150 us -> 437 us  [middle(): pl.pallas_call(functools.partial(middle_kernel, n_steps, n_tiles, n_tok,...]
    dot_general x9 -> x3, matrix products: 409 us -> 131 us  [token_product(): return lax.dot_general(lhs, rhs, TOK, preferred_element_type=F32)]
    convert_element_type x3, other arithmetic: 108 us -> 2.94 us  [the longest x1 2.24 us: block_body(): after(mixed, mixed_y)]
    reduce_sum x5 -> x3, other arithmetic: 56.7 us -> 1.14 us  [the longest x1 1.05 us: block_body(): sums_x = jnp.sum(sums_x + sums_t, axis=1)]
  transfers between devices with their start and end apart: 4 -> 35, of which waited for: 4 -> 9; matrix products, arithmetic and copies ran while one was open for 11% -> 8% of each run, Pallas kernels for 0% -> 64%
where the time goes in v2:
time: 2020 us; the launch traced here: 2010 us
  Pallas kernels  1410 us (70%)
  waiting for transfers between devices  341 us (17%)
  matrix products  131 us (6%)
  local copies, waits for them, and re-layouts  54 us (3%)
  starting transfers between devices  26.8 us (1%)
  other arithmetic  25.4 us (1%)
    pallas_call x4, Pallas kernels, middle(): pl.pallas_call(functools.partial(middle_kernel, n_steps, n_tiles, n_tok,...  437 us
    pallas_call x6, Pallas kernels, up(): pl.pallas_call(functools.partial(up_kernel, n, n_parts, flip), grid=(n_ro...  340 us
    pallas_call x2, Pallas kernels, grad_normed(): pl.pallas_call(functools.partial(dn_kernel, n), grid=(rows // bm, width /...  259 us
    pallas_call x2, Pallas kernels, outputs(): pl.pallas_call(functools.partial(z_kernel, len(own), len(far), 256), grid...  221 us
    ppermute x9, waiting for transfers between devices, swap_x(): return lax.ppermute(v, 'tp', [(j, j ^ 1) for j in range(4)])  170 us
    dot_general x3, matrix products, token_product(): return lax.dot_general(lhs, rhs, TOK, preferred_element_type=F32)  131 us
    pallas_call x2, Pallas kernels, plain_up(): pl.pallas_call(functools.partial(plain_up_kernel, n, flip), grid=(width /...  124 us
    ppermute x9, waiting for transfers between devices, swap_y(): return lax.ppermute(v, 'tp', [(j, j ^ 2) for j in range(4)])  72 us
  transfers between devices with their start and end apart: 35, of which 9 were waited for; matrix products, arithmetic and copies ran while one was open for 8% of the time, Pallas kernels for 64%

profile of v2, /device:TPU:0, one launch (start us, length us, event | category | flops | bytes accessed | tf_op | source)
XLA Modules:
  0.0 2013.7 jit_solution(12447065097496805555)
XLA Ops:
  12.4 1.0 constant_dynamic-update-slice_fusion.1
  13.4 1.0 constant_dynamic-update-slice_fusion.wg_f.wg_b
  15.0 1.1 maximum_bitcast_fusion
  16.1 4.4 dynamic-slice_bitcast_fusion
  20.6 3.8 maximum_convert_fusion.1
  24.4 3.3 collective-permute-start.10
  27.7 1.5 collective-permute-start.8
  29.2 3.9 maximum_convert_fusion
  34.3 33.9 %normalize.1.lhs = bf16[4096,4096]{1,0:T(8,128)(2,1)} custom-call(bf16[4096,4096]{1,0:T(8,128)(2,1)} %bitcast.62, f32[1,4096]{1,0:T(1,128)} %bitcast.92), custom_call_target="tpu_custom_call" | custom-call | flops 10066329600 | bytes 67108864 | tf_op jit(solution)/shard_map/normalize/pallas_call | solution.py:355
  68.2 80.7 %plain_up.2 = (f32[4096,1024]{1,0:T(8,128)}, f32[4096,1024]{1,0:T(8,128)}) custom-call(bf16[4096,4096]{1,0:T(8,128)(2,1)} %normalize.1.lhs, bf16[4096,1024]{1,0:T(8,128)(2,1)} %refs_8_.1, bf16[4096,1024]{1,0:T(8,128)(2,1)} %refs_12_.1), custom_call_target="tpu_custom_call" | custom-call | flops 68719476736 | bytes 67108864 | tf_op jit(solution)/shard_map/plain_up/pallas_call | solution.py:375
  149.2 43.0 %plain_up.3.dm = f32[4096,1024]{1,0:T(8,128)} custom-call(bf16[4096,4096]{1,0:T(8,128)(2,1)} %bitcast.67, bf16[1024,4096]{1,0:T(8,128)(2,1)} %refs_7_.1), custom_call_target="tpu_custom_call" | custom-call | flops 34359738368 | bytes 67108864 | tf_op jit(solution)/shard_map/plain_up/pallas_call | solution.py:375
  192.2 2.2 broadcast_in_dim.11.pos_f.pos_b
  194.4 147.3 %middle.4 = (bf16[4096,1024]{1,0:T(8,128)(2,1)}, bf16[4096,1024]{1,0:T(8,128)(2,1)}, bf16[4096,1024]{1,0:T(8,128)(2,1)}, f32[8,128,256]{2,1,0:T(8,128)}, f32[8,8,128]{2,1,0:T(8,128)}, /*index=5*/f32[8,72,128]{2,1,0:T(8,128)}) custom-call(s32[4,1024,128]{2,1,0:T(8,128)} %broadcast_in_dim.11.pos_f.pos_b, s32[4,1024,128]{2,1,0:T(8,128)} %broadcast_in_dim.11.pos_f.pos_b, ...), custom_call_target="tpu_custom_call" | custom-call | flops 6291456000 | bytes 75497472 | tf_op jit(solution)/shard_map/middle/pallas_call | solution.py:328
  341.7 44.1 %fusion.5 = f32[1024,4096]{1,0:T(8,128)} fusion(bf16[4096,1024]{1,0:T(8,128)(2,1)} %get-tuple-element.133.refs_0_, bf16[4096,4096]{1,0:T(8,128)(2,1)} %bitcast.68), kind=kOutput, calls=%fused_computation.32 | convolution fusion | flops 34359738368 | bytes 58720256 | tf_op jit(solution)/shard_map/dot_general | solution.py:547
  385.8 42.7 %fusion.3 = f32[4096,1024]{1,0:T(8,128)} fusion(bf16[4096,4096]{1,0:T(8,128)(2,1)} %normalize.1.lhs, bf16[4096,1024]{1,0:T(8,128)(2,1)S(1)} %copy-done.17), kind=kOutput, calls=%fused_computation.30 | convolution fusion | flops 34359738368 | bytes 58720256 | tf_op jit(solution)/shard_map/dot_general | solution.py:547
  429.0 2.0 collective-permute-start.4
  431.5 44.1 %fusion.4 = f32[4096,1024]{1,0:T(8,128)} fusion(bf16[4096,4096]{1,0:T(8,128)(2,1)} %normalize.1.lhs, bf16[4096,1024]{1,0:T(8,128)(2,1)} %get-tuple-element.121.refs_0_), kind=kOutput, calls=%fused_computation.31 | convolution fusion | flops 34359738368 | bytes 58720256 | tf_op jit(solution)/shard_map/dot_general | solution.py:547
  475.6 4.4 bitcast_convert_fusion
  480.1 1.5 collective-permute-start.5
  482.1 72.2 %up.6 = (f32[3072,1024]{1,0:T(8,128)}, f32[3072,1024]{1,0:T(8,128)}, bf16[4096,1024]{1,0:T(8,128)(2,1)}, bf16[4096,1024]{1,0:T(8,128)(2,1)}) custom-call(bf16[4096,4096]{1,0:T(8,128)(2,1)} %normalize.1.lhs, f32[2,1024,1024]{2,1,0:T(8,128)} %collective-permute-done.7.refs_0_.refs_4_, f32[2,1024,1024]{2,1,0:T(8,128)} %collective-permute-done.8.refs_1_.refs_5_, ...), custom_call_target="tpu_custom_call" | custom-call | flops 51539607552 | bytes 50331648 | tf_op jit(solution)/shard_map/up/pallas_call | solution.py:430
  554.4 2.0 collective-permute-start.1
  556.4 1.5 collective-permute-start.3
  558.4 72.4 %up.7 = (f32[3072,1024]{1,0:T(8,128)}, f32[3072,1024]{1,0:T(8,128)}, bf16[4096,1024]{1,0:T(8,128)(2,1)}, bf16[4096,1024]{1,0:T(8,128)(2,1)}) custom-call(bf16[4096,4096]{1,0:T(8,128)(2,1)} %normalize.1.lhs, f32[2,1024,1024]{2,1,0:T(8,128)} %collective-permute-done.9.refs_0_.refs_4_, f32[2,1024,1024]{2,1,0:T(8,128)} %collective-permute-done.10.refs_1_.refs_5_, ...), custom_call_target="tpu_custom_call" | custom-call | flops 51539607552 | bytes 50331648 | tf_op jit(solution)/shard_map/up/pallas_call | solution.py:430
  630.8 57.1 %collective-permute-done.6 = f32[2176,128]{1,0:T(8,128)S(1)} collective-permute-done((f32[2176,128]{1,0:T(8,128)S(1)}, f32[2176,128]{1,0:T(8,128)S(1)}, u32[]{:S(2)}, u32[]{:S(2)}) %collective-permute-start.6) | collective-permute-done | bytes 1114144 | tf_op jit(solution)/shard_map/ppermute | solution.py:586
  687.9 1.5 collective-permute-start.23
  690.0 72.0 %collective-permute-done.3.refs_1_ = f32[1,1024,1024]{2,1,0:T(8,128)} collective-permute-done((f32[1,1024,1024]{2,1,0:T(8,128)}, f32[1,1024,1024]{2,1,0:T(8,128)}, u32[]{:S(2)}, u32[]{:S(2)}) %collective-permute-start.3) | collective-permute-done | bytes 4194336 | tf_op jit(solution)/shard_map/ppermute | solution.py:575
  762.5 1.3 slice_bitcast_fusion.2
  763.8 5.6 collective-permute-done.15.refs_2_
  769.6 25.0 %grad_normed.2 = f32[1024,4096]{1,0:T(8,128)} custom-call(bf16[4096,1024]{1,0:T(8,128)(2,1)} %get-tuple-element.121.refs_0_, bf16[4096,1024]{1,0:T(8,128)(2,1)} %get-tuple-element.122.refs_1_.refs_4_, bf16[4096,1024]{1,0:T(8,128)(2,1)} %refs_8_.1, bf16[4096,1024]{1,0:T(8,128)(2,1)} %refs_12_.1), custom_call_target="tpu_custom_call" | custom-call | flops 17179869184 | bytes 450000000 | tf_op jit(solution)/shard_map/grad_normed/pallas_call | solution.py:537
  794.5 1.0 convert_element_type.69.wg_f.wg_b
  796.2 1.0 convert_element_type.67.wg_f.wg_b
  797.8 2.0 collective-permute-start.26
  799.8 40.4 %up.8 = (f32[3072,1024]{1,0:T(8,128)}, bf16[1024,4096]{1,0:T(8,128)(2,1)}) custom-call(bf16[4096,4096]{1,0:T(8,128)(2,1)} %bitcast.69, f32[1,1024,1024]{2,1,0:T(8,128)} %collective-permute-done.refs_0_, f32[1,1024,1024]{2,1,0:T(8,128)} %collective-permute-done.1.refs_1_, f32[1,1024,1024]{2,1,0:T(8,128)} %collective-permute-done.15.refs_2_, ...), custom_call_target="tpu_custom_call" | custom-call | flops 25769803776 | bytes 50331648 | tf_op jit(solution)/shard_map/up/pallas_call | solution.py:430
  840.2 96.4 %middle.5 = (bf16[3072,1024]{1,0:T(8,128)(2,1)}, bf16[3072,1024]{1,0:T(8,128)(2,1)}, bf16[3072,1024]{1,0:T(8,128)(2,1)}) custom-call(s32[4,1024,128]{2,1,0:T(8,128)} %broadcast_in_dim.11.pos_f.pos_b, s32[4,1024,128]{2,1,0:T(8,128)} %broadcast_in_dim.11.pos_f.pos_b, f32[16,1024]{1,0:T(8,128)} %reshape.113.par_f.par_b, f32[16,1024]{1,0:T(8,128)} %reshape.113.par_f.par_b, ...), custom_call_target="tpu_custom_call" | custom-call | flops 4718592000 | bytes 56623104 | tf_op jit(solution)/shard_map/middle/pallas_call | solution.py:328
  936.7 40.4 %up.9 = (f32[3072,1024]{1,0:T(8,128)}, bf16[1024,4096]{1,0:T(8,128)(2,1)}) custom-call(bf16[4096,4096]{1,0:T(8,128)(2,1)} %bitcast.70, f32[1,1024,1024]{2,1,0:T(8,128)} %collective-permute-done.2.refs_0_, f32[1,1024,1024]{2,1,0:T(8,128)} %collective-permute-done.3.refs_1_, f32[1,1024,1024]{2,1,0:T(8,128)} %collective-permute-done.17.refs_2_, ...), custom_call_target="tpu_custom_call" | custom-call | flops 25769803776 | bytes 50331648 | tf_op jit(solution)/shard_map/up/pallas_call | solution.py:430
  977.1 96.5 %middle.6 = (bf16[3072,1024]{1,0:T(8,128)(2,1)}, bf16[3072,1024]{1,0:T(8,128)(2,1)}, bf16[3072,1024]{1,0:T(8,128)(2,1)}) custom-call(s32[4,1024,128]{2,1,0:T(8,128)} %broadcast_in_dim.11.pos_f.pos_b, s32[4,1024,128]{2,1,0:T(8,128)} %broadcast_in_dim.11.pos_f.pos_b, f32[16,1024]{1,0:T(8,128)} %reshape.112.par_f.par_b, f32[16,1024]{1,0:T(8,128)} %reshape.112.par_f.par_b, ...), custom_call_target="tpu_custom_call" | custom-call | flops 4718592000 | bytes 56623104 | tf_op jit(solution)/shard_map/middle/pallas_call | solution.py:328
  1074.2 13.0 collective-permute-done.27.refs_2_.refs_6_
  1087.2 12.0 collective-permute-done.28.refs_3_.refs_7_
  1099.2 72.6 %up.10 = (f32[3072,1024]{1,0:T(8,128)}, f32[3072,1024]{1,0:T(8,128)}, bf16[4096,1024]{1,0:T(8,128)(2,1)}, bf16[4096,1024]{1,0:T(8,128)(2,1)}) custom-call(bf16[4096,4096]{1,0:T(8,128)(2,1)} %normalize.1.lhs, f32[2,1024,1024]{2,1,0:T(8,128)} %collective-permute-done.23.refs_0_.refs_4_, f32[2,1024,1024]{2,1,0:T(8,128)} %collective-permute-done.24.refs_1_.refs_5_, ...), custom_call_target="tpu_custom_call" | custom-call | flops 51539607552 | bytes 50331648 | tf_op jit(solution)/shard_map/up/pallas_call | solution.py:430
  1174.1 1.0 convert_element_type.73.wg_f.wg_b
  1175.7 5.3 collective-permute-done.29.refs_2_
  1181.1 6.0 collective-permute-done.30.refs_3_
  1187.1 41.8 %up.11 = (f32[3072,1024]{1,0:T(8,128)}, bf16[1024,4096]{1,0:T(8,128)(2,1)}) custom-call(bf16[4096,4096]{1,0:T(8,128)(2,1)} %bitcast.71, f32[1,1024,1024]{2,1,0:T(8,128)} %collective-permute-done.25.refs_0_, f32[1,1024,1024]{2,1,0:T(8,128)} %collective-permute-done.26.refs_1_, f32[1,1024,1024]{2,1,0:T(8,128)} %collective-permute-done.29.refs_2_, ...), custom_call_target="tpu_custom_call" | custom-call | flops 25769803776 | bytes 50331648 | tf_op jit(solution)/shard_map/up/pallas_call | solution.py:430
  1228.9 96.4 %middle.7 = (bf16[3072,1024]{1,0:T(8,128)(2,1)}, bf16[3072,1024]{1,0:T(8,128)(2,1)}, bf16[3072,1024]{1,0:T(8,128)(2,1)}) custom-call(s32[4,1024,128]{2,1,0:T(8,128)} %broadcast_in_dim.11.pos_f.pos_b, s32[4,1024,128]{2,1,0:T(8,128)} %broadcast_in_dim.11.pos_f.pos_b, f32[16,1024]{1,0:T(8,128)} %reshape.114.par_f.par_b, f32[16,1024]{1,0:T(8,128)} %reshape.114.par_f.par_b, ...), custom_call_target="tpu_custom_call" | custom-call | flops 4718592000 | bytes 56623104 | tf_op jit(solution)/shard_map/middle/pallas_call | solution.py:328
  1325.4 2.2 slice_convert_fusion
  1327.7 2.0 collective-permute-start.20
  1329.6 1.6 collective-permute-start.21
  1332.9 84.6 %collective-permute-done.19.refs_1_ = f32[512,1024]{1,0:T(8,128)} collective-permute-done((f32[512,1024]{1,0:T(8,128)S(1)}, f32[512,1024]{1,0:T(8,128)}, u32[]{:S(2)}, u32[]{:S(2)}) %collective-permute-start.19) | collective-permute-done | bytes 2097184 | tf_op jit(solution)/shard_map/ppermute | solution.py:572
  1417.5 85.8 %collective-permute-done.20.refs_2_ = f32[512,1024]{1,0:T(8,128)} collective-permute-done((f32[512,1024]{1,0:T(8,128)S(1)}, f32[512,1024]{1,0:T(8,128)}, u32[]{:S(2)}, u32[]{:S(2)}) %collective-permute-start.20) | collective-permute-done | bytes 2097184 | tf_op jit(solution)/shard_map/ppermute | solution.py:572
  1503.3 1.5 collective-permute-start.31
  1504.8 1.0 collective-permute-start.32
  1505.7 233.6 %grad_normed.3.refs_10_ = f32[3072,4096]{1,0:T(8,128)} custom-call(bf16[4096,1024]{1,0:T(8,128)(2,1)} %get-tuple-element.121.refs_0_, bf16[3072,1024]{1,0:T(8,128)(2,1)} %get-tuple-element.164.refs_1_, bf16[3072,1024]{1,0:T(8,128)(2,1)} %get-tuple-element.165.refs_2_, bf16[3072,1024]{1,0:T(8,128)(2,1)} %get-tuple-element.166.refs_3_, ...), custom_call_target="tpu_custom_call" | custom-call | flops 206158430208 | bytes 450000000 | tf_op jit(solution)/shard_map/grad_normed/pallas_call | solution.py:537
  1739.4 160.2 %outputs.2 = (bf16[4096,4096]{1,0:T(8,128)(2,1)}, bf16[4096,4096]{1,0:T(8,128)(2,1)}, f32[2,8,4096]{2,1,0:T(8,128)}) custom-call(bf16[4096,1024]{1,0:T(8,128)(2,1)} %get-tuple-element.133.refs_0_, bf16[3072,1024]{1,0:T(8,128)(2,1)} %get-tuple-element.127.refs_1_, bf16[3072,1024]{1,0:T(8,128)(2,1)} %get-tuple-element.132.refs_2_, ...), custom_call_target="tpu_custom_call" | custom-call | flops 103079215104 | bytes 251658240 | tf_op jit(solution)/shard_map/outputs/pallas_call | solution.py:506
  1899.6 3.6 psum.54
  1905.0 2.3 fusion.1
  1907.3 60.4 %outputs.3 = (bf16[4096,4096]{1,0:T(8,128)(2,1)}, bf16[4096,4096]{1,0:T(8,128)(2,1)}, f32[2,8,4096]{2,1,0:T(8,128)}) custom-call(bf16[4096,1024]{1,0:T(8,128)(2,1)} %get-tuple-element.133.refs_0_, f32[512,1024]{1,0:T(8,128)} %collective-permute-done.19.refs_1_, ...), custom_call_target="tpu_custom_call", output_to_operand_aliasing={{0}: (17, {}), {1}: (18, {})} | custom-call | flops 34359738368 | bytes 83886080 | tf_op jit(solution)/shard_map/outputs/pallas_call | solution.py:506
  1967.7 1.0 add_reduce_fusion
  1968.8 3.6 psum.55
  1973.0 13.7 copy.51
  1986.7 2.7 copy-done
  1989.4 8.5 copy.52
  1997.9 1.4 slice-done.4
  1999.3 1.2 slice-done.5
  2000.5 6.2 copy.53
  (136 shorter events, 19.6 us)
Async XLA Ops:
  7.2 1897.8 %all-reduce.4.cloned.1.call-start = ((), (), s32[]{:S(2)}) async-start(), calls=%async_computation | async-start | bytes 33554432 | tf_op jit(solution)/shard_map/psum | solution.py:644
  12.3 8.2 copy-start.10
  14.4 6.2 copy-start.1
  24.4 9.3 copy-start.11
  24.4 404.1 %collective-permute-start.10 = (f32[2,1024,1024]{2,1,0:T(8,128)}, f32[2,1024,1024]{2,1,0:T(8,128)}, u32[]{:S(2)}, u32[]{:S(2)}) collective-permute-start(f32[2,1024,1024]{2,1,0:T(8,128)} %maximum_convert_fusion.1), channel_id=1, source_target_pairs={{0,4},{2,6},{4,0},{6,2},{1,5},{3,7},{5,1},{7,3}} | collective-permute-start | bytes 25165832 | tf_op jit(solution)/shard_map/ppermute | solution.py:575
  27.7 400.8 %collective-permute-start.8 = (f32[2,1024,1024]{2,1,0:T(8,128)}, f32[2,1024,1024]{2,1,0:T(8,128)}, u32[]{:S(2)}, u32[]{:S(2)}) collective-permute-start(f32[2,1024,1024]{2,1,0:T(8,128)} %maximum_convert_fusion.1), channel_id=1, source_target_pairs={{0,2},{2,0},{4,6},{6,4},{1,3},{3,1},{5,7},{7,5}} | collective-permute-start | bytes 25165832 | tf_op jit(solution)/shard_map/ppermute | solution.py:572
  33.2 395.3 %collective-permute-start.7 = (f32[2,1024,1024]{2,1,0:T(8,128)}, f32[2,1024,1024]{2,1,0:T(8,128)}, u32[]{:S(2)}, u32[]{:S(2)}) collective-permute-start(f32[2,1024,1024]{2,1,0:T(8,128)} %maximum_convert_fusion), channel_id=1, source_target_pairs={{0,2},{2,0},{4,6},{6,4},{1,3},{3,1},{5,7},{7,5}} | collective-permute-start | bytes 25165832 | tf_op jit(solution)/shard_map/ppermute | solution.py:572
  33.7 394.8 %collective-permute-start.9 = (f32[2,1024,1024]{2,1,0:T(8,128)}, f32[2,1024,1024]{2,1,0:T(8,128)}, u32[]{:S(2)}, u32[]{:S(2)}) collective-permute-start(f32[2,1024,1024]{2,1,0:T(8,128)} %maximum_convert_fusion), channel_id=1, source_target_pairs={{0,4},{2,6},{4,0},{6,2},{1,5},{3,7},{5,1},{7,3}} | collective-permute-start | bytes 25165832 | tf_op jit(solution)/shard_map/ppermute | solution.py:575
  68.2 80.7 %copy-start.14 = (s32[32,128]{1,0:T(8,128)S(1)}, s32[32,128]{1,0:T(8,128)}, u32[]{:S(2)}) copy-start(s32[32,128]{1,0:T(8,128)} %param.19) | copy-start | bytes 49156
  341.7 44.1 %copy-start.17 = (bf16[4096,1024]{1,0:T(8,128)(2,1)S(1)}, bf16[4096,1024]{1,0:T(8,128)(2,1)}, u32[]{:S(2)}) copy-start(bf16[4096,1024]{1,0:T(8,128)(2,1)} %get-tuple-element.122.refs_1_.refs_4_) | copy-start | bytes 25165828
  385.8 43.3 %copy-start.2 = (f32[2176,128]{1,0:T(8,128)S(1)}, f32[2176,128]{1,0:T(8,128)}, u32[]{:S(2)}) copy-start(f32[2176,128]{1,0:T(8,128)} %maximum_bitcast_fusion) | copy-start | bytes 3342340
  428.5 51.6 %collective-permute-start.11 = (f32[2,1024,1024]{2,1,0:T(8,128)}, f32[2,1024,1024]{2,1,0:T(8,128)}, u32[]{:S(2)}, u32[]{:S(2)}) collective-permute-start(f32[2,1024,1024]{2,1,0:T(8,128)} %collective-permute-done.7.refs_0_.refs_4_), channel_id=1, source_target_pairs={{0,1},{1,0},{2,3},{3,2},{4,5},{5,4},{6,7},{7,6}} | collective-permute-start | bytes 25165832 | tf_op jit(solution)/shard_map/ppermute | solution.py:578
  428.5 53.0 %collective-permute-start.12 = (f32[2,1024,1024]{2,1,0:T(8,128)}, f32[2,1024,1024]{2,1,0:T(8,128)}, u32[]{:S(2)}, u32[]{:S(2)}) collective-permute-start(f32[2,1024,1024]{2,1,0:T(8,128)} %collective-permute-done.8.refs_1_.refs_5_), channel_id=1, source_target_pairs={{0,1},{1,0},{2,3},{3,2},{4,5},{5,4},{6,7},{7,6}} | collective-permute-start | bytes 25165832 | tf_op jit(solution)/shard_map/ppermute | solution.py:578
  429.0 125.3 %collective-permute-start.4 = (f32[2176,128]{1,0:T(8,128)S(1)}, f32[2176,128]{1,0:T(8,128)S(1)}, u32[]{:S(2)}, u32[]{:S(2)}) collective-permute-start(f32[2176,128]{1,0:T(8,128)S(1)} %copy-done.2), channel_id=1, source_target_pairs={{0,2},{2,0},{4,6},{6,4},{1,3},{3,1},{5,7},{7,5}} | collective-permute-start | bytes 3342344 | tf_op jit(solution)/shard_map/ppermute | solution.py:586
  431.0 44.6 %slice-start = ((s8[8388608]{0:T(1024)(128)(4,1)}), s8[4194304]{0:T(1024)(128)(4,1)S(1)}, s32[]{:S(2)}) async-start(s8[8388608]{0:T(1024)(128)(4,1)} %bitcast.76), calls=%async_computation.2 | async-start | bytes 8388608
  431.0 44.6 %slice-start.1 = ((s8[8388608]{0:T(1024)(128)(4,1)}), s8[4194304]{0:T(1024)(128)(4,1)S(1)}, s32[]{:S(2)}) async-start(s8[8388608]{0:T(1024)(128)(4,1)} %bitcast.76), calls=%async_computation.3 | async-start | bytes 8388608
  431.0 125.4 %collective-permute-start.13 = (f32[2,1024,1024]{2,1,0:T(8,128)}, f32[2,1024,1024]{2,1,0:T(8,128)}, u32[]{:S(2)}, u32[]{:S(2)}) collective-permute-start(f32[2,1024,1024]{2,1,0:T(8,128)} %collective-permute-done.9.refs_0_.refs_4_), channel_id=1, source_target_pairs={{0,1},{1,0},{2,3},{3,2},{4,5},{5,4},{6,7},{7,6}} | collective-permute-start | bytes 25165832 | tf_op jit(solution)/shard_map/ppermute | solution.py:578
  431.0 126.9 %collective-permute-start.14 = (f32[2,1024,1024]{2,1,0:T(8,128)}, f32[2,1024,1024]{2,1,0:T(8,128)}, u32[]{:S(2)}, u32[]{:S(2)}) collective-permute-start(f32[2,1024,1024]{2,1,0:T(8,128)} %collective-permute-done.10.refs_1_.refs_5_), channel_id=1, source_target_pairs={{0,1},{1,0},{2,3},{3,2},{4,5},{5,4},{6,7},{7,6}} | collective-permute-start | bytes 25165832 | tf_op jit(solution)/shard_map/ppermute | solution.py:578
  480.1 74.4 %collective-permute-start.5 = (f32[2176,128]{1,0:T(8,128)S(1)}, f32[2176,128]{1,0:T(8,128)S(1)}, u32[]{:S(2)}, u32[]{:S(2)}) collective-permute-start(f32[2176,128]{1,0:T(8,128)S(1)} %copy-done.2), channel_id=1, source_target_pairs={{0,4},{2,6},{4,0},{6,2},{1,5},{3,7},{5,1},{7,3}} | collective-permute-start | bytes 3342344 | tf_op jit(solution)/shard_map/ppermute | solution.py:586
  481.6 207.9 %collective-permute-start = (f32[1,1024,1024]{2,1,0:T(8,128)}, f32[1,1024,1024]{2,1,0:T(8,128)}, u32[]{:S(2)}, u32[]{:S(2)}) collective-permute-start(f32[1,1024,1024]{2,1,0:T(8,128)} %get-tuple-element.193), channel_id=1, source_target_pairs={{0,2},{2,0},{4,6},{6,4},{1,3},{3,1},{5,7},{7,5}} | collective-permute-start | bytes 12582920 | tf_op jit(solution)/shard_map/ppermute | solution.py:572
  554.4 209.4 %copy-start.5 = (f32[2176,128]{1,0:T(8,128)}, f32[2176,128]{1,0:T(8,128)S(1)}, u32[]{:S(2)}) copy-start(f32[2176,128]{1,0:T(8,128)S(1)} %collective-permute-done.4) | copy-start | bytes 3342340
  554.4 135.6 %collective-permute-start.2 = (f32[1,1024,1024]{2,1,0:T(8,128)}, f32[1,1024,1024]{2,1,0:T(8,128)}, u32[]{:S(2)}, u32[]{:S(2)}) collective-permute-start(f32[1,1024,1024]{2,1,0:T(8,128)} %get-tuple-element.193), channel_id=1, source_target_pairs={{0,4},{2,6},{4,0},{6,2},{1,5},{3,7},{5,1},{7,3}} | collective-permute-start | bytes 12582920 | tf_op jit(solution)/shard_map/ppermute | solution.py:575
  554.4 3.5 copy-start.6
  554.4 135.5 %collective-permute-start.1 = (f32[1,1024,1024]{2,1,0:T(8,128)}, f32[1,1024,1024]{2,1,0:T(8,128)}, u32[]{:S(2)}, u32[]{:S(2)}) collective-permute-start(f32[1,1024,1024]{2,1,0:T(8,128)} %get-tuple-element.192), channel_id=1, source_target_pairs={{0,2},{2,0},{4,6},{6,4},{1,3},{3,1},{5,7},{7,5}} | collective-permute-start | bytes 12582920 | tf_op jit(solution)/shard_map/ppermute | solution.py:572
  556.4 205.5 %collective-permute-start.3 = (f32[1,1024,1024]{2,1,0:T(8,128)}, f32[1,1024,1024]{2,1,0:T(8,128)}, u32[]{:S(2)}, u32[]{:S(2)}) collective-permute-start(f32[1,1024,1024]{2,1,0:T(8,128)} %get-tuple-element.192), channel_id=1, source_target_pairs={{0,4},{2,6},{4,0},{6,2},{1,5},{3,7},{5,1},{7,3}} | collective-permute-start | bytes 12582920 | tf_op jit(solution)/shard_map/ppermute | solution.py:575
  557.9 130.0 %collective-permute-start.6 = (f32[2176,128]{1,0:T(8,128)S(1)}, f32[2176,128]{1,0:T(8,128)S(1)}, u32[]{:S(2)}, u32[]{:S(2)}) collective-permute-start(f32[2176,128]{1,0:T(8,128)S(1)} %copy-done.2), channel_id=1, source_target_pairs={{0,6},{2,4},{4,2},{6,0},{1,7},{3,5},{5,3},{7,1}} | collective-permute-start | bytes 3342344 | tf_op jit(solution)/shard_map/ppermute | solution.py:586
  687.9 74.6 %copy-start.3 = (f32[2176,128]{1,0:T(8,128)}, f32[2176,128]{1,0:T(8,128)S(1)}, u32[]{:S(2)}) copy-start(f32[2176,128]{1,0:T(8,128)S(1)} %collective-permute-done.6) | copy-start | bytes 3342340
  687.9 385.7 %collective-permute-start.23 = (f32[2,1024,1024]{2,1,0:T(8,128)}, f32[2,1024,1024]{2,1,0:T(8,128)}, u32[]{:S(2)}, u32[]{:S(2)}) collective-permute-start(f32[2,1024,1024]{2,1,0:T(8,128)} %collective-permute-done.7.refs_0_.refs_4_), channel_id=1, source_target_pairs={{0,4},{2,6},{4,0},{6,2},{1,5},{3,7},{5,1},{7,3}} | collective-permute-start | bytes 25165832 | tf_op jit(solution)/shard_map/ppermute | solution.py:575
  689.4 384.2 %collective-permute-start.24 = (f32[2,1024,1024]{2,1,0:T(8,128)}, f32[2,1024,1024]{2,1,0:T(8,128)}, u32[]{:S(2)}, u32[]{:S(2)}) collective-permute-start(f32[2,1024,1024]{2,1,0:T(8,128)} %collective-permute-done.10.refs_1_.refs_5_), channel_id=1, source_target_pairs={{0,2},{2,0},{4,6},{6,4},{1,3},{3,1},{5,7},{7,5}} | collective-permute-start | bytes 25165832 | tf_op jit(solution)/shard_map/ppermute | solution.py:572
  761.9 7.5 collective-permute-start.15
  761.9 35.9 %collective-permute-start.16 = (f32[1,1024,1024]{2,1,0:T(8,128)}, f32[1,1024,1024]{2,1,0:T(8,128)}, u32[]{:S(2)}, u32[]{:S(2)}) collective-permute-start(f32[1,1024,1024]{2,1,0:T(8,128)} %collective-permute-done.1.refs_1_), channel_id=1, source_target_pairs={{0,1},{1,0},{2,3},{3,2},{4,5},{5,4},{6,7},{7,6}} | collective-permute-start | bytes 12582920 | tf_op jit(solution)/shard_map/ppermute | solution.py:578
  762.5 35.3 %collective-permute-start.17 = (f32[1,1024,1024]{2,1,0:T(8,128)}, f32[1,1024,1024]{2,1,0:T(8,128)}, u32[]{:S(2)}, u32[]{:S(2)}) collective-permute-start(f32[1,1024,1024]{2,1,0:T(8,128)} %collective-permute-done.2.refs_0_), channel_id=1, source_target_pairs={{0,1},{1,0},{2,3},{3,2},{4,5},{5,4},{6,7},{7,6}} | collective-permute-start | bytes 12582920 | tf_op jit(solution)/shard_map/ppermute | solution.py:578
  763.8 31.7 %slice-start.7 = ((f32[2176,128]{1,0:T(8,128)}), f32[128,128]{1,0:T(8,128)S(1)}, s32[]{:S(2)}) async-start(f32[2176,128]{1,0:T(8,128)} %copy-done.5), calls=%async_computation.9 | async-start | bytes 131072 | tf_op jit(solution)/shard_map/slice | solution.py:607
  763.8 33.3 %slice-start.8 = ((f32[2176,128]{1,0:T(8,128)}), f32[128,128]{1,0:T(8,128)S(1)}, s32[]{:S(2)}) async-start(f32[2176,128]{1,0:T(8,128)} %copy-done.6), calls=%async_computation.10 | async-start | bytes 131072 | tf_op jit(solution)/shard_map/slice | solution.py:607
  769.4 167.2 %collective-permute-start.18 = (f32[1,1024,1024]{2,1,0:T(8,128)}, f32[1,1024,1024]{2,1,0:T(8,128)}, u32[]{:S(2)}, u32[]{:S(2)}) collective-permute-start(f32[1,1024,1024]{2,1,0:T(8,128)} %collective-permute-done.3.refs_1_), channel_id=1, source_target_pairs={{0,1},{1,0},{2,3},{3,2},{4,5},{5,4},{6,7},{7,6}} | collective-permute-start | bytes 12582920 | tf_op jit(solution)/shard_map/ppermute | solution.py:578
  797.8 275.8 %collective-permute-start.25 = (f32[1,1024,1024]{2,1,0:T(8,128)}, f32[1,1024,1024]{2,1,0:T(8,128)}, u32[]{:S(2)}, u32[]{:S(2)}) collective-permute-start(f32[1,1024,1024]{2,1,0:T(8,128)} %collective-permute-done.refs_0_), channel_id=1, source_target_pairs={{0,4},{2,6},{4,0},{6,2},{1,5},{3,7},{5,1},{7,3}} | collective-permute-start | bytes 12582920 | tf_op jit(solution)/shard_map/ppermute | solution.py:575
  797.8 275.8 %collective-permute-start.26 = (f32[1,1024,1024]{2,1,0:T(8,128)}, f32[1,1024,1024]{2,1,0:T(8,128)}, u32[]{:S(2)}, u32[]{:S(2)}) collective-permute-start(f32[1,1024,1024]{2,1,0:T(8,128)} %collective-permute-done.3.refs_1_), channel_id=1, source_target_pairs={{0,2},{2,0},{4,6},{6,4},{1,3},{3,1},{5,7},{7,5}} | collective-permute-start | bytes 12582920 | tf_op jit(solution)/shard_map/ppermute | solution.py:572
  1073.7 13.5 collective-permute-start.27
  1073.7 25.5 %collective-permute-start.28 = (f32[2,1024,1024]{2,1,0:T(8,128)}, f32[2,1024,1024]{2,1,0:T(8,128)}, u32[]{:S(2)}, u32[]{:S(2)}) collective-permute-start(f32[2,1024,1024]{2,1,0:T(8,128)} %collective-permute-done.24.refs_1_.refs_5_), channel_id=1, source_target_pairs={{0,1},{1,0},{2,3},{3,2},{4,5},{5,4},{6,7},{7,6}} | collective-permute-start | bytes 25165832 | tf_op jit(solution)/shard_map/ppermute | solution.py:578
  1171.8 1.0 copy-start.7
  1171.8 1.1 copy-start.13
  1171.8 2.3 copy-start.4
  1171.8 3.3 slice-start.6
  1171.9 733.1 %all-reduce.6.cloned.1.call-start = ((), (), s32[]{:S(2)}) async-start(), calls=%async_computation.1 | async-start | bytes 102760448 | tf_op jit(solution)/shard_map/psum | solution.py:652
  1173.6 7.5 collective-permute-start.29
  1173.7 13.4 collective-permute-start.30
  1325.3 6.4 copy-start.16
  1325.3 7.0 copy-start.12
  1327.6 89.9 %collective-permute-start.19 = (f32[512,1024]{1,0:T(8,128)S(1)}, f32[512,1024]{1,0:T(8,128)}, u32[]{:S(2)}, u32[]{:S(2)}) collective-permute-start(f32[512,1024]{1,0:T(8,128)S(1)} %get-tuple-element.187), channel_id=1, source_target_pairs={{0,2},{2,0},{4,6},{6,4},{1,3},{3,1},{5,7},{7,5}} | collective-permute-start | bytes 6291464 | tf_op jit(solution)/shard_map/ppermute | solution.py:572
  1327.7 175.6 %collective-permute-start.20 = (f32[512,1024]{1,0:T(8,128)S(1)}, f32[512,1024]{1,0:T(8,128)}, u32[]{:S(2)}, u32[]{:S(2)}) collective-permute-start(f32[512,1024]{1,0:T(8,128)S(1)} %get-tuple-element.186), channel_id=1, source_target_pairs={{0,2},{2,0},{4,6},{6,4},{1,3},{3,1},{5,7},{7,5}} | collective-permute-start | bytes 6291464 | tf_op jit(solution)/shard_map/ppermute | solution.py:572
  1329.6 173.6 %collective-permute-start.21 = (f32[512,1024]{1,0:T(8,128)S(1)}, f32[512,1024]{1,0:T(8,128)}, u32[]{:S(2)}, u32[]{:S(2)}) collective-permute-start(f32[512,1024]{1,0:T(8,128)S(1)} %get-tuple-element.187), channel_id=1, source_target_pairs={{0,4},{2,6},{4,0},{6,2},{1,5},{3,7},{5,1},{7,3}} | collective-permute-start | bytes 6291464 | tf_op jit(solution)/shard_map/ppermute | solution.py:575
  1331.2 172.0 %collective-permute-start.22 = (f32[512,1024]{1,0:T(8,128)S(1)}, f32[512,1024]{1,0:T(8,128)}, u32[]{:S(2)}, u32[]{:S(2)}) collective-permute-start(f32[512,1024]{1,0:T(8,128)S(1)} %get-tuple-element.186), channel_id=1, source_target_pairs={{0,4},{2,6},{4,0},{6,2},{1,5},{3,7},{5,1},{7,3}} | collective-permute-start | bytes 6291464 | tf_op jit(solution)/shard_map/ppermute | solution.py:575
  1503.3 404.0 %collective-permute-start.31 = (f32[512,1024]{1,0:T(8,128)}, f32[512,1024]{1,0:T(8,128)}, u32[]{:S(2)}, u32[]{:S(2)}) collective-permute-start(f32[512,1024]{1,0:T(8,128)} %collective-permute-done.19.refs_1_), channel_id=1, source_target_pairs={{0,4},{2,6},{4,0},{6,2},{1,5},{3,7},{5,1},{7,3}} | collective-permute-start | bytes 6291464 | tf_op jit(solution)/shard_map/ppermute | solution.py:575
  1504.8 402.5 %collective-permute-start.32 = (f32[512,1024]{1,0:T(8,128)}, f32[512,1024]{1,0:T(8,128)}, u32[]{:S(2)}, u32[]{:S(2)}) collective-permute-start(f32[512,1024]{1,0:T(8,128)} %collective-permute-done.22.refs_4_), channel_id=1, source_target_pairs={{0,2},{2,0},{4,6},{6,4},{1,3},{3,1},{5,7},{7,5}} | collective-permute-start | bytes 6291464 | tf_op jit(solution)/shard_map/ppermute | solution.py:572
  1739.4 160.2 %copy-start.9 = (f32[10,1024]{1,0:T(8,128)S(1)}, f32[10,1024]{1,0:T(8,128)}, u32[]{:S(2)}) copy-start(f32[10,1024]{1,0:T(8,128)} %pad_maximum_fusion) | copy-start | bytes 122884
  1739.4 165.0 %copy-start.15 = (f32[1024]{0:T(1024)S(1)}, f32[1024]{0:T(1024)}, u32[]{:S(2)}) copy-start(f32[1024]{0:T(1024)} %param.31) | copy-start | bytes 12292
  1907.3 60.4 %copy-start.8 = (f32[2,8,4096]{2,1,0:T(8,128)S(1)}, f32[2,8,4096]{2,1,0:T(8,128)}, u32[]{:S(2)}) copy-start(f32[2,8,4096]{2,1,0:T(8,128)} %get-tuple-element.180) | copy-start | bytes 786436
  1973.0 16.4 copy-start
  1973.0 24.9 %slice-start.2 = ((s8[16777216]{0:T(1024)(128)(4,1)}), s8[4194304]{0:T(1024)(128)(4,1)S(1)}, s32[]{:S(2)}) async-start(s8[16777216]{0:T(1024)(128)(4,1)} %bitcast.78), calls=%async_computation.4 | async-start | bytes 8388608
  1973.0 24.9 %slice-start.3 = ((s8[16777216]{0:T(1024)(128)(4,1)}), s8[4194304]{0:T(1024)(128)(4,1)S(1)}, s32[]{:S(2)}) async-start(s8[16777216]{0:T(1024)(128)(4,1)} %bitcast.78), calls=%async_computation.5 | async-start | bytes 8388608
  1989.4 9.9 slice-start.4
  1989.4 11.1 slice-start.5
Sparse Core Ops, SparseCore 0:
  1172.0 423.9 all-reduce.3
  1599.3 149.4 all-reduce.5

commit v3 on v2

--- a/solution.py
+++ b/solution.py
@@ -20,6 +20,7 @@
 GELU_K0 = 0.7978845608028654
 GELU_K1 = 0.7978845608028654 * 0.044715
 N_SUMS = 9
+SPAN = 32
 N_PAR = 10
 BORROW = TAPS - 1
 
@@ -28,7 +29,7 @@
     return [jnp.broadcast_to(ref[pl.ds(k, 1), :], (SUB, LANES)) for k in range(N_PAR)]
 
 
-def middle_kernel(n_steps, n_tiles, n_tok, grads, pos_f, pos_b, par_f, par_b, wg_f, wg_b, px, py, dm, *rest):
+def middle_kernel(n_steps, n_tiles, n_tok, grads, pos_w, par_w, wg_w, px, py, dm, *rest):
     if grads:
         mix_o, dpy_o, dbr_o, gw_o, sy_o, sb_o = rest[:6]
         rest = rest[6:]
@@ -47,7 +48,11 @@
     b_slot = lax.rem(b_step + SLOTS, SLOTS)
     f_msg = lax.rem(f_step + MSG_SLOTS, MSG_SLOTS)
     b_msg = lax.rem(b_step + MSG_SLOTS, MSG_SLOTS)
-    n_groups = n_tok // SUB
+    n_groups = n_tok // SPAN
+    f_at, b_at = [jnp.clip(v, 0, n_steps - 1) for v in (f_step, b_step)]
+    pos_f, pos_b = [pos_w.at[lax.rem(v, n_tiles)] for v in (f_at, b_at)]
+    par_f, par_b = [par_w.at[:, pl.ds(pl.multiple_of(v // n_tiles * LANES, LANES), LANES)] for v in (f_at, b_at)]
+    wg_f, wg_b = [wg_w.at[v // n_tiles] for v in (f_at, b_at)]
 
     def message(slot):
         return pltpu.make_async_remote_copy(src_ref=send.at[slot], dst_ref=recv.at[slot], send_sem=send_sem.at[slot], recv_sem=recv_sem.at[slot], device_id={"cp": 1 - me}, device_id_type=pl.DeviceIdType.MESH)
@@ -88,8 +93,8 @@
         def conv_body(grp, past):
             past = list(past)
             pend = None
-            for j in range(SUB):
-                t = grp * SUB + j
+            for j in range(SPAN):
+                t = grp * SPAN + j
                 now = (in_x[strided(t), :] + b_x).astype(BF16).astype(F32)
                 pos = pos_f[row8(t * SUB), :]
                 acc = c_b + now * taps[0]
@@ -116,8 +121,8 @@
 
         def gate_body(grp, carry):
             h, sum_y = carry
-            for j in range(SUB):
-                t = grp * SUB + j
+            for j in range(SPAN):
+                t = grp * SPAN + j
                 rows = row8(t * SUB)
                 if j % 2:
                     c = both[SUB:]
@@ -205,8 +210,8 @@
             grp = n_groups - 1 - back
             adh, sum_a, sum_i, sum_p = carry
             pend = None
-            for j in reversed(range(SUB)):
-                t = grp * SUB + j
+            for j in reversed(range(SPAN)):
+                t = grp * SPAN + j
                 rows = row8(t * SUB)
                 dh = g_r[rows, :] + adh
                 adh = a_r[rows, :] * dh
@@ -231,8 +236,8 @@
 
         def conv_body(grp, carry):
             ahead, sums = list(carry[:BORROW]), list(carry[BORROW:])
-            for j in range(SUB):
-                s = grp * SUB + j
+            for j in range(SPAN):
+                s = grp * SPAN + j
                 rows = row8(s * SUB)
                 pos = pos_b[rows, :]
                 dc = d_c[rows, :] + d_gate[rows, :]
@@ -304,11 +309,8 @@
         return pl.BlockSpec(shape, index_map)
 
     big = lambda of: spec((tile, LANES), of, lambda c, t: (t, c))
-    both = (f_of, b_of)
     per_chunk = lambda of, *shape: spec((1,) + shape, of, lambda c, t: (c, 0, 0))
-    in_specs = [spec((None, tile, LANES), of, lambda c, t: (t, 0, 0)) for of in both]
-    in_specs += [spec((par.shape[0], LANES), of, lambda c, t: (0, c)) for of in both]
-    in_specs += [spec((None,) + w_gate.shape[1:], of, lambda c, t: (c, 0, 0)) for of in both]
+    in_specs = [pl.BlockSpec((n_tiles,) + pos_rep.shape[1:], lambda s: (0, 0, 0)), pl.BlockSpec(par.shape, lambda s: (0, 0)), pl.BlockSpec(w_gate.shape, lambda s: (0, 0, 0))]
     in_specs += [big(f_of)] * 3
     out_specs = [big(f_of), big(f_of), big(b_of)]
     out_shape = [jax.ShapeDtypeStruct((n_rows, width), BF16)] * 3
@@ -331,7 +333,7 @@
         name="middle",
         cost_estimate=pl.CostEstimate(flops=n_rows * width * 1500, bytes_accessed=n_rows * width * 18, transcendentals=n_rows * width * 8),
         compiler_params=pltpu.CompilerParams(collective_id=collective_id, has_side_effects=True, vmem_limit_bytes=VMEM_LIMIT, dimension_semantics=("arbitrary",)),
-    )(pos_rep, pos_rep, par, par, w_gate, w_gate, px, py, dm)
+    )(pos_rep, par, w_gate, px, py, dm)
 
 
 NORM_EPS = 1e-6
@@ -458,14 +460,14 @@
             sum_ref[which, :, cols] += sum(val[SUB * r:SUB * (r + 1)] for r in range(rows // SUB))
 
 
-def z_kernel(n_own, n_far, n_cols, *refs):
+def z_kernel(n_own, n_far, n_into, n_moved, *refs):
     own, far, right = refs[:n_own], refs[n_own:n_own + 2 * n_far], refs[n_own + 2 * n_far:2 * n_own + 3 * n_far]
     x_ref, bias_ref, dn_ref, x_rows, gz_rows, scale_ref = refs[2 * n_own + 3 * n_far:][:6]
-    out_ref, grad_ref, sum_ref = refs[-4:-1]
-    far_16 = refs[-1]
+    rest = refs[2 * n_own + 3 * n_far + 6 + n_into:]
+    moved, (out_ref, grad_ref, sum_ref), placed, far_16 = rest[:n_moved], rest[n_moved:n_moved + 3], rest[n_moved + 3:-1], rest[-1]
+    for src, dst in zip(moved, placed):
+        dst[...] = src[...]
     unit = 4 * SUB
-    turns = out_ref.shape[1] // n_cols
-    units = dn_ref.shape[0] // unit // turns
 
     @pl.when(jnp.logical_and(pl.program_id(0) == 0, pl.program_id(1) == 0))
     def _():
@@ -474,20 +476,15 @@
             half = ref.shape[0]
             far_16[k // 2, pl.ds(k % 2 * half, half), :] = ref[...].astype(BF16)
 
-    def column(c, _):
-        cols = pl.ds(pl.multiple_of(c * n_cols, n_cols), n_cols)
-        acc = x_ref[:, cols].astype(F32) + bias_ref[:, cols]
-        for lhs, rhs in zip(list(own) + [far_16.at[k] for k in range(n_far)], right):
-            acc = acc + jnp.dot(lhs[...], rhs[:, cols], preferred_element_type=F32)
-        out_ref[:, cols] = acc.astype(BF16)
-        for u in range(units):
-            finish_rows(unit, (c * units + u) * unit, dn_ref, x_rows, gz_rows, scale_ref, grad_ref, sum_ref)
-        return 0
-
-    lax.fori_loop(0, turns, column, 0)
-
-
-def outputs(own, far, rights, x, bias, dn, gz, scale, first_row, into):
+    acc = x_ref[...].astype(F32) + bias_ref[...]
+    for lhs, rhs in zip(list(own) + [far_16.at[k] for k in range(n_far)], right):
+        acc = acc + jnp.dot(lhs[...], rhs[...], preferred_element_type=F32)
+    out_ref[...] = acc.astype(BF16)
+    for first in range(0, dn_ref.shape[0], unit):
+        finish_rows(unit, first, dn_ref, x_rows, gz_rows, scale_ref, grad_ref, sum_ref)
+
+
+def outputs(own, far, rights, x, bias, dn, gz, scale, first_row, into, moved):
     rows, width = dn.shape
     depth = own[0].shape[1]
     bm, bn = 1024, 512
@@ -497,18 +494,20 @@
     tile = pl.BlockSpec((bm, bn), lambda i, j: (i + skip, j))
     part = pl.BlockSpec((share, width), lambda i, j: (i * n_col + j, 0))
     line = pl.BlockSpec((share, width), lambda i, j: (i * n_col + j + skip_share, 0))
-    args = list(own) + [v for pair in far for v in pair] + list(rights) + [x, bias, dn, x, gz, scale] + list(into)
+    args = list(own) + [v for pair in far for v in pair] + list(rights) + [x, bias, dn, x, gz, scale] + list(into) + list(moved)
     in_specs = [pl.BlockSpec((bm, depth), lambda i, j: (i + skip, 0))] * len(own)
     in_specs += [pl.BlockSpec((bm // 2, depth), lambda i, j: (0, 0))] * (2 * len(far))
     in_specs += [pl.BlockSpec((depth, bn), lambda i, j: (0, j))] * len(rights)
     in_specs += [tile, pl.BlockSpec((1, bn), lambda i, j: (0, j)), part, line, line, pl.BlockSpec((1, width), lambda i, j: (0, 0))]
     in_specs += [pl.BlockSpec(memory_space=pl.ANY)] * len(into)
+    n_move = 16
+    passing = [pl.BlockSpec((v.shape[0] // n_move, v.shape[1]), lambda i, j: (jnp.minimum(i * n_col + j, n_move - 1), 0)) for v in moved]
     return pl.pallas_call(
-        functools.partial(z_kernel, len(own), len(far), 256), grid=(n_row, n_col), name="outputs",
-        in_specs=in_specs, out_specs=[tile, line, pl.BlockSpec((2, SUB, width), lambda i, j: (0, 0, 0))],
-        out_shape=[jax.ShapeDtypeStruct(x.shape, BF16), jax.ShapeDtypeStruct(x.shape, BF16), jax.ShapeDtypeStruct((2, SUB, width), F32)],
+        functools.partial(z_kernel, len(own), len(far), len(into), len(moved)), grid=(n_row, n_col), name="outputs",
+        in_specs=in_specs + passing, out_specs=[tile, line, pl.BlockSpec((2, SUB, width), lambda i, j: (0, 0, 0))] + passing,
+        out_shape=[jax.ShapeDtypeStruct(x.shape, BF16), jax.ShapeDtypeStruct(x.shape, BF16), jax.ShapeDtypeStruct((2, SUB, width), F32)] + [jax.ShapeDtypeStruct(v.shape, v.dtype) for v in moved],
         scratch_shapes=[pltpu.VMEM((max(len(far), 1), bm if far else 2 * SUB, depth), BF16)],
-        input_output_aliases={len(args) - len(into) + k: k for k in range(len(into))},
+        input_output_aliases={len(args) - len(moved) - len(into) + k: k for k in range(len(into))},
         cost_estimate=pl.CostEstimate(flops=2 * len(rights) * rows * width * depth, bytes_accessed=rows * width * 20, transcendentals=rows),
         compiler_params=params_of("arbitrary", "arbitrary"),
     )(*args)
@@ -625,6 +624,10 @@
     side_x, side_y = [cores(values) for values in group_a]
     g_w_x = token_product(normed, after(dbr, g_w_y))
     diag_a = onward(after(group_a, g_w_x))
+
+    s_y = jnp.sum(s_y, axis=1).reshape(1, width)
+    s_b = jnp.swapaxes(jnp.sum(s_b.reshape(s_b.shape[0], N_SUMS, SUB, LANES), axis=2), 0, 1).reshape(N_SUMS, width)
+    own_grads = lax.psum((g_w_x, g_w_y, g_w_out, g_gate), "cp")
 
     px_x, py_x, wx_x, wy_x = up(after(normed, g_w_x), quarters(side_x, 2), False, shared)
     px_y, py_y, wx_y, wy_y = up(after(normed, px_x), quarters(side_y, 2), False, shared)
@@ -647,15 +650,14 @@
 
     far_x, far_y = after((tail_x, tail_y), mixed_d)
     far_d = [swap_y(far_x[0]), swap_x(far_y[1])]
-    s_y = jnp.sum(s_y, axis=1).reshape(1, width)
-    s_b = jnp.swapaxes(jnp.sum(s_b.reshape(s_b.shape[0], N_SUMS, SUB, LANES), axis=2), 0, 1).reshape(N_SUMS, width)
-    own_grads = lax.psum(after((g_w_x, g_w_y, g_w_out, g_gate, jnp.concatenate([s_y, s_b])), mixed_d), "cp")
-    g_w_x, g_w_y, g_w_out, g_gate, lines = own_grads
     wx_all, wy_all, wo_all = [w_x, wx_x, wx_y, wx_d], [w_y, wy_x, wy_y, wy_d], [w_out, wo_x, wo_y, wo_d]
     dn = grad_normed([dbr, dbr_x, dbr_y, dbr_d, dpy, dpy_x, dpy_y, dpy_d], wx_all + wy_all, 0, shared)
     bias = b_out.astype(F32).reshape(1, d_model)
-    z_out, grad_x, sums_x = outputs([mixed, mixed_x, mixed_y, mixed_d], [], wo_all, x, bias, dn, gz, 1.0 + scale, 0, ())
-    z_out, grad_x, sums_t = outputs([mixed], [far_x, far_y, far_d], wo_all, x, bias, after(dn_tail, *own_grads), gz, 1.0 + scale, shared, (z_out, grad_x))
+    *tall, g_gate = own_grads
+    lines = lax.psum(after(jnp.concatenate([s_y, s_b]), mixed_d), "cp")
+    z_out, grad_x, sums_x, *tall = outputs([mixed, mixed_x, mixed_y, mixed_d], [], wo_all, x, bias, after(dn, lines), gz, 1.0 + scale, 0, (), tall)
+    g_w_x, g_w_y, g_w_out = tall
+    z_out, grad_x, sums_t = outputs([mixed], [far_x, far_y, far_d], wo_all, x, bias, dn_tail, gz, 1.0 + scale, shared, (z_out, grad_x), ())
     z_out = z_out.reshape(x_in.shape)
     sums_x = jnp.sum(sums_x + sums_t, axis=1)
 

time: 2020 us -> 1740 us (0.86)
  waiting for transfers between devices: 341 us -> 144 us
  Pallas kernels: 1410 us -> 1360 us
  local copies, waits for them, and re-layouts: 54 us -> 20.3 us
    ppermute x9, waiting for transfers between devices: 170 us -> 0.02 us  [swap_x(): return lax.ppermute(v, 'tp', [(j, j ^ 1) for j in range(4)])]
    pallas_call x4, Pallas kernels: 437 us -> 377 us  [middle(): pl.pallas_call(functools.partial(middle_kernel, n_steps, n_tiles, n_tok,...]
    unnamed x56 -> x43, local copies, waits for them, and re-layouts: 36.2 us -> 3.62 us
  transfers between devices with their start and end apart: 35 -> 35, of which waited for: 9 -> 5; matrix products, arithmetic and copies ran while one was open for 8% -> 9% of each run, Pallas kernels for 64% -> 75%
where the time goes in v3:
time: 1740 us; the launch traced here: 1730 us
  Pallas kernels  1360 us (78%)
  waiting for transfers between devices  144 us (8%)
  matrix products  129 us (7%)
  other arithmetic  31.3 us (2%)
  starting transfers between devices  25.3 us (1%)
  local copies, waits for them, and re-layouts  20.3 us (1%)
    pallas_call x4, Pallas kernels, middle(): pl.pallas_call(functools.partial(middle_kernel, n_steps, n_tiles, n_tok,...  377 us
    pallas_call x6, Pallas kernels, up(): pl.pallas_call(functools.partial(up_kernel, n, n_parts, flip), grid=(n_ro...  353 us
    pallas_call x2, Pallas kernels, grad_normed(): pl.pallas_call(functools.partial(dn_kernel, n), grid=(rows // bm, width /...  255 us
    pallas_call x2, Pallas kernels, outputs(): pl.pallas_call(functools.partial(z_kernel, len(own), len(far), len(into),...  219 us
    dot_general x3, matrix products, token_product(): return lax.dot_general(lhs, rhs, TOK, preferred_element_type=F32)  129 us
    pallas_call x2, Pallas kernels, plain_up(): pl.pallas_call(functools.partial(plain_up_kernel, n, flip), grid=(width /...  124 us
    ppermute x9, waiting for transfers between devices, swap_y(): return lax.ppermute(v, 'tp', [(j, j ^ 2) for j in range(4)])  65 us
    ppermute x3, waiting for transfers between devices, block_body(): lax.ppermute(small, 'tp', [(j, j ^ far) for j in range(4)])  57 us
  transfers between devices with their start and end apart: 35, of which 5 were waited for; matrix products, arithmetic and copies ran while one was open for 9% of the time, Pallas kernels for 75%

profile of v3, /device:TPU:0, one launch (start us, length us, event | category | flops | bytes accessed | tf_op | source)
XLA Modules:
  0.0 1734.5 jit_solution(14293827718667828210)
XLA Ops:
  7.2 0.9 slice_convert_fusion.2
  8.1 0.7 stack.100
  8.8 0.7 stack.101
  9.5 0.7 stack.102
  10.1 0.7 stack.103
  10.8 0.7 stack.104
  11.5 0.7 fusion
  12.3 1.0 constant_dynamic-update-slice_fusion.1
  13.4 1.0 constant_dynamic-update-slice_fusion.wg_w
  15.0 1.1 maximum_bitcast_fusion
  16.1 4.4 dynamic-slice_bitcast_fusion
  20.6 3.8 maximum_convert_fusion.1
  24.4 3.3 collective-permute-start.10
  27.7 1.5 collective-permute-start.8
  29.2 3.9 maximum_convert_fusion
  34.3 33.9 %normalize.1.lhs = bf16[4096,4096]{1,0:T(8,128)(2,1)} custom-call(bf16[4096,4096]{1,0:T(8,128)(2,1)} %bitcast.62, f32[1,4096]{1,0:T(1,128)} %bitcast.88), custom_call_target="tpu_custom_call" | custom-call | flops 10066329600 | bytes 67108864 | tf_op jit(solution)/shard_map/normalize/pallas_call | solution.py:357
  68.2 80.7 %plain_up.2 = (f32[4096,1024]{1,0:T(8,128)}, f32[4096,1024]{1,0:T(8,128)}) custom-call(bf16[4096,4096]{1,0:T(8,128)(2,1)} %normalize.1.lhs, bf16[4096,1024]{1,0:T(8,128)(2,1)} %refs_8_.1, bf16[4096,1024]{1,0:T(8,128)(2,1)} %refs_12_.1), custom_call_target="tpu_custom_call" | custom-call | flops 68719476736 | bytes 67108864 | tf_op jit(solution)/shard_map/plain_up/pallas_call | solution.py:377
  149.2 43.0 %plain_up.3.dm = f32[4096,1024]{1,0:T(8,128)} custom-call(bf16[4096,4096]{1,0:T(8,128)(2,1)} %bitcast.67, bf16[1024,4096]{1,0:T(8,128)(2,1)} %refs_7_.1), custom_call_target="tpu_custom_call" | custom-call | flops 34359738368 | bytes 67108864 | tf_op jit(solution)/shard_map/plain_up/pallas_call | solution.py:377
  192.2 2.2 broadcast_in_dim.11.pos_w
  194.4 130.6 %middle.4 = (bf16[4096,1024]{1,0:T(8,128)(2,1)}, bf16[4096,1024]{1,0:T(8,128)(2,1)}, bf16[4096,1024]{1,0:T(8,128)(2,1)}, f32[8,128,256]{2,1,0:T(8,128)}, f32[8,8,128]{2,1,0:T(8,128)}, /*index=5*/f32[8,72,128]{2,1,0:T(8,128)}) custom-call(s32[4,1024,128]{2,1,0:T(8,128)} %broadcast_in_dim.11.pos_w, f32[16,1024]{1,0:T(8,128)} %copy-done.10, ...), custom_call_target="tpu_custom_call" | custom-call | flops 6291456000 | bytes 75497472 | tf_op jit(solution)/shard_map/middle/pallas_call | solution.py:330
  325.0 44.3 %fusion.3 = f32[4096,1024]{1,0:T(8,128)} fusion(bf16[4096,4096]{1,0:T(8,128)(2,1)} %normalize.1.lhs, bf16[4096,1024]{1,0:T(8,128)(2,1)} %get-tuple-element.121.refs_1_.refs_4_), kind=kOutput, calls=%fused_computation.30 | convolution fusion | flops 34359738368 | bytes 58720256 | tf_op jit(solution)/shard_map/dot_general | solution.py:546
  369.4 42.7 %fusion.5 = f32[1024,4096]{1,0:T(8,128)} fusion(bf16[4096,1024]{1,0:T(8,128)(2,1)S(1)} %copy-done, bf16[4096,4096]{1,0:T(8,128)(2,1)} %bitcast.68), kind=kOutput, calls=%fused_computation.32 | convolution fusion | flops 34359738368 | bytes 58720256 | tf_op jit(solution)/shard_map/dot_general | solution.py:546
  412.6 42.3 %fusion.4 = f32[4096,1024]{1,0:T(8,128)} fusion(bf16[4096,4096]{1,0:T(8,128)(2,1)} %normalize.1.lhs, bf16[4096,1024]{1,0:T(8,128)(2,1)S(1)} %bitcast.106), kind=kOutput, calls=%fused_computation.31 | convolution fusion | flops 34359738368 | bytes 58720256 | tf_op jit(solution)/shard_map/dot_general | solution.py:546
  456.2 2.0 collective-permute-start.4
  458.2 8.6 bitcast_convert_fusion
  466.7 0.7 collective-permute-start.5
  467.4 79.9 %up.6 = (f32[3072,1024]{1,0:T(8,128)}, f32[3072,1024]{1,0:T(8,128)}, bf16[4096,1024]{1,0:T(8,128)(2,1)}, bf16[4096,1024]{1,0:T(8,128)(2,1)}) custom-call(bf16[4096,4096]{1,0:T(8,128)(2,1)} %normalize.1.lhs, f32[2,1024,1024]{2,1,0:T(8,128)} %collective-permute-done.7.refs_0_.refs_4_, f32[2,1024,1024]{2,1,0:T(8,128)} %collective-permute-done.8.refs_1_.refs_5_, ...), custom_call_target="tpu_custom_call" | custom-call | flops 51539607552 | bytes 50331648 | tf_op jit(solution)/shard_map/up/pallas_call | solution.py:432
  547.4 1.2 collective-permute-start.2
  548.5 2.2 collective-permute-start.1
  551.1 1.1 collective-permute-start.6
  552.2 78.6 %up.7 = (f32[3072,1024]{1,0:T(8,128)}, f32[3072,1024]{1,0:T(8,128)}, bf16[4096,1024]{1,0:T(8,128)(2,1)}, bf16[4096,1024]{1,0:T(8,128)(2,1)}) custom-call(bf16[4096,4096]{1,0:T(8,128)(2,1)} %normalize.1.lhs, f32[2,1024,1024]{2,1,0:T(8,128)} %collective-permute-done.9.refs_0_.refs_4_, f32[2,1024,1024]{2,1,0:T(8,128)} %collective-permute-done.10.refs_1_.refs_5_, ...), custom_call_target="tpu_custom_call" | custom-call | flops 51539607552 | bytes 50331648 | tf_op jit(solution)/shard_map/up/pallas_call | solution.py:432
  630.8 57.0 %collective-permute-done.6 = f32[2176,128]{1,0:T(8,128)S(1)} collective-permute-done((f32[2176,128]{1,0:T(8,128)S(1)}, f32[2176,128]{1,0:T(8,128)S(1)}, u32[]{:S(2)}, u32[]{:S(2)}) %collective-permute-start.6) | collective-permute-done | bytes 1114144 | tf_op jit(solution)/shard_map/ppermute | solution.py:585
  688.1 1.7 collective-permute-start.24
  689.9 65.0 %collective-permute-done.3.refs_1_ = f32[1,1024,1024]{2,1,0:T(8,128)} collective-permute-done((f32[1,1024,1024]{2,1,0:T(8,128)}, f32[1,1024,1024]{2,1,0:T(8,128)}, u32[]{:S(2)}, u32[]{:S(2)}) %collective-permute-start.3) | collective-permute-done | bytes 4194336 | tf_op jit(solution)/shard_map/ppermute | solution.py:574
  755.5 1.3 slice_bitcast_fusion.2
  756.8 5.6 collective-permute-done.15.refs_2_
  762.6 25.0 %grad_normed.2 = f32[1024,4096]{1,0:T(8,128)} custom-call(bf16[4096,1024]{1,0:T(8,128)(2,1)} %get-tuple-element.120.refs_0_, bf16[4096,1024]{1,0:T(8,128)(2,1)} %get-tuple-element.121.refs_1_.refs_4_, bf16[4096,1024]{1,0:T(8,128)(2,1)} %refs_8_.1, bf16[4096,1024]{1,0:T(8,128)(2,1)} %refs_12_.1), custom_call_target="tpu_custom_call" | custom-call | flops 17179869184 | bytes 450000000 | tf_op jit(solution)/shard_map/grad_normed/pallas_call | solution.py:536
  787.6 1.0 convert_element_type.69.wg_w
  789.2 1.0 convert_element_type.67.wg_w
  790.8 1.1 collective-permute-start.25
  791.9 2.2 collective-permute-start.26
  794.1 40.4 %up.8 = (f32[3072,1024]{1,0:T(8,128)}, bf16[1024,4096]{1,0:T(8,128)(2,1)}) custom-call(bf16[4096,4096]{1,0:T(8,128)(2,1)} %bitcast.69, f32[1,1024,1024]{2,1,0:T(8,128)} %collective-permute-done.refs_0_, f32[1,1024,1024]{2,1,0:T(8,128)} %collective-permute-done.1.refs_1_, f32[1,1024,1024]{2,1,0:T(8,128)} %collective-permute-done.15.refs_2_, ...), custom_call_target="tpu_custom_call" | custom-call | flops 25769803776 | bytes 50331648 | tf_op jit(solution)/shard_map/up/pallas_call | solution.py:432
  834.5 82.1 %middle.5 = (bf16[3072,1024]{1,0:T(8,128)(2,1)}, bf16[3072,1024]{1,0:T(8,128)(2,1)}, bf16[3072,1024]{1,0:T(8,128)(2,1)}) custom-call(s32[4,1024,128]{2,1,0:T(8,128)} %broadcast_in_dim.11.pos_w, f32[16,1024]{1,0:T(8,128)} %reshape.113.par_w, bf16[8,128,256]{2,1,0:T(8,128)(2,1)} %convert_element_type.69.wg_w, f32[3072,1024]{1,0:T(8,128)} %get-tuple-element.111.px, ...), custom_call_target="tpu_custom_call" | custom-call | flops 4718592000 | bytes 56623104 | tf_op jit(solution)/shard_map/middle/pallas_call | solution.py:330
  916.6 40.6 %up.9 = (f32[3072,1024]{1,0:T(8,128)}, bf16[1024,4096]{1,0:T(8,128)(2,1)}) custom-call(bf16[4096,4096]{1,0:T(8,128)(2,1)} %bitcast.70, f32[1,1024,1024]{2,1,0:T(8,128)} %collective-permute-done.2.refs_0_, f32[1,1024,1024]{2,1,0:T(8,128)} %collective-permute-done.3.refs_1_, f32[1,1024,1024]{2,1,0:T(8,128)} %collective-permute-done.17.refs_2_, ...), custom_call_target="tpu_custom_call" | custom-call | flops 25769803776 | bytes 50331648 | tf_op jit(solution)/shard_map/up/pallas_call | solution.py:432
  957.2 82.1 %middle.6 = (bf16[3072,1024]{1,0:T(8,128)(2,1)}, bf16[3072,1024]{1,0:T(8,128)(2,1)}, bf16[3072,1024]{1,0:T(8,128)(2,1)}) custom-call(s32[4,1024,128]{2,1,0:T(8,128)} %broadcast_in_dim.11.pos_w, f32[16,1024]{1,0:T(8,128)} %reshape.112.par_w, bf16[8,128,256]{2,1,0:T(8,128)(2,1)} %convert_element_type.67.wg_w, f32[3072,1024]{1,0:T(8,128)} %get-tuple-element.115.px, ...), custom_call_target="tpu_custom_call" | custom-call | flops 4718592000 | bytes 56623104 | tf_op jit(solution)/shard_map/middle/pallas_call | solution.py:330
  1042.0 1.0 convert_element_type.73.wg_w
  1043.6 4.1 slice_convert_fusion
  1047.8 0.7 collective-permute-start.21
  1048.5 4.5 collective-permute-done.27.refs_2_.refs_6_
  1053.1 11.9 collective-permute-done.28.refs_3_.refs_7_
  1065.0 72.2 %up.10 = (f32[3072,1024]{1,0:T(8,128)}, f32[3072,1024]{1,0:T(8,128)}, bf16[4096,1024]{1,0:T(8,128)(2,1)}, bf16[4096,1024]{1,0:T(8,128)(2,1)}) custom-call(bf16[4096,4096]{1,0:T(8,128)(2,1)} %normalize.1.lhs, f32[2,1024,1024]{2,1,0:T(8,128)} %collective-permute-done.23.refs_0_.refs_4_, f32[2,1024,1024]{2,1,0:T(8,128)} %collective-permute-done.24.refs_1_.refs_5_, ...), custom_call_target="tpu_custom_call" | custom-call | flops 51539607552 | bytes 50331648 | tf_op jit(solution)/shard_map/up/pallas_call | solution.py:432
  1137.3 0.7 collective-permute-start.22
  1137.9 41.7 %up.11 = (f32[3072,1024]{1,0:T(8,128)}, bf16[1024,4096]{1,0:T(8,128)(2,1)}) custom-call(bf16[4096,4096]{1,0:T(8,128)(2,1)} %bitcast.71, f32[1,1024,1024]{2,1,0:T(8,128)} %collective-permute-done.25.refs_0_, f32[1,1024,1024]{2,1,0:T(8,128)} %collective-permute-done.26.refs_1_, f32[1,1024,1024]{2,1,0:T(8,128)} %collective-permute-done.29.refs_2_, ...), custom_call_target="tpu_custom_call" | custom-call | flops 25769803776 | bytes 50331648 | tf_op jit(solution)/shard_map/up/pallas_call | solution.py:432
  1179.6 82.4 %middle.7 = (bf16[3072,1024]{1,0:T(8,128)(2,1)}, bf16[3072,1024]{1,0:T(8,128)(2,1)}, bf16[3072,1024]{1,0:T(8,128)(2,1)}) custom-call(s32[4,1024,128]{2,1,0:T(8,128)} %broadcast_in_dim.11.pos_w, f32[16,1024]{1,0:T(8,128)} %reshape.114.par_w, bf16[8,128,256]{2,1,0:T(8,128)(2,1)} %convert_element_type.73.wg_w, f32[3072,1024]{1,0:T(8,128)} %get-tuple-element.139.px, ...), custom_call_target="tpu_custom_call" | custom-call | flops 4718592000 | bytes 56623104 | tf_op jit(solution)/shard_map/middle/pallas_call | solution.py:330
  1262.0 230.1 %grad_normed.3.refs_10_ = f32[3072,4096]{1,0:T(8,128)} custom-call(bf16[4096,1024]{1,0:T(8,128)(2,1)} %get-tuple-element.120.refs_0_, bf16[3072,1024]{1,0:T(8,128)(2,1)} %get-tuple-element.154.refs_1_, bf16[3072,1024]{1,0:T(8,128)(2,1)} %get-tuple-element.155.refs_2_, bf16[3072,1024]{1,0:T(8,128)(2,1)} %get-tuple-element.156.refs_3_, ...), custom_call_target="tpu_custom_call" | custom-call | flops 206158430208 | bytes 450000000 | tf_op jit(solution)/shard_map/grad_normed/pallas_call | solution.py:536
  1492.2 3.6 psum.50
  1496.4 1.2 collective-permute-start.31
  1497.6 2.0 collective-permute-start.32
  1500.8 161.3 %outputs.2 = (bf16[4096,4096]{1,0:T(8,128)(2,1)}, bf16[4096,4096]{1,0:T(8,128)(2,1)}, f32[2,8,4096]{2,1,0:T(8,128)}, f32[4096,1024]{1,0:T(8,128)}, f32[4096,1024]{1,0:T(8,128)}, /*index=5*/f32[1024,4096]{1,0:T(8,128)}) custom-call(bf16[4096,1024]{1,0:T(8,128)(2,1)} %get-tuple-element.132.refs_0_, bf16[3072,1024]{1,0:T(8,128)(2,1)} %get-tuple-element.126.refs_1_, ...), custom_call_target="tpu_custom_call" | custom-call | flops 103079215104 | bytes 251658240 | tf_op jit(solution)/shard_map/outputs/pallas_call | solution.py:505
  1662.2 1.3 copy-done.1
  1663.5 57.7 %outputs.3 = (bf16[4096,4096]{1,0:T(8,128)(2,1)}, bf16[4096,4096]{1,0:T(8,128)(2,1)}, f32[2,8,4096]{2,1,0:T(8,128)}) custom-call(bf16[4096,1024]{1,0:T(8,128)(2,1)} %get-tuple-element.132.refs_0_, f32[512,1024]{1,0:T(8,128)} %collective-permute-done.19.refs_1_, ...), custom_call_target="tpu_custom_call", output_to_operand_aliasing={{0}: (17, {}), {1}: (18, {})} | custom-call | flops 34359738368 | bytes 83886080 | tf_op jit(solution)/shard_map/outputs/pallas_call | solution.py:505
  1721.2 1.0 add_reduce_fusion
  1722.3 3.4 psum.54
  1726.3 1.1 fusion.1
  (121 shorter events, 12.8 us)
Async XLA Ops:
  7.2 1493.6 %all-reduce.6.cloned.1.call-start = ((), (), s32[]{:S(2)}) async-start(), calls=%async_computation.1 | async-start | bytes 102760448 | tf_op jit(solution)/shard_map/psum | solution.py:630
  12.3 8.2 copy-start.10
  14.4 6.2 copy-start.2
  24.4 9.3 copy-start.11
  24.4 387.7 %collective-permute-start.10 = (f32[2,1024,1024]{2,1,0:T(8,128)}, f32[2,1024,1024]{2,1,0:T(8,128)}, u32[]{:S(2)}, u32[]{:S(2)}) collective-permute-start(f32[2,1024,1024]{2,1,0:T(8,128)} %maximum_convert_fusion.1), channel_id=1, source_target_pairs={{0,4},{2,6},{4,0},{6,2},{1,5},{3,7},{5,1},{7,3}} | collective-permute-start | bytes 25165832 | tf_op jit(solution)/shard_map/ppermute | solution.py:574
  27.7 384.3 %collective-permute-start.8 = (f32[2,1024,1024]{2,1,0:T(8,128)}, f32[2,1024,1024]{2,1,0:T(8,128)}, u32[]{:S(2)}, u32[]{:S(2)}) collective-permute-start(f32[2,1024,1024]{2,1,0:T(8,128)} %maximum_convert_fusion.1), channel_id=1, source_target_pairs={{0,2},{2,0},{4,6},{6,4},{1,3},{3,1},{5,7},{7,5}} | collective-permute-start | bytes 25165832 | tf_op jit(solution)/shard_map/ppermute | solution.py:571
  33.1 378.9 %collective-permute-start.7 = (f32[2,1024,1024]{2,1,0:T(8,128)}, f32[2,1024,1024]{2,1,0:T(8,128)}, u32[]{:S(2)}, u32[]{:S(2)}) collective-permute-start(f32[2,1024,1024]{2,1,0:T(8,128)} %maximum_convert_fusion), channel_id=1, source_target_pairs={{0,2},{2,0},{4,6},{6,4},{1,3},{3,1},{5,7},{7,5}} | collective-permute-start | bytes 25165832 | tf_op jit(solution)/shard_map/ppermute | solution.py:571
  33.7 378.4 %collective-permute-start.9 = (f32[2,1024,1024]{2,1,0:T(8,128)}, f32[2,1024,1024]{2,1,0:T(8,128)}, u32[]{:S(2)}, u32[]{:S(2)}) collective-permute-start(f32[2,1024,1024]{2,1,0:T(8,128)} %maximum_convert_fusion), channel_id=1, source_target_pairs={{0,4},{2,6},{4,0},{6,2},{1,5},{3,7},{5,1},{7,3}} | collective-permute-start | bytes 25165832 | tf_op jit(solution)/shard_map/ppermute | solution.py:574
  68.2 80.7 %copy-start.14 = (s32[32,128]{1,0:T(8,128)S(1)}, s32[32,128]{1,0:T(8,128)}, u32[]{:S(2)}) copy-start(s32[32,128]{1,0:T(8,128)} %param.19) | copy-start | bytes 49156
  325.0 44.4 %copy-start = (bf16[4096,1024]{1,0:T(8,128)(2,1)S(1)}, bf16[4096,1024]{1,0:T(8,128)(2,1)}, u32[]{:S(2)}) copy-start(bf16[4096,1024]{1,0:T(8,128)(2,1)} %get-tuple-element.132.refs_0_) | copy-start | bytes 25165828
  325.0 87.6 %slice-start.2 = ((s8[8388608]{0:T(1024)(128)(4,1)}), s8[4194304]{0:T(1024)(128)(4,1)S(1)}, s32[]{:S(2)}) async-start(s8[8388608]{0:T(1024)(128)(4,1)} %bitcast.105), calls=%async_computation.4 | async-start | bytes 8388608
  369.4 43.2 %slice-start.3 = ((s8[8388608]{0:T(1024)(128)(4,1)}), s8[4194304]{0:T(1024)(128)(4,1)S(1)}, s32[]{:S(2)}) async-start(s8[8388608]{0:T(1024)(128)(4,1)} %bitcast.105), calls=%async_computation.5 | async-start | bytes 8388608
  412.1 54.7 %collective-permute-start.11 = (f32[2,1024,1024]{2,1,0:T(8,128)}, f32[2,1024,1024]{2,1,0:T(8,128)}, u32[]{:S(2)}, u32[]{:S(2)}) collective-permute-start(f32[2,1024,1024]{2,1,0:T(8,128)} %collective-permute-done.7.refs_0_.refs_4_), channel_id=1, source_target_pairs={{0,1},{1,0},{2,3},{3,2},{4,5},{5,4},{6,7},{7,6}} | collective-permute-start | bytes 25165832 | tf_op jit(solution)/shard_map/ppermute | solution.py:577
  412.1 55.3 %collective-permute-start.12 = (f32[2,1024,1024]{2,1,0:T(8,128)}, f32[2,1024,1024]{2,1,0:T(8,128)}, u32[]{:S(2)}, u32[]{:S(2)}) collective-permute-start(f32[2,1024,1024]{2,1,0:T(8,128)} %collective-permute-done.8.refs_1_.refs_5_), channel_id=1, source_target_pairs={{0,1},{1,0},{2,3},{3,2},{4,5},{5,4},{6,7},{7,6}} | collective-permute-start | bytes 25165832 | tf_op jit(solution)/shard_map/ppermute | solution.py:577
  454.9 1.2 copy-start.3
  454.9 1207.2 %all-reduce.4.cloned.1.call-start = ((), (), s32[]{:S(2)}) async-start(), calls=%async_computation | async-start | bytes 33554432 | tf_op jit(solution)/shard_map/psum | solution.py:647
  455.0 95.7 %collective-permute-start.13 = (f32[2,1024,1024]{2,1,0:T(8,128)}, f32[2,1024,1024]{2,1,0:T(8,128)}, u32[]{:S(2)}, u32[]{:S(2)}) collective-permute-start(f32[2,1024,1024]{2,1,0:T(8,128)} %collective-permute-done.9.refs_0_.refs_4_), channel_id=1, source_target_pairs={{0,1},{1,0},{2,3},{3,2},{4,5},{5,4},{6,7},{7,6}} | collective-permute-start | bytes 25165832 | tf_op jit(solution)/shard_map/ppermute | solution.py:577
  455.1 96.0 %collective-permute-start.14 = (f32[2,1024,1024]{2,1,0:T(8,128)}, f32[2,1024,1024]{2,1,0:T(8,128)}, u32[]{:S(2)}, u32[]{:S(2)}) collective-permute-start(f32[2,1024,1024]{2,1,0:T(8,128)} %collective-permute-done.10.refs_1_.refs_5_), channel_id=1, source_target_pairs={{0,1},{1,0},{2,3},{3,2},{4,5},{5,4},{6,7},{7,6}} | collective-permute-start | bytes 25165832 | tf_op jit(solution)/shard_map/ppermute | solution.py:577
  456.2 91.2 %collective-permute-start.4 = (f32[2176,128]{1,0:T(8,128)S(1)}, f32[2176,128]{1,0:T(8,128)S(1)}, u32[]{:S(2)}, u32[]{:S(2)}) collective-permute-start(f32[2176,128]{1,0:T(8,128)S(1)} %copy-done.3), channel_id=1, source_target_pairs={{0,2},{2,0},{4,6},{6,4},{1,3},{3,1},{5,7},{7,5}} | collective-permute-start | bytes 3342344 | tf_op jit(solution)/shard_map/ppermute | solution.py:585
  466.7 81.8 %collective-permute-start.5 = (f32[2176,128]{1,0:T(8,128)S(1)}, f32[2176,128]{1,0:T(8,128)S(1)}, u32[]{:S(2)}, u32[]{:S(2)}) collective-permute-start(f32[2176,128]{1,0:T(8,128)S(1)} %copy-done.3), channel_id=1, source_target_pairs={{0,4},{2,6},{4,0},{6,2},{1,5},{3,7},{5,1},{7,3}} | collective-permute-start | bytes 3342344 | tf_op jit(solution)/shard_map/ppermute | solution.py:585
  467.4 220.7 %collective-permute-start = (f32[1,1024,1024]{2,1,0:T(8,128)}, f32[1,1024,1024]{2,1,0:T(8,128)}, u32[]{:S(2)}, u32[]{:S(2)}) collective-permute-start(f32[1,1024,1024]{2,1,0:T(8,128)} %get-tuple-element.191), channel_id=1, source_target_pairs={{0,2},{2,0},{4,6},{6,4},{1,3},{3,1},{5,7},{7,5}} | collective-permute-start | bytes 12582920 | tf_op jit(solution)/shard_map/ppermute | solution.py:571
  547.4 209.4 %copy-start.5 = (f32[2176,128]{1,0:T(8,128)}, f32[2176,128]{1,0:T(8,128)S(1)}, u32[]{:S(2)}) copy-start(f32[2176,128]{1,0:T(8,128)S(1)} %collective-permute-done.4) | copy-start | bytes 3342340
  547.4 142.5 %collective-permute-start.2 = (f32[1,1024,1024]{2,1,0:T(8,128)}, f32[1,1024,1024]{2,1,0:T(8,128)}, u32[]{:S(2)}, u32[]{:S(2)}) collective-permute-start(f32[1,1024,1024]{2,1,0:T(8,128)} %get-tuple-element.191), channel_id=1, source_target_pairs={{0,4},{2,6},{4,0},{6,2},{1,5},{3,7},{5,1},{7,3}} | collective-permute-start | bytes 12582920 | tf_op jit(solution)/shard_map/ppermute | solution.py:574
  548.5 2.5 copy-start.6
  548.5 141.3 %collective-permute-start.1 = (f32[1,1024,1024]{2,1,0:T(8,128)}, f32[1,1024,1024]{2,1,0:T(8,128)}, u32[]{:S(2)}, u32[]{:S(2)}) collective-permute-start(f32[1,1024,1024]{2,1,0:T(8,128)} %get-tuple-element.190), channel_id=1, source_target_pairs={{0,2},{2,0},{4,6},{6,4},{1,3},{3,1},{5,7},{7,5}} | collective-permute-start | bytes 12582920 | tf_op jit(solution)/shard_map/ppermute | solution.py:571
  550.7 204.2 %collective-permute-start.3 = (f32[1,1024,1024]{2,1,0:T(8,128)}, f32[1,1024,1024]{2,1,0:T(8,128)}, u32[]{:S(2)}, u32[]{:S(2)}) collective-permute-start(f32[1,1024,1024]{2,1,0:T(8,128)} %get-tuple-element.190), channel_id=1, source_target_pairs={{0,4},{2,6},{4,0},{6,2},{1,5},{3,7},{5,1},{7,3}} | collective-permute-start | bytes 12582920 | tf_op jit(solution)/shard_map/ppermute | solution.py:574
  551.1 136.8 %collective-permute-start.6 = (f32[2176,128]{1,0:T(8,128)S(1)}, f32[2176,128]{1,0:T(8,128)S(1)}, u32[]{:S(2)}, u32[]{:S(2)}) collective-permute-start(f32[2176,128]{1,0:T(8,128)S(1)} %copy-done.3), channel_id=1, source_target_pairs={{0,6},{2,4},{4,2},{6,0},{1,7},{3,5},{5,3},{7,1}} | collective-permute-start | bytes 3342344 | tf_op jit(solution)/shard_map/ppermute | solution.py:585
  687.9 351.5 %collective-permute-start.23 = (f32[2,1024,1024]{2,1,0:T(8,128)}, f32[2,1024,1024]{2,1,0:T(8,128)}, u32[]{:S(2)}, u32[]{:S(2)}) collective-permute-start(f32[2,1024,1024]{2,1,0:T(8,128)} %collective-permute-done.7.refs_0_.refs_4_), channel_id=1, source_target_pairs={{0,4},{2,6},{4,0},{6,2},{1,5},{3,7},{5,1},{7,3}} | collective-permute-start | bytes 25165832 | tf_op jit(solution)/shard_map/ppermute | solution.py:574
  688.1 351.2 %collective-permute-start.24 = (f32[2,1024,1024]{2,1,0:T(8,128)}, f32[2,1024,1024]{2,1,0:T(8,128)}, u32[]{:S(2)}, u32[]{:S(2)}) collective-permute-start(f32[2,1024,1024]{2,1,0:T(8,128)} %collective-permute-done.10.refs_1_.refs_5_), channel_id=1, source_target_pairs={{0,2},{2,0},{4,6},{6,4},{1,3},{3,1},{5,7},{7,5}} | collective-permute-start | bytes 25165832 | tf_op jit(solution)/shard_map/ppermute | solution.py:571
  754.9 7.5 collective-permute-start.15
  754.9 35.9 %collective-permute-start.16 = (f32[1,1024,1024]{2,1,0:T(8,128)}, f32[1,1024,1024]{2,1,0:T(8,128)}, u32[]{:S(2)}, u32[]{:S(2)}) collective-permute-start(f32[1,1024,1024]{2,1,0:T(8,128)} %collective-permute-done.1.refs_1_), channel_id=1, source_target_pairs={{0,1},{1,0},{2,3},{3,2},{4,5},{5,4},{6,7},{7,6}} | collective-permute-start | bytes 12582920 | tf_op jit(solution)/shard_map/ppermute | solution.py:577
  755.4 36.5 %collective-permute-start.17 = (f32[1,1024,1024]{2,1,0:T(8,128)}, f32[1,1024,1024]{2,1,0:T(8,128)}, u32[]{:S(2)}, u32[]{:S(2)}) collective-permute-start(f32[1,1024,1024]{2,1,0:T(8,128)} %collective-permute-done.2.refs_0_), channel_id=1, source_target_pairs={{0,1},{1,0},{2,3},{3,2},{4,5},{5,4},{6,7},{7,6}} | collective-permute-start | bytes 12582920 | tf_op jit(solution)/shard_map/ppermute | solution.py:577
  756.8 31.8 %slice-start = ((f32[2176,128]{1,0:T(8,128)}), f32[128,128]{1,0:T(8,128)S(1)}, s32[]{:S(2)}) async-start(f32[2176,128]{1,0:T(8,128)} %copy-done.5), calls=%async_computation.2 | async-start | bytes 131072 | tf_op jit(solution)/shard_map/slice | solution.py:606
  756.8 33.4 %slice-start.1 = ((f32[2176,128]{1,0:T(8,128)}), f32[128,128]{1,0:T(8,128)S(1)}, s32[]{:S(2)}) async-start(f32[2176,128]{1,0:T(8,128)} %copy-done.6), calls=%async_computation.3 | async-start | bytes 131072 | tf_op jit(solution)/shard_map/slice | solution.py:606
  762.4 154.2 %collective-permute-start.18 = (f32[1,1024,1024]{2,1,0:T(8,128)}, f32[1,1024,1024]{2,1,0:T(8,128)}, u32[]{:S(2)}, u32[]{:S(2)}) collective-permute-start(f32[1,1024,1024]{2,1,0:T(8,128)} %collective-permute-done.3.refs_1_), channel_id=1, source_target_pairs={{0,1},{1,0},{2,3},{3,2},{4,5},{5,4},{6,7},{7,6}} | collective-permute-start | bytes 12582920 | tf_op jit(solution)/shard_map/ppermute | solution.py:577
  790.8 248.6 %collective-permute-start.25 = (f32[1,1024,1024]{2,1,0:T(8,128)}, f32[1,1024,1024]{2,1,0:T(8,128)}, u32[]{:S(2)}, u32[]{:S(2)}) collective-permute-start(f32[1,1024,1024]{2,1,0:T(8,128)} %collective-permute-done.refs_0_), channel_id=1, source_target_pairs={{0,4},{2,6},{4,0},{6,2},{1,5},{3,7},{5,1},{7,3}} | collective-permute-start | bytes 12582920 | tf_op jit(solution)/shard_map/ppermute | solution.py:574
  791.9 247.5 %collective-permute-start.26 = (f32[1,1024,1024]{2,1,0:T(8,128)}, f32[1,1024,1024]{2,1,0:T(8,128)}, u32[]{:S(2)}, u32[]{:S(2)}) collective-permute-start(f32[1,1024,1024]{2,1,0:T(8,128)} %collective-permute-done.3.refs_1_), channel_id=1, source_target_pairs={{0,2},{2,0},{4,6},{6,4},{1,3},{3,1},{5,7},{7,5}} | collective-permute-start | bytes 12582920 | tf_op jit(solution)/shard_map/ppermute | solution.py:571
  957.2 82.7 %copy-start.7 = (f32[8,72,128]{2,1,0:T(8,128)S(1)}, f32[8,72,128]{2,1,0:T(8,128)}, u32[]{:S(2)}) copy-start(f32[8,72,128]{2,1,0:T(8,128)} %get-tuple-element.167) | copy-start | bytes 884740
  957.2 82.9 %copy-start.13 = (f32[8,8,128]{2,1,0:T(8,128)S(1)}, f32[8,8,128]{2,1,0:T(8,128)}, u32[]{:S(2)}) copy-start(f32[8,8,128]{2,1,0:T(8,128)} %get-tuple-element.166) | copy-start | bytes 98308
  957.2 82.9 %copy-start.16 = (bf16[4096]{0:T(1024)(128)(2,1)S(1)}, bf16[4096]{0:T(1024)(128)(2,1)}, u32[]{:S(2)}) copy-start(bf16[4096]{0:T(1024)(128)(2,1)} %param.33) | copy-start | bytes 24580
  957.2 84.1 %copy-start.12 = (bf16[4096]{0:T(1024)(128)(2,1)S(1)}, bf16[4096]{0:T(1024)(128)(2,1)}, u32[]{:S(2)}) copy-start(bf16[4096]{0:T(1024)(128)(2,1)} %param.20) | copy-start | bytes 24580
  1039.4 13.5 collective-permute-start.27
  1039.4 25.5 %collective-permute-start.28 = (f32[2,1024,1024]{2,1,0:T(8,128)}, f32[2,1024,1024]{2,1,0:T(8,128)}, u32[]{:S(2)}, u32[]{:S(2)}) collective-permute-start(f32[2,1024,1024]{2,1,0:T(8,128)} %collective-permute-done.24.refs_1_.refs_5_), channel_id=1, source_target_pairs={{0,1},{1,0},{2,3},{3,2},{4,5},{5,4},{6,7},{7,6}} | collective-permute-start | bytes 25165832 | tf_op jit(solution)/shard_map/ppermute | solution.py:577
  1047.7 448.7 %collective-permute-start.19 = (f32[512,1024]{1,0:T(8,128)}, f32[512,1024]{1,0:T(8,128)}, u32[]{:S(2)}, u32[]{:S(2)}) collective-permute-start(f32[512,1024]{1,0:T(8,128)} %get-tuple-element.185), channel_id=1, source_target_pairs={{0,2},{2,0},{4,6},{6,4},{1,3},{3,1},{5,7},{7,5}} | collective-permute-start | bytes 6291464 | tf_op jit(solution)/shard_map/ppermute | solution.py:571
  1047.8 448.6 %collective-permute-start.21 = (f32[512,1024]{1,0:T(8,128)}, f32[512,1024]{1,0:T(8,128)}, u32[]{:S(2)}, u32[]{:S(2)}) collective-permute-start(f32[512,1024]{1,0:T(8,128)} %get-tuple-element.185), channel_id=1, source_target_pairs={{0,4},{2,6},{4,0},{6,2},{1,5},{3,7},{5,1},{7,3}} | collective-permute-start | bytes 6291464 | tf_op jit(solution)/shard_map/ppermute | solution.py:574
  1048.5 88.8 %collective-permute-start.29 = (f32[1,1024,1024]{2,1,0:T(8,128)}, f32[1,1024,1024]{2,1,0:T(8,128)}, u32[]{:S(2)}, u32[]{:S(2)}) collective-permute-start(f32[1,1024,1024]{2,1,0:T(8,128)} %collective-permute-done.25.refs_0_), channel_id=1, source_target_pairs={{0,1},{1,0},{2,3},{3,2},{4,5},{5,4},{6,7},{7,6}} | collective-permute-start | bytes 12582920 | tf_op jit(solution)/shard_map/ppermute | solution.py:577
  1052.9 85.0 %collective-permute-start.30 = (f32[1,1024,1024]{2,1,0:T(8,128)}, f32[1,1024,1024]{2,1,0:T(8,128)}, u32[]{:S(2)}, u32[]{:S(2)}) collective-permute-start(f32[1,1024,1024]{2,1,0:T(8,128)} %collective-permute-done.26.refs_1_), channel_id=1, source_target_pairs={{0,1},{1,0},{2,3},{3,2},{4,5},{5,4},{6,7},{7,6}} | collective-permute-start | bytes 12582920 | tf_op jit(solution)/shard_map/ppermute | solution.py:577
  1064.9 431.4 %collective-permute-start.20 = (f32[512,1024]{1,0:T(8,128)}, f32[512,1024]{1,0:T(8,128)}, u32[]{:S(2)}, u32[]{:S(2)}) collective-permute-start(f32[512,1024]{1,0:T(8,128)} %get-tuple-element.184), channel_id=1, source_target_pairs={{0,2},{2,0},{4,6},{6,4},{1,3},{3,1},{5,7},{7,5}} | collective-permute-start | bytes 6291464 | tf_op jit(solution)/shard_map/ppermute | solution.py:571
  1137.3 359.1 %collective-permute-start.22 = (f32[512,1024]{1,0:T(8,128)}, f32[512,1024]{1,0:T(8,128)}, u32[]{:S(2)}, u32[]{:S(2)}) collective-permute-start(f32[512,1024]{1,0:T(8,128)} %get-tuple-element.184), channel_id=1, source_target_pairs={{0,4},{2,6},{4,0},{6,2},{1,5},{3,7},{5,1},{7,3}} | collective-permute-start | bytes 6291464 | tf_op jit(solution)/shard_map/ppermute | solution.py:574
  1262.0 230.2 %copy-start.9 = (f32[10,1024]{1,0:T(8,128)S(1)}, f32[10,1024]{1,0:T(8,128)}, u32[]{:S(2)}) copy-start(f32[10,1024]{1,0:T(8,128)} %pad_maximum_fusion) | copy-start | bytes 122884
  1262.0 238.2 %copy-start.15 = (f32[1024]{0:T(1024)S(1)}, f32[1024]{0:T(1024)}, u32[]{:S(2)}) copy-start(f32[1024]{0:T(1024)} %param.31) | copy-start | bytes 12292
  1496.4 165.8 %collective-permute-start.31 = (f32[512,1024]{1,0:T(8,128)}, f32[512,1024]{1,0:T(8,128)S(1)}, u32[]{:S(2)}, u32[]{:S(2)}) collective-permute-start(f32[512,1024]{1,0:T(8,128)} %collective-permute-done.19.refs_1_), channel_id=1, source_target_pairs={{0,4},{2,6},{4,0},{6,2},{1,5},{3,7},{5,1},{7,3}} | collective-permute-start | bytes 6291464 | tf_op jit(solution)/shard_map/ppermute | solution.py:574
  1497.6 164.6 %collective-permute-start.32 = (f32[512,1024]{1,0:T(8,128)}, f32[512,1024]{1,0:T(8,128)}, u32[]{:S(2)}, u32[]{:S(2)}) collective-permute-start(f32[512,1024]{1,0:T(8,128)} %collective-permute-done.22.refs_4_), channel_id=1, source_target_pairs={{0,2},{2,0},{4,6},{6,4},{1,3},{3,1},{5,7},{7,5}} | collective-permute-start | bytes 6291464 | tf_op jit(solution)/shard_map/ppermute | solution.py:571
  1662.2 1.4 copy-start.1
  1663.5 57.7 %copy-start.8 = (f32[2,8,4096]{2,1,0:T(8,128)S(1)}, f32[2,8,4096]{2,1,0:T(8,128)}, u32[]{:S(2)}) copy-start(f32[2,8,4096]{2,1,0:T(8,128)} %get-tuple-element.174) | copy-start | bytes 786436
  1663.5 62.8 %copy-start.4 = (f32[8,128,256]{2,1,0:T(8,128)S(1)}, f32[8,128,256]{2,1,0:T(8,128)}, u32[]{:S(2)}) copy-start(f32[8,128,256]{2,1,0:T(8,128)} %get-tuple-element.183) | copy-start | bytes 3145732
Sparse Core Ops, SparseCore 0:
  455.1 155.0 all-reduce.5
  1137.4 339.5 all-reduce.3

commit v4 on v3

--- a/solution.py
+++ b/solution.py
@@ -17,10 +17,10 @@
 ROW = (((1,), (0,)), ((), ()))
 CHAN = (((1,), (1,)), ((), ()))
 TOK = (((0,), (0,)), ((), ()))
-GELU_K0 = 0.7978845608028654
-GELU_K1 = 0.7978845608028654 * 0.044715
+GELU_K0 = 1.5957691216057308
+GELU_K1 = GELU_K0 * 0.044715
 N_SUMS = 9
-SPAN = 32
+SPAN = 64
 N_PAR = 10
 BORROW = TAPS - 1
 
@@ -80,7 +80,7 @@
     def _():
         for seq in range(SUB):
             in_x[pl.ds(seq * pitch, n_tok), :] = px[pl.ds(seq * n_tok, n_tok), :]
-        b_x, b_y, *taps, c_b, b_a, b_i, nsp = param_rows(par_f)
+        b_x, b_y, *taps, c_b, nb_a, nb_i, nsp = param_rows(par_f)
         h_in, *halo = [jnp.where(me == 0, 0.0, recv[f_msg, pl.ds(SUB * j, SUB), :]) for j in range(TAPS)]
         xb_r = s_xb.at[f_slot] if grads else None
         if grads:
@@ -130,15 +130,15 @@
                     both = c16_r[pair(t), :].astype(F32)
                     c = both[:SUB]
                 reset = pos_f[rows, :] == 0
-                r = jax.nn.sigmoid(pre_a[rows, :] + b_a)
-                i = jax.nn.sigmoid(pre_i[rows, :] + b_i)
+                r = 1.0 / (1.0 + jnp.exp(nb_a - pre_a[rows, :]))
+                i = 1.0 / (1.0 + jnp.exp(nb_i - pre_i[rows, :]))
                 la = nsp * r
                 a = jnp.exp(la)
-                y2 = la + la
-                poly = -y2 * (1.0 + y2 * (0.5 + y2 * (1.0 / 6.0 + y2 * (1.0 / 24.0))))
-                q = jnp.maximum(jnp.where(y2 > -0.0625, poly, 1.0 - a * a), 1e-37)
-                rm = lax.rsqrt(q)
-                m = jnp.where(reset, 1.0, q * rm)
+                th = jnp.tanh(jnp.abs(la))
+                twice, more = th + th, 1.0 + th
+                root = lax.rsqrt(jnp.maximum(twice * more, 1e-37))
+                rm = more * root
+                m = jnp.where(reset, 1.0, twice * root)
                 ic = i * c
                 k = a * ic * rm
                 a = jnp.where(reset, 0.0, a)
@@ -154,10 +154,9 @@
                     r_r[rows, :] = r
                 v = in_y[strided(t), :] + b_y
                 v2 = v * v
-                th = jnp.tanh(v * (GELU_K0 + GELU_K1 * v2))
-                hv = 0.5 * v
-                y = hv + hv * th
-                dy = (0.5 + 0.5 * th) + hv * (1.0 - th * th) * (GELU_K0 + (3.0 * GELU_K1) * v2)
+                cdf = jax.nn.sigmoid(v * (GELU_K0 + GELU_K1 * v2))
+                y = v * cdf
+                dy = cdf + (y - y * cdf) * (GELU_K0 + (3.0 * GELU_K1) * v2)
                 d = in_d[strided(t), :]
                 g_r[rows, :] = d * y
                 out_m[strided(t), :] = h * y
@@ -337,6 +336,7 @@
 
 
 NORM_EPS = 1e-6
+UNIT = 4 * SUB
 IN_SPECS = (P(None, "cp", None), P(None, "cp", None), P(None, "cp"), P(), P(None, "tp"), P("tp"), P(None, "tp"), P("tp"), P(None, "tp"), P("tp"), P("tp", None, None), P("tp"), P("tp", None, None), P("tp"), P("tp"), P("tp", None), P())
 OUT_SPECS = (P(None, "cp", None), P(None, "cp", None), P(), P(None, "tp"), P("tp"), P(None, "tp"), P("tp"), P(None, "tp"), P("tp"), P("tp", None, None), P("tp"), P("tp", None, None), P("tp"), P("tp"), P("tp", None), P())
 
@@ -346,14 +346,26 @@
 
 
 def norm_kernel(x_ref, scale_ref, n_ref):
-    x = x_ref[...].astype(F32)
-    inv = lax.rsqrt(jnp.mean(x * x, axis=-1, keepdims=True) + NORM_EPS)
-    n_ref[...] = (x * inv * (1.0 + scale_ref[...])).astype(BF16)
+    rows, width = 4 * SUB, x_ref.shape[1]
+    tiles = [pl.ds(n * LANES, LANES) for n in range(width // LANES)]
+
+    def unit(u, _):
+        here = pl.ds(pl.multiple_of(u * rows, rows), rows)
+        square = jnp.zeros((rows, LANES), F32)
+        for cols in tiles:
+            x = x_ref[here, cols].astype(F32)
+            square = square + x * x
+        inv = jnp.broadcast_to(lax.rsqrt(jnp.sum(square, axis=-1, keepdims=True) / width + NORM_EPS), (rows, LANES))
+        for cols in tiles:
+            n_ref[here, cols] = (x_ref[here, cols].astype(F32) * inv * scale_ref[:, cols]).astype(BF16)
+        return 0
+
+    lax.fori_loop(0, x_ref.shape[0] // rows, unit, 0)
 
 
 def normalize(x, scale):
     rows, width = x.shape
-    tile = 256
+    tile = 512
     return pl.pallas_call(
         norm_kernel, grid=(rows // tile,), name="normalize",
         in_specs=[pl.BlockSpec((tile, width), lambda i: (i, 0)), pl.BlockSpec((1, width), lambda i: (0, 0))],
@@ -460,82 +472,102 @@
             sum_ref[which, :, cols] += sum(val[SUB * r:SUB * (r + 1)] for r in range(rows // SUB))
 
 
-def z_kernel(n_own, n_far, n_into, n_moved, *refs):
-    own, far, right = refs[:n_own], refs[n_own:n_own + 2 * n_far], refs[n_own + 2 * n_far:2 * n_own + 3 * n_far]
-    x_ref, bias_ref, dn_ref, x_rows, gz_rows, scale_ref = refs[2 * n_own + 3 * n_far:][:6]
-    rest = refs[2 * n_own + 3 * n_far + 6 + n_into:]
-    moved, (out_ref, grad_ref, sum_ref), placed, far_16 = rest[:n_moved], rest[n_moved:n_moved + 3], rest[n_moved + 3:-1], rest[-1]
+def z_kernel(n_pairs, n_moved, *refs):
+    left, right = refs[:n_pairs], refs[n_pairs:2 * n_pairs]
+    x_ref, bias_ref, *rows_in = refs[2 * n_pairs:2 * n_pairs + 6]
+    moved, (out_ref, *rows_out), placed = refs[2 * n_pairs + 6:-3 - n_moved], refs[-3 - n_moved:len(refs) - n_moved], refs[len(refs) - n_moved:]
     for src, dst in zip(moved, placed):
         dst[...] = src[...]
-    unit = 4 * SUB
 
     @pl.when(jnp.logical_and(pl.program_id(0) == 0, pl.program_id(1) == 0))
     def _():
-        sum_ref[...] = jnp.zeros_like(sum_ref)
-        for k, ref in enumerate(far):
-            half = ref.shape[0]
-            far_16[k // 2, pl.ds(k % 2 * half, half), :] = ref[...].astype(BF16)
+        rows_out[-1][...] = jnp.zeros_like(rows_out[-1])
 
     acc = x_ref[...].astype(F32) + bias_ref[...]
-    for lhs, rhs in zip(list(own) + [far_16.at[k] for k in range(n_far)], right):
+    for lhs, rhs in zip(left, right):
         acc = acc + jnp.dot(lhs[...], rhs[...], preferred_element_type=F32)
     out_ref[...] = acc.astype(BF16)
-    for first in range(0, dn_ref.shape[0], unit):
-        finish_rows(unit, first, dn_ref, x_rows, gz_rows, scale_ref, grad_ref, sum_ref)
-
-
-def outputs(own, far, rights, x, bias, dn, gz, scale, first_row, into, moved):
+    for first in range(0, rows_in[0].shape[0], UNIT):
+        finish_rows(UNIT, first, *rows_in, *rows_out)
+
+
+def outputs(left, right, x, bias, dn, gz, scale, moved):
     rows, width = dn.shape
-    depth = own[0].shape[1]
+    depth = left[0].shape[1]
     bm, bn = 1024, 512
     n_row, n_col = rows // bm, width // bn
     share = rows // (n_row * n_col)
-    skip, skip_share = first_row // bm, first_row // share
-    tile = pl.BlockSpec((bm, bn), lambda i, j: (i + skip, j))
-    part = pl.BlockSpec((share, width), lambda i, j: (i * n_col + j, 0))
-    line = pl.BlockSpec((share, width), lambda i, j: (i * n_col + j + skip_share, 0))
-    args = list(own) + [v for pair in far for v in pair] + list(rights) + [x, bias, dn, x, gz, scale] + list(into) + list(moved)
-    in_specs = [pl.BlockSpec((bm, depth), lambda i, j: (i + skip, 0))] * len(own)
-    in_specs += [pl.BlockSpec((bm // 2, depth), lambda i, j: (0, 0))] * (2 * len(far))
-    in_specs += [pl.BlockSpec((depth, bn), lambda i, j: (0, j))] * len(rights)
-    in_specs += [tile, pl.BlockSpec((1, bn), lambda i, j: (0, j)), part, line, line, pl.BlockSpec((1, width), lambda i, j: (0, 0))]
-    in_specs += [pl.BlockSpec(memory_space=pl.ANY)] * len(into)
+    tile = pl.BlockSpec((bm, bn), lambda i, j: (i, j))
+    line = pl.BlockSpec((share, width), lambda i, j: (i * n_col + j, 0))
+    in_specs = [pl.BlockSpec((bm, depth), lambda i, j: (i, 0))] * len(left) + [pl.BlockSpec((depth, bn), lambda i, j: (0, j))] * len(right)
+    in_specs += [tile, pl.BlockSpec((1, bn), lambda i, j: (0, j)), line, line, line, pl.BlockSpec((1, width), lambda i, j: (0, 0))]
     n_move = 16
     passing = [pl.BlockSpec((v.shape[0] // n_move, v.shape[1]), lambda i, j: (jnp.minimum(i * n_col + j, n_move - 1), 0)) for v in moved]
     return pl.pallas_call(
-        functools.partial(z_kernel, len(own), len(far), len(into), len(moved)), grid=(n_row, n_col), name="outputs",
+        functools.partial(z_kernel, len(left), len(moved)), grid=(n_row, n_col), name="outputs",
         in_specs=in_specs + passing, out_specs=[tile, line, pl.BlockSpec((2, SUB, width), lambda i, j: (0, 0, 0))] + passing,
-        out_shape=[jax.ShapeDtypeStruct(x.shape, BF16), jax.ShapeDtypeStruct(x.shape, BF16), jax.ShapeDtypeStruct((2, SUB, width), F32)] + [jax.ShapeDtypeStruct(v.shape, v.dtype) for v in moved],
-        scratch_shapes=[pltpu.VMEM((max(len(far), 1), bm if far else 2 * SUB, depth), BF16)],
-        input_output_aliases={len(args) - len(moved) - len(into) + k: k for k in range(len(into))},
-        cost_estimate=pl.CostEstimate(flops=2 * len(rights) * rows * width * depth, bytes_accessed=rows * width * 20, transcendentals=rows),
+        out_shape=[jax.ShapeDtypeStruct(x.shape, BF16)] * 2 + [jax.ShapeDtypeStruct((2, SUB, width), F32)] + [jax.ShapeDtypeStruct(v.shape, v.dtype) for v in moved],
+        cost_estimate=pl.CostEstimate(flops=2 * len(right) * rows * width * depth, bytes_accessed=rows * width * 20, transcendentals=rows),
         compiler_params=params_of("arbitrary", "arbitrary"),
-    )(*args)
-
-
-def dn_kernel(n_pairs, *refs):
+    )(*left, *right, x, bias, dn, x, gz, scale, *moved)
+
+
+def tail_kernel(z_ref, bias_ref, dn_ref, x_ref, gz_ref, scale_ref, _, __, out_ref, grad_ref, sum_ref):
+    @pl.when(pl.program_id(0) == 0)
+    def _():
+        sum_ref[...] = jnp.zeros_like(sum_ref)
+
+    def unit(u, _):
+        here = pl.ds(pl.multiple_of(u * UNIT, UNIT), UNIT)
+        for n in range(out_ref.shape[1] // LANES):
+            cols = pl.ds(n * LANES, LANES)
+            out_ref[here, cols] = (x_ref[here, cols].astype(F32) + (z_ref[here, cols] + bias_ref[:, cols])).astype(BF16)
+        finish_rows(UNIT, u * UNIT, dn_ref, x_ref, gz_ref, scale_ref, grad_ref, sum_ref)
+        return 0
+
+    lax.fori_loop(0, out_ref.shape[0] // UNIT, unit, 0)
+
+
+def tail_outputs(z_sum, bias, dn, x, gz, scale, z, grad_x, first_row):
+    rows, width = dn.shape
+    share = 128
+    skip = first_row // share
+    near = pl.BlockSpec((share, width), lambda i: (i, 0))
+    line = pl.BlockSpec((share, width), lambda i: (i + skip, 0))
+    whole = pl.BlockSpec((1, width), lambda i: (0, 0))
+    here = pl.BlockSpec(memory_space=pl.ANY)
+    return pl.pallas_call(
+        tail_kernel, grid=(rows // share,), name="tail_outputs",
+        in_specs=[near, whole, near, line, line, whole, here, here], out_specs=[line, line, pl.BlockSpec((2, SUB, width), lambda i: (0, 0, 0))],
+        out_shape=[jax.ShapeDtypeStruct(x.shape, BF16)] * 2 + [jax.ShapeDtypeStruct((2, SUB, width), F32)], input_output_aliases={6: 0, 7: 1},
+        cost_estimate=pl.CostEstimate(flops=rows * width * 1500, bytes_accessed=rows * width * 16, transcendentals=rows),
+        compiler_params=params_of("arbitrary"),
+    )(z_sum, bias, dn, x, gz, scale, z, grad_x)
+
+
+def wide_kernel(n_pairs, flip, *refs):
     left, right, out_ref = refs[:n_pairs], refs[n_pairs:2 * n_pairs], refs[2 * n_pairs]
 
     def column(c, _):
         cols = pl.ds(pl.multiple_of(c * 256, 256), 256)
-        acc = lax.dot_general(left[0][...], right[0][cols, :], CHAN, preferred_element_type=F32)
-        for lhs, rhs in zip(left[1:], right[1:]):
-            acc = acc + lax.dot_general(lhs[...], rhs[cols, :], CHAN, preferred_element_type=F32)
+        acc = 0.0
+        for lhs, rhs in zip(left, right):
+            acc = acc + lax.dot_general(lhs[...], rhs[cols, :] if flip else rhs[:, cols], CHAN if flip else ROW, preferred_element_type=F32)
         out_ref[:, cols] = acc
         return 0
 
     lax.fori_loop(0, out_ref.shape[1] // 256, column, 0)
 
 
-def grad_normed(lefts, rights, first_row, rows):
+def wide_product(lefts, rights, flip, first_row, rows):
     depth = lefts[0].shape[1]
-    width = rights[0].shape[0]
+    width = rights[0].shape[0 if flip else 1]
     bm, bn = 1024, 512
     skip = first_row // bm
     n = len(lefts)
     return pl.pallas_call(
-        functools.partial(dn_kernel, n), grid=(rows // bm, width // bn), name="grad_normed",
-        in_specs=[pl.BlockSpec((bm, depth), lambda i, j: (i + skip, 0))] * n + [pl.BlockSpec((bn, depth), lambda i, j: (j, 0))] * n,
+        functools.partial(wide_kernel, n, flip), grid=(rows // bm, width // bn), name="wide_product",
+        in_specs=[pl.BlockSpec((bm, depth), lambda i, j: (i + skip, 0))] * n + [pl.BlockSpec((bn, depth), lambda i, j: (j, 0)) if flip else pl.BlockSpec((depth, bn), lambda i, j: (0, j))] * n,
         out_specs=pl.BlockSpec((bm, bn), lambda i, j: (i, j)), out_shape=jax.ShapeDtypeStruct((rows, width), F32),
         cost_estimate=pl.CostEstimate(flops=2 * n * rows * width * depth, bytes_accessed=450000000, transcendentals=0),
         compiler_params=params_of("arbitrary", "arbitrary"),
@@ -553,7 +585,7 @@
 
 
 def stack_params(b_x, b_y, conv_w, conv_b, b_a, b_i, a_param):
-    rows = [b_x, b_y, conv_w[0], conv_w[1], conv_w[2], conv_w[3], conv_b, b_a, b_i]
+    rows = [b_x, b_y, *conv_w, conv_b, -b_a, -b_i]
     rows = [row.astype(F32) for row in rows] + [-8.0 * jax.nn.softplus(a_param)]
     return jnp.concatenate([jnp.stack(rows), jnp.zeros((16 - len(rows), a_param.shape[0]), F32)], axis=0)
 
@@ -582,7 +614,6 @@
     par = stack_params(b_x, b_y, conv_w, conv_b, b_a, b_i, a_param)
     w_gate = jnp.concatenate([w_a, w_i], axis=2)
     small = jnp.concatenate([par.reshape(-1), w_gate.astype(F32).reshape(-1)]).reshape(-1, LANES)
-    smalls = [lax.ppermute(small, "tp", [(j, j ^ far) for j in range(4)]) for far in range(1, 4)]
 
     def after(values, *before):
         return lax.optimization_barrier((values, before))[0]
@@ -599,7 +630,7 @@
     def cores(values):
         return values, [swap_core(v) for v in values]
 
-    group_a = to_neighbours((w_x, w_y), 0, small)
+    group_a = to_neighbours((w_x, w_y), 0, seg_pos)
 
     def unpack(s):
         flat = s.reshape(-1)
@@ -612,10 +643,11 @@
         own, other = side
         return [tuple((v, (k,)) for v in list(own) + list(other)) for k in range(n)]
 
-    normed = normalize(x, scale)
+    normed = normalize(x, 1.0 + scale)
     pos_rep = spread_positions(seg_pos)
     px, py = plain_up(normed, [w_x, w_y], False)
     group_b = to_neighbours((w_out,), 1, px)
+    smalls = [lax.ppermute(after(small, px), "tp", [(j, j ^ far) for j in range(4)]) for far in range(1, 4)]
     dm, = plain_up(after(gz, px), [w_out], True)
     mixed, dpy, dbr, g_gate, s_y, s_b = middle(px, py, dm, pos_rep, par, w_gate, True, 0)
     g_w_out = token_product(mixed, gz)
@@ -631,33 +663,31 @@
 
     px_x, py_x, wx_x, wy_x = up(after(normed, g_w_x), quarters(side_x, 2), False, shared)
     px_y, py_y, wx_y, wy_y = up(after(normed, px_x), quarters(side_y, 2), False, shared)
-    group_b, smalls = after((group_b, smalls), px_y)
+    group_b = after(group_b, px_y)
     out_x, out_y = [cores(values) for values in group_b]
     diag_b = onward(group_b)
-    dn_tail = grad_normed(after([dbr, dpy], px_y), [w_x, w_y], shared, tile)
+    dn_tail = wide_product(after([dbr, dpy], px_y), [w_x, w_y], True, shared, tile)
+    smalls = after(smalls, dn_tail)
     dm_x, wo_x = up(after(gz, dn_tail), quarters(out_x, 1), True, shared)
     mixed_x, dpy_x, dbr_x = middle(px_x, py_x, dm_x, pos_rep, *unpack(smalls[0]), False, 1)
     dm_y, wo_y = up(after(gz, mixed_x), quarters(out_y, 1), True, shared)
     mixed_y, dpy_y, dbr_y = middle(px_y, py_y, dm_y, pos_rep, *unpack(smalls[1]), False, 1)
     diag_a, diag_b = after((diag_a, diag_b), mixed_y)
     diag_a, diag_b = cores(diag_a), cores(diag_b)
-    rows_tail = [after(mixed, mixed_y)[shared + h * (tile // 2):shared + (h + 1) * (tile // 2)].astype(F32) for h in range(2)]
-    tail_x, tail_y = [swap_x(v) for v in rows_tail], [swap_y(v) for v in rows_tail]
-    px_d, py_d, wx_d, wy_d = up(after(normed, mixed_y), quarters(diag_a, 2), False, shared)
-    dn_tail = lax.psum(after(dn_tail, px_d), "tp")
+    z_tail = wide_product(after([mixed], mixed_y), [w_out], False, shared, tile)
+    dn_sum, z_sum = lax.psum((dn_tail, z_tail), "tp")
+    px_d, py_d, wx_d, wy_d = up(after(normed, z_tail), quarters(diag_a, 2), False, shared)
     dm_d, wo_d = up(after(gz, px_d), quarters(diag_b, 1), True, shared)
     mixed_d, dpy_d, dbr_d = middle(px_d, py_d, dm_d, pos_rep, *unpack(smalls[2]), False, 1)
 
-    far_x, far_y = after((tail_x, tail_y), mixed_d)
-    far_d = [swap_y(far_x[0]), swap_x(far_y[1])]
     wx_all, wy_all, wo_all = [w_x, wx_x, wx_y, wx_d], [w_y, wy_x, wy_y, wy_d], [w_out, wo_x, wo_y, wo_d]
-    dn = grad_normed([dbr, dbr_x, dbr_y, dbr_d, dpy, dpy_x, dpy_y, dpy_d], wx_all + wy_all, 0, shared)
+    dn = wide_product([dbr, dbr_x, dbr_y, dbr_d, dpy, dpy_x, dpy_y, dpy_d], wx_all + wy_all, True, 0, shared)
     bias = b_out.astype(F32).reshape(1, d_model)
     *tall, g_gate = own_grads
     lines = lax.psum(after(jnp.concatenate([s_y, s_b]), mixed_d), "cp")
-    z_out, grad_x, sums_x, *tall = outputs([mixed, mixed_x, mixed_y, mixed_d], [], wo_all, x, bias, after(dn, lines), gz, 1.0 + scale, 0, (), tall)
+    z_out, grad_x, sums_x, *tall = outputs([mixed, mixed_x, mixed_y, mixed_d], wo_all, x, bias, after(dn, lines), gz, 1.0 + scale, tall)
     g_w_x, g_w_y, g_w_out = tall
-    z_out, grad_x, sums_t = outputs([mixed], [far_x, far_y, far_d], wo_all, x, bias, dn_tail, gz, 1.0 + scale, shared, (z_out, grad_x), ())
+    z_out, grad_x, sums_t = tail_outputs(z_sum, bias, dn_sum, x, gz, 1.0 + scale, z_out, grad_x, shared)
     z_out = z_out.reshape(x_in.shape)
     sums_x = jnp.sum(sums_x + sums_t, axis=1)
 

time: 1740 us -> 1710 us (0.983)
  Pallas kernels: 1360 us -> 1330 us
    ppermute x3, waiting for transfers between devices: 57 us -> 19.7 us  [block_body(): lax.ppermute(after(small, px), 'tp', [(j, j ^ far) for j in range(4)])]
    ppermute x12, waiting for transfers between devices: 22 us -> 46.5 us  [swap_core(): return lax.ppermute(v, 'cp', [(0, 1), (1, 0)])]
    ppermute x9 -> x6, waiting for transfers between devices: 65 us -> 88 us  [swap_y(): return lax.ppermute(v, 'tp', [(j, j ^ 2) for j in range(4)])]
    pallas_call x4 -> x5, Pallas kernels: 474 us -> 461 us  [the longest x3 272 us: wide_product(): pl.pallas_call(functools.partial(wide_kernel, n, flip), grid=(rows // bm,...]
  transfers between devices with their start and end apart: 35 -> 29, of which waited for: 5 -> 8; matrix products, arithmetic and copies ran while one was open for 9% -> 9% of each run, Pallas kernels for 75% -> 77%
where the time goes in v4:
time: 1710 us; the launch traced here: 1700 us
  Pallas kernels  1330 us (78%)
  waiting for transfers between devices  154 us (9%)
  matrix products  129 us (8%)
  starting transfers between devices  24.9 us (1%)
  other arithmetic  21 us (1%)
  local copies, waits for them, and re-layouts  20.4 us (1%)
    pallas_call x4, Pallas kernels, middle(): pl.pallas_call(functools.partial(middle_kernel, n_steps, n_tiles, n_tok,...  362 us
    pallas_call x6, Pallas kernels, up(): pl.pallas_call(functools.partial(up_kernel, n, n_parts, flip), grid=(n_ro...  351 us
    pallas_call x3, Pallas kernels, wide_product(): pl.pallas_call(functools.partial(wide_kernel, n, flip), grid=(rows // bm,...  272 us
    pallas_call x1, Pallas kernels, outputs(): pl.pallas_call(functools.partial(z_kernel, len(left), len(moved)), grid=(...  164 us
    dot_general x3, matrix products, token_product(): return lax.dot_general(lhs, rhs, TOK, preferred_element_type=F32)  129 us
    pallas_call x2, Pallas kernels, plain_up(): pl.pallas_call(functools.partial(plain_up_kernel, n, flip), grid=(width /...  124 us
    ppermute x6, waiting for transfers between devices, swap_y(): return lax.ppermute(v, 'tp', [(j, j ^ 2) for j in range(4)])  88 us
    ppermute x12, waiting for transfers between devices, swap_core(): return lax.ppermute(v, 'cp', [(0, 1), (1, 0)])  46.5 us
  transfers between devices with their start and end apart: 29, of which 8 were waited for; matrix products, arithmetic and copies ran while one was open for 9% of the time, Pallas kernels for 77%

profile of v4, /device:TPU:0, one launch (start us, length us, event | category | flops | bytes accessed | tf_op | source)
XLA Modules:
  0.0 1701.4 jit_solution(1564728595385083533)
XLA Ops:
  7.2 4.5 dynamic-slice_bitcast_fusion
  11.7 3.9 maximum_convert_fusion
  15.7 3.3 collective-permute-start.3
  19.0 1.5 collective-permute-start.5
  20.6 3.8 maximum_convert_fusion.1
  24.9 0.6 convert_add_fusion
  26.1 30.6 %normalize.1.lhs = bf16[4096,4096]{1,0:T(8,128)(2,1)} custom-call(bf16[4096,4096]{1,0:T(8,128)(2,1)} %bitcast.61, f32[1,4096]{1,0:T(1,128)} %bitcast.84), custom_call_target="tpu_custom_call" | custom-call | flops 10066329600 | bytes 67108864 | tf_op jit(solution)/shard_map/normalize/pallas_call | solution.py:369
  56.6 80.7 %plain_up.2 = (f32[4096,1024]{1,0:T(8,128)}, f32[4096,1024]{1,0:T(8,128)}) custom-call(bf16[4096,4096]{1,0:T(8,128)(2,1)} %normalize.1.lhs, bf16[4096,1024]{1,0:T(8,128)(2,1)} %refs_8_.1, bf16[4096,1024]{1,0:T(8,128)(2,1)} %refs_12_.1), custom_call_target="tpu_custom_call" | custom-call | flops 68719476736 | bytes 67108864 | tf_op jit(solution)/shard_map/plain_up/pallas_call | solution.py:389
  137.5 43.2 %plain_up.3.dm = f32[4096,1024]{1,0:T(8,128)} custom-call(bf16[4096,4096]{1,0:T(8,128)(2,1)} %bitcast.65, bf16[1024,4096]{1,0:T(8,128)(2,1)} %refs_4_.1), custom_call_target="tpu_custom_call" | custom-call | flops 34359738368 | bytes 67108864 | tf_op jit(solution)/shard_map/plain_up/pallas_call | solution.py:389
  180.7 1.3 concatenate.12.par_w
  182.0 2.2 broadcast_in_dim.11.pos_w
  184.2 124.3 %middle.4 = (bf16[4096,1024]{1,0:T(8,128)(2,1)}, bf16[4096,1024]{1,0:T(8,128)(2,1)}, bf16[4096,1024]{1,0:T(8,128)(2,1)}, f32[8,128,256]{2,1,0:T(8,128)}, f32[8,8,128]{2,1,0:T(8,128)}, /*index=5*/f32[8,72,128]{2,1,0:T(8,128)}) custom-call(s32[4,1024,128]{2,1,0:T(8,128)} %broadcast_in_dim.11.pos_w, f32[16,1024]{1,0:T(8,128)} %concatenate.12.par_w, ...), custom_call_target="tpu_custom_call" | custom-call | flops 6291456000 | bytes 75497472 | tf_op jit(solution)/shard_map/middle/pallas_call | solution.py:329
  308.6 44.3 %fusion.3 = f32[4096,1024]{1,0:T(8,128)} fusion(bf16[4096,4096]{1,0:T(8,128)(2,1)} %normalize.1.lhs, bf16[4096,1024]{1,0:T(8,128)(2,1)} %get-tuple-element.113.refs_1_.refs_4_), kind=kOutput, calls=%fused_computation.30 | convolution fusion | flops 34359738368 | bytes 58720256 | tf_op jit(solution)/shard_map/dot_general | solution.py:578
  352.8 42.4 %fusion.4 = f32[4096,1024]{1,0:T(8,128)} fusion(bf16[4096,4096]{1,0:T(8,128)(2,1)} %normalize.1.lhs, bf16[4096,1024]{1,0:T(8,128)(2,1)S(1)} %copy-done.22), kind=kOutput, calls=%fused_computation.31 | convolution fusion | flops 34359738368 | bytes 58720256 | tf_op jit(solution)/shard_map/dot_general | solution.py:578
  395.3 42.5 %fusion.5 = f32[1024,4096]{1,0:T(8,128)} fusion(bf16[4096,1024]{1,0:T(8,128)(2,1)S(1)} %bitcast.75, bf16[4096,4096]{1,0:T(8,128)(2,1)} %bitcast.66), kind=kOutput, calls=%fused_computation.32 | convolution fusion | flops 34359738368 | bytes 58720256 | tf_op jit(solution)/shard_map/dot_general | solution.py:578
  439.7 2.0 collective-permute-start
  441.8 8.6 bitcast_convert_fusion
  450.3 9.7 collective-permute-done.7.refs_2_.refs_6_
  460.0 2.4 collective-permute-start.1
  462.4 21.6 %collective-permute-done.8.refs_3_.refs_7_ = f32[2,1024,1024]{2,1,0:T(8,128)} collective-permute-done((f32[2,1024,1024]{2,1,0:T(8,128)}, f32[2,1024,1024]{2,1,0:T(8,128)}, u32[]{:S(2)}, u32[]{:S(2)}) %collective-permute-start.8) | collective-permute-done | bytes 8388640 | tf_op jit(solution)/shard_map/ppermute | solution.py:609
  484.0 2.3 collective-permute-start.11
  486.3 79.1 %up.6 = (f32[3072,1024]{1,0:T(8,128)}, f32[3072,1024]{1,0:T(8,128)}, bf16[4096,1024]{1,0:T(8,128)(2,1)}, bf16[4096,1024]{1,0:T(8,128)(2,1)}) custom-call(bf16[4096,4096]{1,0:T(8,128)(2,1)} %normalize.1.lhs, f32[2,1024,1024]{2,1,0:T(8,128)} %collective-permute-done.3.refs_0_.refs_4_, f32[2,1024,1024]{2,1,0:T(8,128)} %collective-permute-done.4.refs_1_.refs_5_, ...), custom_call_target="tpu_custom_call" | custom-call | flops 51539607552 | bytes 50331648 | tf_op jit(solution)/shard_map/up/pallas_call | solution.py:444
  565.4 1.7 collective-permute-start.13
  567.1 0.8 collective-permute-start.12
  568.0 76.6 %up.7 = (f32[3072,1024]{1,0:T(8,128)}, f32[3072,1024]{1,0:T(8,128)}, bf16[4096,1024]{1,0:T(8,128)(2,1)}, bf16[4096,1024]{1,0:T(8,128)(2,1)}) custom-call(bf16[4096,4096]{1,0:T(8,128)(2,1)} %normalize.1.lhs, f32[2,1024,1024]{2,1,0:T(8,128)} %collective-permute-done.5.refs_0_.refs_4_, f32[2,1024,1024]{2,1,0:T(8,128)} %collective-permute-done.6.refs_1_.refs_5_, ...), custom_call_target="tpu_custom_call" | custom-call | flops 51539607552 | bytes 50331648 | tf_op jit(solution)/shard_map/up/pallas_call | solution.py:444
  644.7 3.1 collective-permute-start.2
  647.8 25.0 %wide_product.3 = f32[1024,4096]{1,0:T(8,128)} custom-call(bf16[4096,1024]{1,0:T(8,128)(2,1)} %get-tuple-element.112.refs_0_, bf16[4096,1024]{1,0:T(8,128)(2,1)} %get-tuple-element.113.refs_1_.refs_4_, bf16[4096,1024]{1,0:T(8,128)(2,1)} %refs_8_.1, bf16[4096,1024]{1,0:T(8,128)(2,1)} %refs_12_.1), custom_call_target="tpu_custom_call" | custom-call | flops 17179869184 | bytes 450000000 | tf_op jit(solution)/shard_map/wide_product/pallas_call | solution.py:568
  672.8 19.7 %collective-permute-done.2 = f32[2176,128]{1,0:T(8,128)S(1)} collective-permute-done((f32[2176,128]{1,0:T(8,128)S(1)}, f32[2176,128]{1,0:T(8,128)S(1)}, u32[]{:S(2)}, u32[]{:S(2)}) %collective-permute-start.2) | collective-permute-done | bytes 1114144 | tf_op jit(solution)/shard_map/ppermute | solution.py:650
  692.7 1.7 collective-permute-start.20
  694.4 78.5 %collective-permute-done.14.refs_1_ = f32[1,1024,1024]{2,1,0:T(8,128)} collective-permute-done((f32[1,1024,1024]{2,1,0:T(8,128)}, f32[1,1024,1024]{2,1,0:T(8,128)}, u32[]{:S(2)}, u32[]{:S(2)}) %collective-permute-start.14) | collective-permute-done | bytes 4194336 | tf_op jit(solution)/shard_map/ppermute | solution.py:606
  773.4 1.3 slice_bitcast_fusion.2
  774.7 5.6 collective-permute-done.15.refs_2_
  780.5 1.9 copy-done.21
  782.4 0.8 slice.70
  783.2 0.6 reshape.109.par_w
  783.9 1.0 convert_element_type.61.wg_w
  784.8 0.6 reshape.110.par_w
  785.5 1.0 convert_element_type.63.wg_w
  786.4 1.7 collective-permute-start.21
  788.2 4.3 collective-permute-done.17.refs_2_
  793.0 40.5 %up.8 = (f32[3072,1024]{1,0:T(8,128)}, bf16[1024,4096]{1,0:T(8,128)(2,1)}) custom-call(bf16[4096,4096]{1,0:T(8,128)(2,1)} %bitcast.67, f32[1,1024,1024]{2,1,0:T(8,128)} %collective-permute-done.11.refs_0_, f32[1,1024,1024]{2,1,0:T(8,128)} %collective-permute-done.12.refs_1_, f32[1,1024,1024]{2,1,0:T(8,128)} %copy-done.21, ...), custom_call_target="tpu_custom_call" | custom-call | flops 25769803776 | bytes 50331648 | tf_op jit(solution)/shard_map/up/pallas_call | solution.py:444
  833.4 79.0 %middle.5 = (bf16[3072,1024]{1,0:T(8,128)(2,1)}, bf16[3072,1024]{1,0:T(8,128)(2,1)}, bf16[3072,1024]{1,0:T(8,128)(2,1)}) custom-call(s32[4,1024,128]{2,1,0:T(8,128)} %broadcast_in_dim.11.pos_w, f32[16,1024]{1,0:T(8,128)} %reshape.110.par_w, bf16[8,128,256]{2,1,0:T(8,128)(2,1)} %convert_element_type.63.wg_w, f32[3072,1024]{1,0:T(8,128)} %get-tuple-element.107.px, ...), custom_call_target="tpu_custom_call" | custom-call | flops 4718592000 | bytes 56623104 | tf_op jit(solution)/shard_map/middle/pallas_call | solution.py:329
  912.4 40.6 %up.9 = (f32[3072,1024]{1,0:T(8,128)}, bf16[1024,4096]{1,0:T(8,128)(2,1)}) custom-call(bf16[4096,4096]{1,0:T(8,128)(2,1)} %bitcast.68, f32[1,1024,1024]{2,1,0:T(8,128)} %collective-permute-done.13.refs_0_, f32[1,1024,1024]{2,1,0:T(8,128)} %collective-permute-done.14.refs_1_, f32[1,1024,1024]{2,1,0:T(8,128)} %collective-permute-done.17.refs_2_, ...), custom_call_target="tpu_custom_call" | custom-call | flops 25769803776 | bytes 50331648 | tf_op jit(solution)/shard_map/up/pallas_call | solution.py:444
  953.0 79.0 %middle.6 = (bf16[3072,1024]{1,0:T(8,128)(2,1)}, bf16[3072,1024]{1,0:T(8,128)(2,1)}, bf16[3072,1024]{1,0:T(8,128)(2,1)}) custom-call(s32[4,1024,128]{2,1,0:T(8,128)} %broadcast_in_dim.11.pos_w, f32[16,1024]{1,0:T(8,128)} %reshape.109.par_w, bf16[8,128,256]{2,1,0:T(8,128)(2,1)} %convert_element_type.61.wg_w, f32[3072,1024]{1,0:T(8,128)} %get-tuple-element.111.px, ...), custom_call_target="tpu_custom_call" | custom-call | flops 4718592000 | bytes 56623104 | tf_op jit(solution)/shard_map/middle/pallas_call | solution.py:329
  1032.1 9.5 collective-permute-done.21.refs_0_
  1042.1 0.6 reshape.127
  1042.9 0.6 reshape.113.par_w
  1043.6 1.0 convert_element_type.65.wg_w
  1044.6 16.6 wide_product.4
  1061.8 5.3 collective-permute-done.24.refs_3_.refs_7_
  1067.1 73.0 %up.10 = (f32[3072,1024]{1,0:T(8,128)}, f32[3072,1024]{1,0:T(8,128)}, bf16[4096,1024]{1,0:T(8,128)(2,1)}, bf16[4096,1024]{1,0:T(8,128)(2,1)}) custom-call(bf16[4096,4096]{1,0:T(8,128)(2,1)} %normalize.1.lhs, f32[2,1024,1024]{2,1,0:T(8,128)} %collective-permute-done.19.refs_0_.refs_4_, f32[2,1024,1024]{2,1,0:T(8,128)} %collective-permute-done.20.refs_1_.refs_5_, ...), custom_call_target="tpu_custom_call" | custom-call | flops 51539607552 | bytes 50331648 | tf_op jit(solution)/shard_map/up/pallas_call | solution.py:444
  1140.1 41.4 %up.11 = (f32[3072,1024]{1,0:T(8,128)}, bf16[1024,4096]{1,0:T(8,128)(2,1)}) custom-call(bf16[4096,4096]{1,0:T(8,128)(2,1)} %bitcast.69, f32[1,1024,1024]{2,1,0:T(8,128)} %collective-permute-done.21.refs_0_, f32[1,1024,1024]{2,1,0:T(8,128)} %collective-permute-done.22.refs_1_, f32[1,1024,1024]{2,1,0:T(8,128)} %collective-permute-done.25.refs_2_, ...), custom_call_target="tpu_custom_call" | custom-call | flops 25769803776 | bytes 50331648 | tf_op jit(solution)/shard_map/up/pallas_call | solution.py:444
  1181.5 79.9 %middle.7 = (bf16[3072,1024]{1,0:T(8,128)(2,1)}, bf16[3072,1024]{1,0:T(8,128)(2,1)}, bf16[3072,1024]{1,0:T(8,128)(2,1)}) custom-call(s32[4,1024,128]{2,1,0:T(8,128)} %broadcast_in_dim.11.pos_w, f32[16,1024]{1,0:T(8,128)} %reshape.113.par_w, bf16[8,128,256]{2,1,0:T(8,128)(2,1)} %convert_element_type.65.wg_w, f32[3072,1024]{1,0:T(8,128)} %get-tuple-element.136.px, ...), custom_call_target="tpu_custom_call" | custom-call | flops 4718592000 | bytes 56623104 | tf_op jit(solution)/shard_map/middle/pallas_call | solution.py:329
  1261.4 3.6 psum.58
  1265.0 0.6 slice.93
  1265.6 230.1 %wide_product.5.refs_10_ = f32[3072,4096]{1,0:T(8,128)} custom-call(bf16[4096,1024]{1,0:T(8,128)(2,1)} %get-tuple-element.112.refs_0_, bf16[3072,1024]{1,0:T(8,128)(2,1)} %get-tuple-element.146.refs_1_, bf16[3072,1024]{1,0:T(8,128)(2,1)} %get-tuple-element.147.refs_2_, bf16[3072,1024]{1,0:T(8,128)(2,1)} %get-tuple-element.148.refs_3_, ...), custom_call_target="tpu_custom_call" | custom-call | flops 206158430208 | bytes 450000000 | tf_op jit(solution)/shard_map/wide_product/pallas_call | solution.py:568
  1495.7 1.5 slice_multiply_fusion
  1497.3 0.6 divide_multiply_fusion
  1497.9 163.6 %outputs.1 = (bf16[4096,4096]{1,0:T(8,128)(2,1)}, bf16[4096,4096]{1,0:T(8,128)(2,1)}, f32[2,8,4096]{2,1,0:T(8,128)}, f32[4096,1024]{1,0:T(8,128)}, f32[4096,1024]{1,0:T(8,128)}, /*index=5*/f32[1024,4096]{1,0:T(8,128)}) custom-call(bf16[4096,1024]{1,0:T(8,128)(2,1)} %get-tuple-element.129.refs_0_, bf16[3072,1024]{1,0:T(8,128)(2,1)} %get-tuple-element.123.refs_1_, ...), custom_call_target="tpu_custom_call" | custom-call | flops 103079215104 | bytes 251658240 | tf_op jit(solution)/shard_map/outputs/pallas_call | solution.py:506
  1661.5 25.6 %tail_outputs.1 = (bf16[4096,4096]{1,0:T(8,128)(2,1)}, bf16[4096,4096]{1,0:T(8,128)(2,1)}, f32[2,8,4096]{2,1,0:T(8,128)}) custom-call(f32[1024,4096]{1,0:T(8,128)} %get-tuple-element.172.z_ref, f32[1,4096]{1,0:T(1,128)} %bitcast.88, f32[1024,4096]{1,0:T(8,128)} %get-tuple-element.173.dn_ref, ...), custom_call_target="tpu_custom_call", output_to_operand_aliasing={{0}: (6, {}), {1}: (7, {})} | custom-call | flops 6291456000 | bytes 67108864 | tf_op jit(solution)/shard_map/tail_outputs/pallas_call | solution.py:539
  1687.2 1.0 add_reduce_fusion
  1688.3 4.3 psum.62
  1692.6 0.6 fusion.2
  1693.2 1.1 fusion.1
  (118 shorter events, 5.8 us)
Async XLA Ops:
  7.2 1490.7 %all-reduce.7.cloned.1.call-start = ((), (), s32[]{:S(2)}) async-start(), calls=%async_computation.1 | async-start | bytes 102760448 | tf_op jit(solution)/shard_map/psum | solution.py:662
  15.6 9.3 copy-start.14
  15.6 9.9 copy-start.11
  15.6 10.2 copy-start.16
  15.6 10.2 copy-start.17
  15.6 10.2 copy-start.10
  15.7 10.3 copy-start.18
  15.7 10.3 copy-start.19
  15.7 10.3 copy-start.20
  15.7 10.3 copy-start.12
  15.7 10.3 copy-start.4
  15.7 422.1 %collective-permute-start.3 = (f32[2,1024,1024]{2,1,0:T(8,128)}, f32[2,1024,1024]{2,1,0:T(8,128)}, u32[]{:S(2)}, u32[]{:S(2)}) collective-permute-start(f32[2,1024,1024]{2,1,0:T(8,128)} %maximum_convert_fusion), channel_id=1, source_target_pairs={{0,2},{2,0},{4,6},{6,4},{1,3},{3,1},{5,7},{7,5}} | collective-permute-start | bytes 25165832 | tf_op jit(solution)/shard_map/ppermute | solution.py:603
  19.0 418.8 %collective-permute-start.5 = (f32[2,1024,1024]{2,1,0:T(8,128)}, f32[2,1024,1024]{2,1,0:T(8,128)}, u32[]{:S(2)}, u32[]{:S(2)}) collective-permute-start(f32[2,1024,1024]{2,1,0:T(8,128)} %maximum_convert_fusion), channel_id=1, source_target_pairs={{0,4},{2,6},{4,0},{6,2},{1,5},{3,7},{5,1},{7,3}} | collective-permute-start | bytes 25165832 | tf_op jit(solution)/shard_map/ppermute | solution.py:606
  24.4 413.4 %collective-permute-start.4 = (f32[2,1024,1024]{2,1,0:T(8,128)}, f32[2,1024,1024]{2,1,0:T(8,128)}, u32[]{:S(2)}, u32[]{:S(2)}) collective-permute-start(f32[2,1024,1024]{2,1,0:T(8,128)} %maximum_convert_fusion.1), channel_id=1, source_target_pairs={{0,2},{2,0},{4,6},{6,4},{1,3},{3,1},{5,7},{7,5}} | collective-permute-start | bytes 25165832 | tf_op jit(solution)/shard_map/ppermute | solution.py:603
  24.9 412.9 %collective-permute-start.6 = (f32[2,1024,1024]{2,1,0:T(8,128)}, f32[2,1024,1024]{2,1,0:T(8,128)}, u32[]{:S(2)}, u32[]{:S(2)}) collective-permute-start(f32[2,1024,1024]{2,1,0:T(8,128)} %maximum_convert_fusion.1), channel_id=1, source_target_pairs={{0,4},{2,6},{4,0},{6,2},{1,5},{3,7},{5,1},{7,3}} | collective-permute-start | bytes 25165832 | tf_op jit(solution)/shard_map/ppermute | solution.py:606
  56.6 80.7 %copy-start.5 = (bf16[8,128,128]{2,1,0:T(8,128)(2,1)S(1)}, bf16[8,128,128]{2,1,0:T(8,128)(2,1)}, u32[]{:S(2)}) copy-start(bf16[8,128,128]{2,1,0:T(8,128)(2,1)} %param.29) | copy-start | bytes 786436
  137.5 43.2 %copy-start = (bf16[8,128,256]{2,1,0:T(8,128)(2,1)}, bf16[8,128,256]{2,1,0:T(8,128)(2,1)S(1)}, u32[]{:S(2)}) copy-start(bf16[8,128,256]{2,1,0:T(8,128)(2,1)S(1)} %constant_dynamic-update-slice_fusion.wg_w) | copy-start | bytes 1572868
  308.5 44.3 %copy-start.22 = (bf16[4096,1024]{1,0:T(8,128)(2,1)S(1)}, bf16[4096,1024]{1,0:T(8,128)(2,1)}, u32[]{:S(2)}) copy-start(bf16[4096,1024]{1,0:T(8,128)(2,1)} %get-tuple-element.112.refs_0_) | copy-start | bytes 25165828
  308.5 86.7 %slice-start = ((s8[8388608]{0:T(1024)(128)(4,1)}), s8[4194304]{0:T(1024)(128)(4,1)S(1)}, s32[]{:S(2)}) async-start(s8[8388608]{0:T(1024)(128)(4,1)} %bitcast.74), calls=%async_computation.2 | async-start | bytes 8388608
  352.8 42.4 %slice-start.1 = ((s8[8388608]{0:T(1024)(128)(4,1)}), s8[4194304]{0:T(1024)(128)(4,1)S(1)}, s32[]{:S(2)}) async-start(s8[8388608]{0:T(1024)(128)(4,1)} %bitcast.74), calls=%async_computation.3 | async-start | bytes 8388608
  437.8 1.1 copy-start.1
  437.8 1.8 copy-start.7
  437.9 1223.6 %all-reduce.5.cloned.1.call-start = ((), (), s32[]{:S(2)}) async-start(), calls=%async_computation | async-start | bytes 67108864 | tf_op jit(solution)/shard_map/psum | solution.py:678
  437.9 22.0 %collective-permute-start.7 = (f32[2,1024,1024]{2,1,0:T(8,128)}, f32[2,1024,1024]{2,1,0:T(8,128)}, u32[]{:S(2)}, u32[]{:S(2)}) collective-permute-start(f32[2,1024,1024]{2,1,0:T(8,128)} %collective-permute-done.3.refs_0_.refs_4_), channel_id=1, source_target_pairs={{0,1},{1,0},{2,3},{3,2},{4,5},{5,4},{6,7},{7,6}} | collective-permute-start | bytes 25165832 | tf_op jit(solution)/shard_map/ppermute | solution.py:609
  438.0 46.0 %collective-permute-start.8 = (f32[2,1024,1024]{2,1,0:T(8,128)}, f32[2,1024,1024]{2,1,0:T(8,128)}, u32[]{:S(2)}, u32[]{:S(2)}) collective-permute-start(f32[2,1024,1024]{2,1,0:T(8,128)} %collective-permute-done.4.refs_1_.refs_5_), channel_id=1, source_target_pairs={{0,1},{1,0},{2,3},{3,2},{4,5},{5,4},{6,7},{7,6}} | collective-permute-start | bytes 25165832 | tf_op jit(solution)/shard_map/ppermute | solution.py:609
  438.5 128.7 %collective-permute-start.9 = (f32[2,1024,1024]{2,1,0:T(8,128)}, f32[2,1024,1024]{2,1,0:T(8,128)}, u32[]{:S(2)}, u32[]{:S(2)}) collective-permute-start(f32[2,1024,1024]{2,1,0:T(8,128)} %collective-permute-done.5.refs_0_.refs_4_), channel_id=1, source_target_pairs={{0,1},{1,0},{2,3},{3,2},{4,5},{5,4},{6,7},{7,6}} | collective-permute-start | bytes 25165832 | tf_op jit(solution)/shard_map/ppermute | solution.py:609
  438.5 129.5 %collective-permute-start.10 = (f32[2,1024,1024]{2,1,0:T(8,128)}, f32[2,1024,1024]{2,1,0:T(8,128)}, u32[]{:S(2)}, u32[]{:S(2)}) collective-permute-start(f32[2,1024,1024]{2,1,0:T(8,128)} %collective-permute-done.6.refs_1_.refs_5_), channel_id=1, source_target_pairs={{0,1},{1,0},{2,3},{3,2},{4,5},{5,4},{6,7},{7,6}} | collective-permute-start | bytes 25165832 | tf_op jit(solution)/shard_map/ppermute | solution.py:609
  439.7 125.7 %collective-permute-start = (f32[2176,128]{1,0:T(8,128)S(1)}, f32[2176,128]{1,0:T(8,128)S(1)}, u32[]{:S(2)}, u32[]{:S(2)}) collective-permute-start(f32[2176,128]{1,0:T(8,128)S(1)} %maximum_bitcast_fusion), channel_id=1, source_target_pairs={{0,2},{2,0},{4,6},{6,4},{1,3},{3,1},{5,7},{7,5}} | collective-permute-start | bytes 3342344 | tf_op jit(solution)/shard_map/ppermute | solution.py:650
  460.0 184.7 %collective-permute-start.1 = (f32[2176,128]{1,0:T(8,128)S(1)}, f32[2176,128]{1,0:T(8,128)}, u32[]{:S(2)}, u32[]{:S(2)}) collective-permute-start(f32[2176,128]{1,0:T(8,128)S(1)} %maximum_bitcast_fusion), channel_id=1, source_target_pairs={{0,4},{2,6},{4,0},{6,2},{1,5},{3,7},{5,1},{7,3}} | collective-permute-start | bytes 3342344 | tf_op jit(solution)/shard_map/ppermute | solution.py:650
  484.0 208.7 %collective-permute-start.11 = (f32[1,1024,1024]{2,1,0:T(8,128)}, f32[1,1024,1024]{2,1,0:T(8,128)}, u32[]{:S(2)}, u32[]{:S(2)}) collective-permute-start(f32[1,1024,1024]{2,1,0:T(8,128)} %get-tuple-element.179), channel_id=1, source_target_pairs={{0,2},{2,0},{4,6},{6,4},{1,3},{3,1},{5,7},{7,5}} | collective-permute-start | bytes 12582920 | tf_op jit(solution)/shard_map/ppermute | solution.py:603
  565.4 129.1 %collective-permute-start.13 = (f32[1,1024,1024]{2,1,0:T(8,128)}, f32[1,1024,1024]{2,1,0:T(8,128)}, u32[]{:S(2)}, u32[]{:S(2)}) collective-permute-start(f32[1,1024,1024]{2,1,0:T(8,128)} %get-tuple-element.179), channel_id=1, source_target_pairs={{0,4},{2,6},{4,0},{6,2},{1,5},{3,7},{5,1},{7,3}} | collective-permute-start | bytes 12582920 | tf_op jit(solution)/shard_map/ppermute | solution.py:606
  567.1 127.3 %collective-permute-start.12 = (f32[1,1024,1024]{2,1,0:T(8,128)}, f32[1,1024,1024]{2,1,0:T(8,128)}, u32[]{:S(2)}, u32[]{:S(2)}) collective-permute-start(f32[1,1024,1024]{2,1,0:T(8,128)} %get-tuple-element.178), channel_id=1, source_target_pairs={{0,2},{2,0},{4,6},{6,4},{1,3},{3,1},{5,7},{7,5}} | collective-permute-start | bytes 12582920 | tf_op jit(solution)/shard_map/ppermute | solution.py:603
  568.0 205.0 %collective-permute-start.14 = (f32[1,1024,1024]{2,1,0:T(8,128)}, f32[1,1024,1024]{2,1,0:T(8,128)}, u32[]{:S(2)}, u32[]{:S(2)}) collective-permute-start(f32[1,1024,1024]{2,1,0:T(8,128)} %get-tuple-element.178), channel_id=1, source_target_pairs={{0,4},{2,6},{4,0},{6,2},{1,5},{3,7},{5,1},{7,3}} | collective-permute-start | bytes 12582920 | tf_op jit(solution)/shard_map/ppermute | solution.py:606
  644.7 47.8 %collective-permute-start.2 = (f32[2176,128]{1,0:T(8,128)S(1)}, f32[2176,128]{1,0:T(8,128)S(1)}, u32[]{:S(2)}, u32[]{:S(2)}) collective-permute-start(f32[2176,128]{1,0:T(8,128)S(1)} %maximum_bitcast_fusion), channel_id=1, source_target_pairs={{0,6},{2,4},{4,2},{6,0},{1,7},{3,5},{5,3},{7,1}} | collective-permute-start | bytes 3342344 | tf_op jit(solution)/shard_map/ppermute | solution.py:650
  692.5 339.6 %collective-permute-start.19 = (f32[2,1024,1024]{2,1,0:T(8,128)}, f32[2,1024,1024]{2,1,0:T(8,128)}, u32[]{:S(2)}, u32[]{:S(2)}) collective-permute-start(f32[2,1024,1024]{2,1,0:T(8,128)} %collective-permute-done.3.refs_0_.refs_4_), channel_id=1, source_target_pairs={{0,4},{2,6},{4,0},{6,2},{1,5},{3,7},{5,1},{7,3}} | collective-permute-start | bytes 25165832 | tf_op jit(solution)/shard_map/ppermute | solution.py:606
  692.7 339.4 %collective-permute-start.20 = (f32[2,1024,1024]{2,1,0:T(8,128)}, f32[2,1024,1024]{2,1,0:T(8,128)}, u32[]{:S(2)}, u32[]{:S(2)}) collective-permute-start(f32[2,1024,1024]{2,1,0:T(8,128)} %collective-permute-done.6.refs_1_.refs_5_), channel_id=1, source_target_pairs={{0,2},{2,0},{4,6},{6,4},{1,3},{3,1},{5,7},{7,5}} | collective-permute-start | bytes 25165832 | tf_op jit(solution)/shard_map/ppermute | solution.py:603
  772.9 7.4 collective-permute-start.15
  772.9 13.5 collective-permute-start.16
  773.4 19.0 %collective-permute-start.17 = (f32[1,1024,1024]{2,1,0:T(8,128)}, f32[1,1024,1024]{2,1,0:T(8,128)}, u32[]{:S(2)}, u32[]{:S(2)}) collective-permute-start(f32[1,1024,1024]{2,1,0:T(8,128)} %collective-permute-done.13.refs_0_), channel_id=1, source_target_pairs={{0,1},{1,0},{2,3},{3,2},{4,5},{5,4},{6,7},{7,6}} | collective-permute-start | bytes 12582920 | tf_op jit(solution)/shard_map/ppermute | solution.py:609
  780.3 2.1 copy-start.21
  780.3 132.1 %collective-permute-start.18 = (f32[1,1024,1024]{2,1,0:T(8,128)}, f32[1,1024,1024]{2,1,0:T(8,128)}, u32[]{:S(2)}, u32[]{:S(2)}) collective-permute-start(f32[1,1024,1024]{2,1,0:T(8,128)} %collective-permute-done.14.refs_1_), channel_id=1, source_target_pairs={{0,1},{1,0},{2,3},{3,2},{4,5},{5,4},{6,7},{7,6}} | collective-permute-start | bytes 12582920 | tf_op jit(solution)/shard_map/ppermute | solution.py:609
  786.4 255.1 %collective-permute-start.21 = (f32[1,1024,1024]{2,1,0:T(8,128)}, f32[1,1024,1024]{2,1,0:T(8,128)}, u32[]{:S(2)}, u32[]{:S(2)}) collective-permute-start(f32[1,1024,1024]{2,1,0:T(8,128)} %collective-permute-done.11.refs_0_), channel_id=1, source_target_pairs={{0,4},{2,6},{4,0},{6,2},{1,5},{3,7},{5,1},{7,3}} | collective-permute-start | bytes 12582920 | tf_op jit(solution)/shard_map/ppermute | solution.py:606
  792.4 249.2 %collective-permute-start.22 = (f32[1,1024,1024]{2,1,0:T(8,128)}, f32[1,1024,1024]{2,1,0:T(8,128)}, u32[]{:S(2)}, u32[]{:S(2)}) collective-permute-start(f32[1,1024,1024]{2,1,0:T(8,128)} %collective-permute-done.14.refs_1_), channel_id=1, source_target_pairs={{0,2},{2,0},{4,6},{6,4},{1,3},{3,1},{5,7},{7,5}} | collective-permute-start | bytes 12582920 | tf_op jit(solution)/shard_map/ppermute | solution.py:603
  953.0 89.1 %copy-start.15 = (bf16[4096]{0:T(1024)(128)(2,1)S(1)}, bf16[4096]{0:T(1024)(128)(2,1)}, u32[]{:S(2)}) copy-start(bf16[4096]{0:T(1024)(128)(2,1)} %param.33) | copy-start | bytes 24580
  953.0 89.7 %copy-start.3 = (f32[8,72,128]{2,1,0:T(8,128)S(1)}, f32[8,72,128]{2,1,0:T(8,128)}, u32[]{:S(2)}) copy-start(f32[8,72,128]{2,1,0:T(8,128)} %get-tuple-element.159) | copy-start | bytes 884740
  953.0 89.8 %copy-start.9 = (f32[8,8,128]{2,1,0:T(8,128)S(1)}, f32[8,8,128]{2,1,0:T(8,128)}, u32[]{:S(2)}) copy-start(f32[8,8,128]{2,1,0:T(8,128)} %get-tuple-element.158) | copy-start | bytes 98308
  1041.6 20.2 %collective-permute-start.23 = (f32[2,1024,1024]{2,1,0:T(8,128)}, f32[2,1024,1024]{2,1,0:T(8,128)}, u32[]{:S(2)}, u32[]{:S(2)}) collective-permute-start(f32[2,1024,1024]{2,1,0:T(8,128)} %collective-permute-done.19.refs_0_.refs_4_), channel_id=1, source_target_pairs={{0,1},{1,0},{2,3},{3,2},{4,5},{5,4},{6,7},{7,6}} | collective-permute-start | bytes 25165832 | tf_op jit(solution)/shard_map/ppermute | solution.py:609
  1041.6 25.5 %collective-permute-start.24 = (f32[2,1024,1024]{2,1,0:T(8,128)}, f32[2,1024,1024]{2,1,0:T(8,128)}, u32[]{:S(2)}, u32[]{:S(2)}) collective-permute-start(f32[2,1024,1024]{2,1,0:T(8,128)} %collective-permute-done.20.refs_1_.refs_5_), channel_id=1, source_target_pairs={{0,1},{1,0},{2,3},{3,2},{4,5},{5,4},{6,7},{7,6}} | collective-permute-start | bytes 25165832 | tf_op jit(solution)/shard_map/ppermute | solution.py:609
  1061.2 78.9 %collective-permute-start.25 = (f32[1,1024,1024]{2,1,0:T(8,128)}, f32[1,1024,1024]{2,1,0:T(8,128)}, u32[]{:S(2)}, u32[]{:S(2)}) collective-permute-start(f32[1,1024,1024]{2,1,0:T(8,128)} %collective-permute-done.21.refs_0_), channel_id=1, source_target_pairs={{0,1},{1,0},{2,3},{3,2},{4,5},{5,4},{6,7},{7,6}} | collective-permute-start | bytes 12582920 | tf_op jit(solution)/shard_map/ppermute | solution.py:609
  1061.2 78.9 %collective-permute-start.26 = (f32[1,1024,1024]{2,1,0:T(8,128)}, f32[1,1024,1024]{2,1,0:T(8,128)}, u32[]{:S(2)}, u32[]{:S(2)}) collective-permute-start(f32[1,1024,1024]{2,1,0:T(8,128)} %collective-permute-done.22.refs_1_), channel_id=1, source_target_pairs={{0,1},{1,0},{2,3},{3,2},{4,5},{5,4},{6,7},{7,6}} | collective-permute-start | bytes 12582920 | tf_op jit(solution)/shard_map/ppermute | solution.py:609
  1264.9 230.8 %copy-start.8 = (f32[10,1024]{1,0:T(8,128)}, f32[10,1024]{1,0:T(8,128)S(1)}, u32[]{:S(2)}) copy-start(f32[10,1024]{1,0:T(8,128)S(1)} %psum.58) | copy-start | bytes 122884
  1265.6 231.7 %copy-start.13 = (f32[1024]{0:T(1024)S(1)}, f32[1024]{0:T(1024)}, u32[]{:S(2)}) copy-start(f32[1024]{0:T(1024)} %param.31) | copy-start | bytes 12292
  1661.5 25.7 %copy-start.6 = (f32[2,8,4096]{2,1,0:T(8,128)S(1)}, f32[2,8,4096]{2,1,0:T(8,128)}, u32[]{:S(2)}) copy-start(f32[2,8,4096]{2,1,0:T(8,128)} %get-tuple-element.166) | copy-start | bytes 786436
  1661.5 31.7 %copy-start.2 = (f32[8,128,256]{2,1,0:T(8,128)S(1)}, f32[8,128,256]{2,1,0:T(8,128)}, u32[]{:S(2)}) copy-start(f32[8,128,256]{2,1,0:T(8,128)} %get-tuple-element.177) | copy-start | bytes 3145732
Sparse Core Ops, SparseCore 0:
  438.0 162.3 all-reduce.6
  1061.9 566.8 all-reduce.4

commit v5 on v4

--- a/solution.py
+++ b/solution.py
@@ -547,16 +547,10 @@
 
 def wide_kernel(n_pairs, flip, *refs):
     left, right, out_ref = refs[:n_pairs], refs[n_pairs:2 * n_pairs], refs[2 * n_pairs]
-
-    def column(c, _):
-        cols = pl.ds(pl.multiple_of(c * 256, 256), 256)
-        acc = 0.0
-        for lhs, rhs in zip(left, right):
-            acc = acc + lax.dot_general(lhs[...], rhs[cols, :] if flip else rhs[:, cols], CHAN if flip else ROW, preferred_element_type=F32)
-        out_ref[:, cols] = acc
-        return 0
-
-    lax.fori_loop(0, out_ref.shape[1] // 256, column, 0)
+    acc = 0.0
+    for lhs, rhs in zip(left, right):
+        acc = acc + lax.dot_general(lhs[...], rhs[...], CHAN if flip else ROW, preferred_element_type=F32)
+    out_ref[...] = acc
 
 
 def wide_product(lefts, rights, flip, first_row, rows):

time: 1710 us -> 1710 us (level)
  transfers between devices with their start and end apart: 29 -> 29, of which waited for: 8 -> 8; matrix products, arithmetic and copies ran while one was open for 9% -> 9% of each run, Pallas kernels for 77% -> 76%
where the time goes in v5:
time: 1710 us; the launch traced here: 1700 us
  Pallas kernels  1320 us (77%)
  waiting for transfers between devices  157 us (9%)
  matrix products  129 us (8%)
  starting transfers between devices  24.9 us (1%)
  other arithmetic  21 us (1%)
  local copies, waits for them, and re-layouts  20.4 us (1%)
    pallas_call x4, Pallas kernels, middle(): pl.pallas_call(functools.partial(middle_kernel, n_steps, n_tiles, n_tok,...  362 us
    pallas_call x6, Pallas kernels, up(): pl.pallas_call(functools.partial(up_kernel, n, n_parts, flip), grid=(n_ro...  352 us
    pallas_call x3, Pallas kernels, wide_product(): pl.pallas_call(functools.partial(wide_kernel, n, flip), grid=(rows // bm,...  265 us
    pallas_call x1, Pallas kernels, outputs(): pl.pallas_call(functools.partial(z_kernel, len(left), len(moved)), grid=(...  164 us
    dot_general x3, matrix products, token_product(): return lax.dot_general(lhs, rhs, TOK, preferred_element_type=F32)  129 us
    pallas_call x2, Pallas kernels, plain_up(): pl.pallas_call(functools.partial(plain_up_kernel, n, flip), grid=(width /...  124 us
    ppermute x6, waiting for transfers between devices, swap_y(): return lax.ppermute(v, 'tp', [(j, j ^ 2) for j in range(4)])  88 us
    ppermute x12, waiting for transfers between devices, swap_core(): return lax.ppermute(v, 'cp', [(0, 1), (1, 0)])  47.4 us
  transfers between devices with their start and end apart: 29, of which 8 were waited for; matrix products, arithmetic and copies ran while one was open for 9% of the time, Pallas kernels for 76%

profile of v5, /device:TPU:0, one launch (start us, length us, event | category | flops | bytes accessed | tf_op | source)
XLA Modules:
  0.0 1697.4 jit_solution(2544427438101134845)
XLA Ops:
  7.2 4.5 dynamic-slice_bitcast_fusion
  11.7 3.9 maximum_convert_fusion
  15.7 3.3 collective-permute-start.3
  19.0 1.5 collective-permute-start.5
  20.6 3.8 maximum_convert_fusion.1
  24.9 0.6 convert_add_fusion
  26.1 30.6 %normalize.1.lhs = bf16[4096,4096]{1,0:T(8,128)(2,1)} custom-call(bf16[4096,4096]{1,0:T(8,128)(2,1)} %bitcast.61, f32[1,4096]{1,0:T(1,128)} %bitcast.84), custom_call_target="tpu_custom_call" | custom-call | flops 10066329600 | bytes 67108864 | tf_op jit(solution)/shard_map/normalize/pallas_call | solution.py:369
  56.6 80.7 %plain_up.2 = (f32[4096,1024]{1,0:T(8,128)}, f32[4096,1024]{1,0:T(8,128)}) custom-call(bf16[4096,4096]{1,0:T(8,128)(2,1)} %normalize.1.lhs, bf16[4096,1024]{1,0:T(8,128)(2,1)} %refs_8_.1, bf16[4096,1024]{1,0:T(8,128)(2,1)} %refs_12_.1), custom_call_target="tpu_custom_call" | custom-call | flops 68719476736 | bytes 67108864 | tf_op jit(solution)/shard_map/plain_up/pallas_call | solution.py:389
  137.5 43.2 %plain_up.3.dm = f32[4096,1024]{1,0:T(8,128)} custom-call(bf16[4096,4096]{1,0:T(8,128)(2,1)} %bitcast.65, bf16[1024,4096]{1,0:T(8,128)(2,1)} %refs_4_.1), custom_call_target="tpu_custom_call" | custom-call | flops 34359738368 | bytes 67108864 | tf_op jit(solution)/shard_map/plain_up/pallas_call | solution.py:389
  180.7 1.3 concatenate.12.par_w
  182.0 2.2 broadcast_in_dim.11.pos_w
  184.2 124.3 %middle.4 = (bf16[4096,1024]{1,0:T(8,128)(2,1)}, bf16[4096,1024]{1,0:T(8,128)(2,1)}, bf16[4096,1024]{1,0:T(8,128)(2,1)}, f32[8,128,256]{2,1,0:T(8,128)}, f32[8,8,128]{2,1,0:T(8,128)}, /*index=5*/f32[8,72,128]{2,1,0:T(8,128)}) custom-call(s32[4,1024,128]{2,1,0:T(8,128)} %broadcast_in_dim.11.pos_w, f32[16,1024]{1,0:T(8,128)} %concatenate.12.par_w, ...), custom_call_target="tpu_custom_call" | custom-call | flops 6291456000 | bytes 75497472 | tf_op jit(solution)/shard_map/middle/pallas_call | solution.py:329
  308.6 44.3 %fusion.3 = f32[4096,1024]{1,0:T(8,128)} fusion(bf16[4096,4096]{1,0:T(8,128)(2,1)} %normalize.1.lhs, bf16[4096,1024]{1,0:T(8,128)(2,1)} %get-tuple-element.113.refs_1_.refs_4_), kind=kOutput, calls=%fused_computation.30 | convolution fusion | flops 34359738368 | bytes 58720256 | tf_op jit(solution)/shard_map/dot_general | solution.py:572
  352.8 42.4 %fusion.4 = f32[4096,1024]{1,0:T(8,128)} fusion(bf16[4096,4096]{1,0:T(8,128)(2,1)} %normalize.1.lhs, bf16[4096,1024]{1,0:T(8,128)(2,1)S(1)} %copy-done.22), kind=kOutput, calls=%fused_computation.31 | convolution fusion | flops 34359738368 | bytes 58720256 | tf_op jit(solution)/shard_map/dot_general | solution.py:572
  395.3 42.5 %fusion.5 = f32[1024,4096]{1,0:T(8,128)} fusion(bf16[4096,1024]{1,0:T(8,128)(2,1)S(1)} %bitcast.75, bf16[4096,4096]{1,0:T(8,128)(2,1)} %bitcast.66), kind=kOutput, calls=%fused_computation.32 | convolution fusion | flops 34359738368 | bytes 58720256 | tf_op jit(solution)/shard_map/dot_general | solution.py:572
  439.7 2.0 collective-permute-start
  441.8 8.6 bitcast_convert_fusion
  450.3 9.7 collective-permute-done.7.refs_2_.refs_6_
  460.0 2.4 collective-permute-start.1
  462.4 21.6 %collective-permute-done.8.refs_3_.refs_7_ = f32[2,1024,1024]{2,1,0:T(8,128)} collective-permute-done((f32[2,1024,1024]{2,1,0:T(8,128)}, f32[2,1024,1024]{2,1,0:T(8,128)}, u32[]{:S(2)}, u32[]{:S(2)}) %collective-permute-start.8) | collective-permute-done | bytes 8388640 | tf_op jit(solution)/shard_map/ppermute | solution.py:603
  484.0 2.3 collective-permute-start.11
  486.3 79.1 %up.6 = (f32[3072,1024]{1,0:T(8,128)}, f32[3072,1024]{1,0:T(8,128)}, bf16[4096,1024]{1,0:T(8,128)(2,1)}, bf16[4096,1024]{1,0:T(8,128)(2,1)}) custom-call(bf16[4096,4096]{1,0:T(8,128)(2,1)} %normalize.1.lhs, f32[2,1024,1024]{2,1,0:T(8,128)} %collective-permute-done.3.refs_0_.refs_4_, f32[2,1024,1024]{2,1,0:T(8,128)} %collective-permute-done.4.refs_1_.refs_5_, ...), custom_call_target="tpu_custom_call" | custom-call | flops 51539607552 | bytes 50331648 | tf_op jit(solution)/shard_map/up/pallas_call | solution.py:444
  565.4 1.7 collective-permute-start.13
  567.1 0.8 collective-permute-start.12
  568.0 76.6 %up.7 = (f32[3072,1024]{1,0:T(8,128)}, f32[3072,1024]{1,0:T(8,128)}, bf16[4096,1024]{1,0:T(8,128)(2,1)}, bf16[4096,1024]{1,0:T(8,128)(2,1)}) custom-call(bf16[4096,4096]{1,0:T(8,128)(2,1)} %normalize.1.lhs, f32[2,1024,1024]{2,1,0:T(8,128)} %collective-permute-done.5.refs_0_.refs_4_, f32[2,1024,1024]{2,1,0:T(8,128)} %collective-permute-done.6.refs_1_.refs_5_, ...), custom_call_target="tpu_custom_call" | custom-call | flops 51539607552 | bytes 50331648 | tf_op jit(solution)/shard_map/up/pallas_call | solution.py:444
  644.7 3.1 collective-permute-start.2
  647.8 23.3 %wide_product.3 = f32[1024,4096]{1,0:T(8,128)} custom-call(bf16[4096,1024]{1,0:T(8,128)(2,1)} %get-tuple-element.112.refs_0_, bf16[4096,1024]{1,0:T(8,128)(2,1)} %get-tuple-element.113.refs_1_.refs_4_, bf16[4096,1024]{1,0:T(8,128)(2,1)} %refs_8_.1, bf16[4096,1024]{1,0:T(8,128)(2,1)} %refs_12_.1), custom_call_target="tpu_custom_call" | custom-call | flops 17179869184 | bytes 450000000 | tf_op jit(solution)/shard_map/wide_product/pallas_call | solution.py:562
  671.1 21.4 %collective-permute-done.2 = f32[2176,128]{1,0:T(8,128)S(1)} collective-permute-done((f32[2176,128]{1,0:T(8,128)S(1)}, f32[2176,128]{1,0:T(8,128)S(1)}, u32[]{:S(2)}, u32[]{:S(2)}) %collective-permute-start.2) | collective-permute-done | bytes 1114144 | tf_op jit(solution)/shard_map/ppermute | solution.py:644
  692.7 1.7 collective-permute-start.20
  694.4 78.5 %collective-permute-done.14.refs_1_ = f32[1,1024,1024]{2,1,0:T(8,128)} collective-permute-done((f32[1,1024,1024]{2,1,0:T(8,128)}, f32[1,1024,1024]{2,1,0:T(8,128)}, u32[]{:S(2)}, u32[]{:S(2)}) %collective-permute-start.14) | collective-permute-done | bytes 4194336 | tf_op jit(solution)/shard_map/ppermute | solution.py:600
  773.4 1.3 slice_bitcast_fusion.2
  774.7 5.6 collective-permute-done.15.refs_2_
  780.5 1.9 copy-done.21
  782.4 0.8 slice.70
  783.2 0.6 reshape.109.par_w
  783.9 1.0 convert_element_type.61.wg_w
  784.8 0.6 reshape.110.par_w
  785.5 1.0 convert_element_type.63.wg_w
  786.4 1.7 collective-permute-start.21
  788.2 4.3 collective-permute-done.17.refs_2_
  793.0 40.5 %up.8 = (f32[3072,1024]{1,0:T(8,128)}, bf16[1024,4096]{1,0:T(8,128)(2,1)}) custom-call(bf16[4096,4096]{1,0:T(8,128)(2,1)} %bitcast.67, f32[1,1024,1024]{2,1,0:T(8,128)} %collective-permute-done.11.refs_0_, f32[1,1024,1024]{2,1,0:T(8,128)} %collective-permute-done.12.refs_1_, f32[1,1024,1024]{2,1,0:T(8,128)} %copy-done.21, ...), custom_call_target="tpu_custom_call" | custom-call | flops 25769803776 | bytes 50331648 | tf_op jit(solution)/shard_map/up/pallas_call | solution.py:444
  833.4 79.0 %middle.5 = (bf16[3072,1024]{1,0:T(8,128)(2,1)}, bf16[3072,1024]{1,0:T(8,128)(2,1)}, bf16[3072,1024]{1,0:T(8,128)(2,1)}) custom-call(s32[4,1024,128]{2,1,0:T(8,128)} %broadcast_in_dim.11.pos_w, f32[16,1024]{1,0:T(8,128)} %reshape.110.par_w, bf16[8,128,256]{2,1,0:T(8,128)(2,1)} %convert_element_type.63.wg_w, f32[3072,1024]{1,0:T(8,128)} %get-tuple-element.107.px, ...), custom_call_target="tpu_custom_call" | custom-call | flops 4718592000 | bytes 56623104 | tf_op jit(solution)/shard_map/middle/pallas_call | solution.py:329
  912.4 40.6 %up.9 = (f32[3072,1024]{1,0:T(8,128)}, bf16[1024,4096]{1,0:T(8,128)(2,1)}) custom-call(bf16[4096,4096]{1,0:T(8,128)(2,1)} %bitcast.68, f32[1,1024,1024]{2,1,0:T(8,128)} %collective-permute-done.13.refs_0_, f32[1,1024,1024]{2,1,0:T(8,128)} %collective-permute-done.14.refs_1_, f32[1,1024,1024]{2,1,0:T(8,128)} %collective-permute-done.17.refs_2_, ...), custom_call_target="tpu_custom_call" | custom-call | flops 25769803776 | bytes 50331648 | tf_op jit(solution)/shard_map/up/pallas_call | solution.py:444
  953.0 79.0 %middle.6 = (bf16[3072,1024]{1,0:T(8,128)(2,1)}, bf16[3072,1024]{1,0:T(8,128)(2,1)}, bf16[3072,1024]{1,0:T(8,128)(2,1)}) custom-call(s32[4,1024,128]{2,1,0:T(8,128)} %broadcast_in_dim.11.pos_w, f32[16,1024]{1,0:T(8,128)} %reshape.109.par_w, bf16[8,128,256]{2,1,0:T(8,128)(2,1)} %convert_element_type.61.wg_w, f32[3072,1024]{1,0:T(8,128)} %get-tuple-element.111.px, ...), custom_call_target="tpu_custom_call" | custom-call | flops 4718592000 | bytes 56623104 | tf_op jit(solution)/shard_map/middle/pallas_call | solution.py:329
  1032.1 9.5 collective-permute-done.21.refs_0_
  1042.1 0.6 reshape.127
  1042.9 0.6 reshape.113.par_w
  1043.6 1.0 convert_element_type.65.wg_w
  1044.6 15.7 wide_product.4
  1060.9 6.2 collective-permute-done.24.refs_3_.refs_7_
  1067.1 73.2 %up.10 = (f32[3072,1024]{1,0:T(8,128)}, f32[3072,1024]{1,0:T(8,128)}, bf16[4096,1024]{1,0:T(8,128)(2,1)}, bf16[4096,1024]{1,0:T(8,128)(2,1)}) custom-call(bf16[4096,4096]{1,0:T(8,128)(2,1)} %normalize.1.lhs, f32[2,1024,1024]{2,1,0:T(8,128)} %collective-permute-done.19.refs_0_.refs_4_, f32[2,1024,1024]{2,1,0:T(8,128)} %collective-permute-done.20.refs_1_.refs_5_, ...), custom_call_target="tpu_custom_call" | custom-call | flops 51539607552 | bytes 50331648 | tf_op jit(solution)/shard_map/up/pallas_call | solution.py:444
  1140.3 41.7 %up.11 = (f32[3072,1024]{1,0:T(8,128)}, bf16[1024,4096]{1,0:T(8,128)(2,1)}) custom-call(bf16[4096,4096]{1,0:T(8,128)(2,1)} %bitcast.69, f32[1,1024,1024]{2,1,0:T(8,128)} %collective-permute-done.21.refs_0_, f32[1,1024,1024]{2,1,0:T(8,128)} %collective-permute-done.22.refs_1_, f32[1,1024,1024]{2,1,0:T(8,128)} %collective-permute-done.25.refs_2_, ...), custom_call_target="tpu_custom_call" | custom-call | flops 25769803776 | bytes 50331648 | tf_op jit(solution)/shard_map/up/pallas_call | solution.py:444
  1182.0 79.5 %middle.7 = (bf16[3072,1024]{1,0:T(8,128)(2,1)}, bf16[3072,1024]{1,0:T(8,128)(2,1)}, bf16[3072,1024]{1,0:T(8,128)(2,1)}) custom-call(s32[4,1024,128]{2,1,0:T(8,128)} %broadcast_in_dim.11.pos_w, f32[16,1024]{1,0:T(8,128)} %reshape.113.par_w, bf16[8,128,256]{2,1,0:T(8,128)(2,1)} %convert_element_type.65.wg_w, f32[3072,1024]{1,0:T(8,128)} %get-tuple-element.136.px, ...), custom_call_target="tpu_custom_call" | custom-call | flops 4718592000 | bytes 56623104 | tf_op jit(solution)/shard_map/middle/pallas_call | solution.py:329
  1261.4 3.6 psum.58
  1265.0 0.6 slice.93
  1265.6 225.7 %wide_product.5.refs_10_ = f32[3072,4096]{1,0:T(8,128)} custom-call(bf16[4096,1024]{1,0:T(8,128)(2,1)} %get-tuple-element.112.refs_0_, bf16[3072,1024]{1,0:T(8,128)(2,1)} %get-tuple-element.146.refs_1_, bf16[3072,1024]{1,0:T(8,128)(2,1)} %get-tuple-element.147.refs_2_, bf16[3072,1024]{1,0:T(8,128)(2,1)} %get-tuple-element.148.refs_3_, ...), custom_call_target="tpu_custom_call" | custom-call | flops 206158430208 | bytes 450000000 | tf_op jit(solution)/shard_map/wide_product/pallas_call | solution.py:562
  1491.3 1.5 slice_multiply_fusion
  1492.9 0.6 divide_multiply_fusion
  1493.5 164.4 %outputs.1 = (bf16[4096,4096]{1,0:T(8,128)(2,1)}, bf16[4096,4096]{1,0:T(8,128)(2,1)}, f32[2,8,4096]{2,1,0:T(8,128)}, f32[4096,1024]{1,0:T(8,128)}, f32[4096,1024]{1,0:T(8,128)}, /*index=5*/f32[1024,4096]{1,0:T(8,128)}) custom-call(bf16[4096,1024]{1,0:T(8,128)(2,1)} %get-tuple-element.129.refs_0_, bf16[3072,1024]{1,0:T(8,128)(2,1)} %get-tuple-element.123.refs_1_, ...), custom_call_target="tpu_custom_call" | custom-call | flops 103079215104 | bytes 251658240 | tf_op jit(solution)/shard_map/outputs/pallas_call | solution.py:506
  1658.0 25.6 %tail_outputs.1 = (bf16[4096,4096]{1,0:T(8,128)(2,1)}, bf16[4096,4096]{1,0:T(8,128)(2,1)}, f32[2,8,4096]{2,1,0:T(8,128)}) custom-call(f32[1024,4096]{1,0:T(8,128)} %get-tuple-element.172.z_ref, f32[1,4096]{1,0:T(1,128)} %bitcast.88, f32[1024,4096]{1,0:T(8,128)} %get-tuple-element.173.dn_ref, ...), custom_call_target="tpu_custom_call", output_to_operand_aliasing={{0}: (6, {}), {1}: (7, {})} | custom-call | flops 6291456000 | bytes 67108864 | tf_op jit(solution)/shard_map/tail_outputs/pallas_call | solution.py:539
  1683.6 1.0 add_reduce_fusion
  1684.7 3.9 psum.62
  1688.6 0.6 fusion.2
  1689.2 1.1 fusion.1
  (118 shorter events, 5.8 us)
Async XLA Ops:
  7.2 1486.3 %all-reduce.7.cloned.1.call-start = ((), (), s32[]{:S(2)}) async-start(), calls=%async_computation.1 | async-start | bytes 102760448 | tf_op jit(solution)/shard_map/psum | solution.py:656
  15.6 9.3 copy-start.14
  15.6 9.9 copy-start.11
  15.6 10.2 copy-start.16
  15.6 10.2 copy-start.17
  15.6 10.2 copy-start.10
  15.7 10.3 copy-start.18
  15.7 10.3 copy-start.19
  15.7 10.3 copy-start.20
  15.7 10.3 copy-start.12
  15.7 10.3 copy-start.4
  15.7 422.1 %collective-permute-start.3 = (f32[2,1024,1024]{2,1,0:T(8,128)}, f32[2,1024,1024]{2,1,0:T(8,128)}, u32[]{:S(2)}, u32[]{:S(2)}) collective-permute-start(f32[2,1024,1024]{2,1,0:T(8,128)} %maximum_convert_fusion), channel_id=1, source_target_pairs={{0,2},{2,0},{4,6},{6,4},{1,3},{3,1},{5,7},{7,5}} | collective-permute-start | bytes 25165832 | tf_op jit(solution)/shard_map/ppermute | solution.py:597
  19.0 418.8 %collective-permute-start.5 = (f32[2,1024,1024]{2,1,0:T(8,128)}, f32[2,1024,1024]{2,1,0:T(8,128)}, u32[]{:S(2)}, u32[]{:S(2)}) collective-permute-start(f32[2,1024,1024]{2,1,0:T(8,128)} %maximum_convert_fusion), channel_id=1, source_target_pairs={{0,4},{2,6},{4,0},{6,2},{1,5},{3,7},{5,1},{7,3}} | collective-permute-start | bytes 25165832 | tf_op jit(solution)/shard_map/ppermute | solution.py:600
  24.4 413.4 %collective-permute-start.4 = (f32[2,1024,1024]{2,1,0:T(8,128)}, f32[2,1024,1024]{2,1,0:T(8,128)}, u32[]{:S(2)}, u32[]{:S(2)}) collective-permute-start(f32[2,1024,1024]{2,1,0:T(8,128)} %maximum_convert_fusion.1), channel_id=1, source_target_pairs={{0,2},{2,0},{4,6},{6,4},{1,3},{3,1},{5,7},{7,5}} | collective-permute-start | bytes 25165832 | tf_op jit(solution)/shard_map/ppermute | solution.py:597
  24.9 412.9 %collective-permute-start.6 = (f32[2,1024,1024]{2,1,0:T(8,128)}, f32[2,1024,1024]{2,1,0:T(8,128)}, u32[]{:S(2)}, u32[]{:S(2)}) collective-permute-start(f32[2,1024,1024]{2,1,0:T(8,128)} %maximum_convert_fusion.1), channel_id=1, source_target_pairs={{0,4},{2,6},{4,0},{6,2},{1,5},{3,7},{5,1},{7,3}} | collective-permute-start | bytes 25165832 | tf_op jit(solution)/shard_map/ppermute | solution.py:600
  56.6 80.7 %copy-start.5 = (bf16[8,128,128]{2,1,0:T(8,128)(2,1)S(1)}, bf16[8,128,128]{2,1,0:T(8,128)(2,1)}, u32[]{:S(2)}) copy-start(bf16[8,128,128]{2,1,0:T(8,128)(2,1)} %param.29) | copy-start | bytes 786436
  137.5 43.2 %copy-start = (bf16[8,128,256]{2,1,0:T(8,128)(2,1)}, bf16[8,128,256]{2,1,0:T(8,128)(2,1)S(1)}, u32[]{:S(2)}) copy-start(bf16[8,128,256]{2,1,0:T(8,128)(2,1)S(1)} %constant_dynamic-update-slice_fusion.wg_w) | copy-start | bytes 1572868
  308.5 44.3 %copy-start.22 = (bf16[4096,1024]{1,0:T(8,128)(2,1)S(1)}, bf16[4096,1024]{1,0:T(8,128)(2,1)}, u32[]{:S(2)}) copy-start(bf16[4096,1024]{1,0:T(8,128)(2,1)} %get-tuple-element.112.refs_0_) | copy-start | bytes 25165828
  308.5 86.7 %slice-start = ((s8[8388608]{0:T(1024)(128)(4,1)}), s8[4194304]{0:T(1024)(128)(4,1)S(1)}, s32[]{:S(2)}) async-start(s8[8388608]{0:T(1024)(128)(4,1)} %bitcast.74), calls=%async_computation.2 | async-start | bytes 8388608
  352.8 42.4 %slice-start.1 = ((s8[8388608]{0:T(1024)(128)(4,1)}), s8[4194304]{0:T(1024)(128)(4,1)S(1)}, s32[]{:S(2)}) async-start(s8[8388608]{0:T(1024)(128)(4,1)} %bitcast.74), calls=%async_computation.3 | async-start | bytes 8388608
  437.8 1.1 copy-start.1
  437.8 1.8 copy-start.7
  437.9 1220.1 %all-reduce.5.cloned.1.call-start = ((), (), s32[]{:S(2)}) async-start(), calls=%async_computation | async-start | bytes 67108864 | tf_op jit(solution)/shard_map/psum | solution.py:672
  437.9 22.0 %collective-permute-start.7 = (f32[2,1024,1024]{2,1,0:T(8,128)}, f32[2,1024,1024]{2,1,0:T(8,128)}, u32[]{:S(2)}, u32[]{:S(2)}) collective-permute-start(f32[2,1024,1024]{2,1,0:T(8,128)} %collective-permute-done.3.refs_0_.refs_4_), channel_id=1, source_target_pairs={{0,1},{1,0},{2,3},{3,2},{4,5},{5,4},{6,7},{7,6}} | collective-permute-start | bytes 25165832 | tf_op jit(solution)/shard_map/ppermute | solution.py:603
  438.0 46.0 %collective-permute-start.8 = (f32[2,1024,1024]{2,1,0:T(8,128)}, f32[2,1024,1024]{2,1,0:T(8,128)}, u32[]{:S(2)}, u32[]{:S(2)}) collective-permute-start(f32[2,1024,1024]{2,1,0:T(8,128)} %collective-permute-done.4.refs_1_.refs_5_), channel_id=1, source_target_pairs={{0,1},{1,0},{2,3},{3,2},{4,5},{5,4},{6,7},{7,6}} | collective-permute-start | bytes 25165832 | tf_op jit(solution)/shard_map/ppermute | solution.py:603
  438.5 128.7 %collective-permute-start.9 = (f32[2,1024,1024]{2,1,0:T(8,128)}, f32[2,1024,1024]{2,1,0:T(8,128)}, u32[]{:S(2)}, u32[]{:S(2)}) collective-permute-start(f32[2,1024,1024]{2,1,0:T(8,128)} %collective-permute-done.5.refs_0_.refs_4_), channel_id=1, source_target_pairs={{0,1},{1,0},{2,3},{3,2},{4,5},{5,4},{6,7},{7,6}} | collective-permute-start | bytes 25165832 | tf_op jit(solution)/shard_map/ppermute | solution.py:603
  438.5 129.5 %collective-permute-start.10 = (f32[2,1024,1024]{2,1,0:T(8,128)}, f32[2,1024,1024]{2,1,0:T(8,128)}, u32[]{:S(2)}, u32[]{:S(2)}) collective-permute-start(f32[2,1024,1024]{2,1,0:T(8,128)} %collective-permute-done.6.refs_1_.refs_5_), channel_id=1, source_target_pairs={{0,1},{1,0},{2,3},{3,2},{4,5},{5,4},{6,7},{7,6}} | collective-permute-start | bytes 25165832 | tf_op jit(solution)/shard_map/ppermute | solution.py:603
  439.7 125.7 %collective-permute-start = (f32[2176,128]{1,0:T(8,128)S(1)}, f32[2176,128]{1,0:T(8,128)S(1)}, u32[]{:S(2)}, u32[]{:S(2)}) collective-permute-start(f32[2176,128]{1,0:T(8,128)S(1)} %maximum_bitcast_fusion), channel_id=1, source_target_pairs={{0,2},{2,0},{4,6},{6,4},{1,3},{3,1},{5,7},{7,5}} | collective-permute-start | bytes 3342344 | tf_op jit(solution)/shard_map/ppermute | solution.py:644
  460.0 184.7 %collective-permute-start.1 = (f32[2176,128]{1,0:T(8,128)S(1)}, f32[2176,128]{1,0:T(8,128)}, u32[]{:S(2)}, u32[]{:S(2)}) collective-permute-start(f32[2176,128]{1,0:T(8,128)S(1)} %maximum_bitcast_fusion), channel_id=1, source_target_pairs={{0,4},{2,6},{4,0},{6,2},{1,5},{3,7},{5,1},{7,3}} | collective-permute-start | bytes 3342344 | tf_op jit(solution)/shard_map/ppermute | solution.py:644
  484.0 208.7 %collective-permute-start.11 = (f32[1,1024,1024]{2,1,0:T(8,128)}, f32[1,1024,1024]{2,1,0:T(8,128)}, u32[]{:S(2)}, u32[]{:S(2)}) collective-permute-start(f32[1,1024,1024]{2,1,0:T(8,128)} %get-tuple-element.179), channel_id=1, source_target_pairs={{0,2},{2,0},{4,6},{6,4},{1,3},{3,1},{5,7},{7,5}} | collective-permute-start | bytes 12582920 | tf_op jit(solution)/shard_map/ppermute | solution.py:597
  565.4 129.1 %collective-permute-start.13 = (f32[1,1024,1024]{2,1,0:T(8,128)}, f32[1,1024,1024]{2,1,0:T(8,128)}, u32[]{:S(2)}, u32[]{:S(2)}) collective-permute-start(f32[1,1024,1024]{2,1,0:T(8,128)} %get-tuple-element.179), channel_id=1, source_target_pairs={{0,4},{2,6},{4,0},{6,2},{1,5},{3,7},{5,1},{7,3}} | collective-permute-start | bytes 12582920 | tf_op jit(solution)/shard_map/ppermute | solution.py:600
  567.1 127.3 %collective-permute-start.12 = (f32[1,1024,1024]{2,1,0:T(8,128)}, f32[1,1024,1024]{2,1,0:T(8,128)}, u32[]{:S(2)}, u32[]{:S(2)}) collective-permute-start(f32[1,1024,1024]{2,1,0:T(8,128)} %get-tuple-element.178), channel_id=1, source_target_pairs={{0,2},{2,0},{4,6},{6,4},{1,3},{3,1},{5,7},{7,5}} | collective-permute-start | bytes 12582920 | tf_op jit(solution)/shard_map/ppermute | solution.py:597
  568.0 205.0 %collective-permute-start.14 = (f32[1,1024,1024]{2,1,0:T(8,128)}, f32[1,1024,1024]{2,1,0:T(8,128)}, u32[]{:S(2)}, u32[]{:S(2)}) collective-permute-start(f32[1,1024,1024]{2,1,0:T(8,128)} %get-tuple-element.178), channel_id=1, source_target_pairs={{0,4},{2,6},{4,0},{6,2},{1,5},{3,7},{5,1},{7,3}} | collective-permute-start | bytes 12582920 | tf_op jit(solution)/shard_map/ppermute | solution.py:600
  644.7 47.8 %collective-permute-start.2 = (f32[2176,128]{1,0:T(8,128)S(1)}, f32[2176,128]{1,0:T(8,128)S(1)}, u32[]{:S(2)}, u32[]{:S(2)}) collective-permute-start(f32[2176,128]{1,0:T(8,128)S(1)} %maximum_bitcast_fusion), channel_id=1, source_target_pairs={{0,6},{2,4},{4,2},{6,0},{1,7},{3,5},{5,3},{7,1}} | collective-permute-start | bytes 3342344 | tf_op jit(solution)/shard_map/ppermute | solution.py:644
  692.5 339.6 %collective-permute-start.19 = (f32[2,1024,1024]{2,1,0:T(8,128)}, f32[2,1024,1024]{2,1,0:T(8,128)}, u32[]{:S(2)}, u32[]{:S(2)}) collective-permute-start(f32[2,1024,1024]{2,1,0:T(8,128)} %collective-permute-done.3.refs_0_.refs_4_), channel_id=1, source_target_pairs={{0,4},{2,6},{4,0},{6,2},{1,5},{3,7},{5,1},{7,3}} | collective-permute-start | bytes 25165832 | tf_op jit(solution)/shard_map/ppermute | solution.py:600
  692.7 339.4 %collective-permute-start.20 = (f32[2,1024,1024]{2,1,0:T(8,128)}, f32[2,1024,1024]{2,1,0:T(8,128)}, u32[]{:S(2)}, u32[]{:S(2)}) collective-permute-start(f32[2,1024,1024]{2,1,0:T(8,128)} %collective-permute-done.6.refs_1_.refs_5_), channel_id=1, source_target_pairs={{0,2},{2,0},{4,6},{6,4},{1,3},{3,1},{5,7},{7,5}} | collective-permute-start | bytes 25165832 | tf_op jit(solution)/shard_map/ppermute | solution.py:597
  772.9 7.4 collective-permute-start.15
  772.9 13.5 collective-permute-start.16
  773.4 19.0 %collective-permute-start.17 = (f32[1,1024,1024]{2,1,0:T(8,128)}, f32[1,1024,1024]{2,1,0:T(8,128)}, u32[]{:S(2)}, u32[]{:S(2)}) collective-permute-start(f32[1,1024,1024]{2,1,0:T(8,128)} %collective-permute-done.13.refs_0_), channel_id=1, source_target_pairs={{0,1},{1,0},{2,3},{3,2},{4,5},{5,4},{6,7},{7,6}} | collective-permute-start | bytes 12582920 | tf_op jit(solution)/shard_map/ppermute | solution.py:603
  780.3 2.1 copy-start.21
  780.3 132.1 %collective-permute-start.18 = (f32[1,1024,1024]{2,1,0:T(8,128)}, f32[1,1024,1024]{2,1,0:T(8,128)}, u32[]{:S(2)}, u32[]{:S(2)}) collective-permute-start(f32[1,1024,1024]{2,1,0:T(8,128)} %collective-permute-done.14.refs_1_), channel_id=1, source_target_pairs={{0,1},{1,0},{2,3},{3,2},{4,5},{5,4},{6,7},{7,6}} | collective-permute-start | bytes 12582920 | tf_op jit(solution)/shard_map/ppermute | solution.py:603
  786.4 255.1 %collective-permute-start.21 = (f32[1,1024,1024]{2,1,0:T(8,128)}, f32[1,1024,1024]{2,1,0:T(8,128)}, u32[]{:S(2)}, u32[]{:S(2)}) collective-permute-start(f32[1,1024,1024]{2,1,0:T(8,128)} %collective-permute-done.11.refs_0_), channel_id=1, source_target_pairs={{0,4},{2,6},{4,0},{6,2},{1,5},{3,7},{5,1},{7,3}} | collective-permute-start | bytes 12582920 | tf_op jit(solution)/shard_map/ppermute | solution.py:600
  792.4 249.2 %collective-permute-start.22 = (f32[1,1024,1024]{2,1,0:T(8,128)}, f32[1,1024,1024]{2,1,0:T(8,128)}, u32[]{:S(2)}, u32[]{:S(2)}) collective-permute-start(f32[1,1024,1024]{2,1,0:T(8,128)} %collective-permute-done.14.refs_1_), channel_id=1, source_target_pairs={{0,2},{2,0},{4,6},{6,4},{1,3},{3,1},{5,7},{7,5}} | collective-permute-start | bytes 12582920 | tf_op jit(solution)/shard_map/ppermute | solution.py:597
  953.0 89.1 %copy-start.15 = (bf16[4096]{0:T(1024)(128)(2,1)S(1)}, bf16[4096]{0:T(1024)(128)(2,1)}, u32[]{:S(2)}) copy-start(bf16[4096]{0:T(1024)(128)(2,1)} %param.33) | copy-start | bytes 24580
  953.0 89.7 %copy-start.3 = (f32[8,72,128]{2,1,0:T(8,128)S(1)}, f32[8,72,128]{2,1,0:T(8,128)}, u32[]{:S(2)}) copy-start(f32[8,72,128]{2,1,0:T(8,128)} %get-tuple-element.159) | copy-start | bytes 884740
  953.0 89.8 %copy-start.9 = (f32[8,8,128]{2,1,0:T(8,128)S(1)}, f32[8,8,128]{2,1,0:T(8,128)}, u32[]{:S(2)}) copy-start(f32[8,8,128]{2,1,0:T(8,128)} %get-tuple-element.158) | copy-start | bytes 98308
  1041.6 19.3 %collective-permute-start.23 = (f32[2,1024,1024]{2,1,0:T(8,128)}, f32[2,1024,1024]{2,1,0:T(8,128)}, u32[]{:S(2)}, u32[]{:S(2)}) collective-permute-start(f32[2,1024,1024]{2,1,0:T(8,128)} %collective-permute-done.19.refs_0_.refs_4_), channel_id=1, source_target_pairs={{0,1},{1,0},{2,3},{3,2},{4,5},{5,4},{6,7},{7,6}} | collective-permute-start | bytes 25165832 | tf_op jit(solution)/shard_map/ppermute | solution.py:603
  1041.6 25.5 %collective-permute-start.24 = (f32[2,1024,1024]{2,1,0:T(8,128)}, f32[2,1024,1024]{2,1,0:T(8,128)}, u32[]{:S(2)}, u32[]{:S(2)}) collective-permute-start(f32[2,1024,1024]{2,1,0:T(8,128)} %collective-permute-done.20.refs_1_.refs_5_), channel_id=1, source_target_pairs={{0,1},{1,0},{2,3},{3,2},{4,5},{5,4},{6,7},{7,6}} | collective-permute-start | bytes 25165832 | tf_op jit(solution)/shard_map/ppermute | solution.py:603
  1060.3 79.9 %collective-permute-start.25 = (f32[1,1024,1024]{2,1,0:T(8,128)}, f32[1,1024,1024]{2,1,0:T(8,128)}, u32[]{:S(2)}, u32[]{:S(2)}) collective-permute-start(f32[1,1024,1024]{2,1,0:T(8,128)} %collective-permute-done.21.refs_0_), channel_id=1, source_target_pairs={{0,1},{1,0},{2,3},{3,2},{4,5},{5,4},{6,7},{7,6}} | collective-permute-start | bytes 12582920 | tf_op jit(solution)/shard_map/ppermute | solution.py:603
  1060.3 79.9 %collective-permute-start.26 = (f32[1,1024,1024]{2,1,0:T(8,128)}, f32[1,1024,1024]{2,1,0:T(8,128)}, u32[]{:S(2)}, u32[]{:S(2)}) collective-permute-start(f32[1,1024,1024]{2,1,0:T(8,128)} %collective-permute-done.22.refs_1_), channel_id=1, source_target_pairs={{0,1},{1,0},{2,3},{3,2},{4,5},{5,4},{6,7},{7,6}} | collective-permute-start | bytes 12582920 | tf_op jit(solution)/shard_map/ppermute | solution.py:603
  1265.0 226.3 %copy-start.8 = (f32[10,1024]{1,0:T(8,128)}, f32[10,1024]{1,0:T(8,128)S(1)}, u32[]{:S(2)}) copy-start(f32[10,1024]{1,0:T(8,128)S(1)} %psum.58) | copy-start | bytes 122884
  1265.6 227.2 %copy-start.13 = (f32[1024]{0:T(1024)S(1)}, f32[1024]{0:T(1024)}, u32[]{:S(2)}) copy-start(f32[1024]{0:T(1024)} %param.31) | copy-start | bytes 12292
  1657.9 25.7 %copy-start.6 = (f32[2,8,4096]{2,1,0:T(8,128)S(1)}, f32[2,8,4096]{2,1,0:T(8,128)}, u32[]{:S(2)}) copy-start(f32[2,8,4096]{2,1,0:T(8,128)} %get-tuple-element.166) | copy-start | bytes 786436
  1658.0 31.3 %copy-start.2 = (f32[8,128,256]{2,1,0:T(8,128)S(1)}, f32[8,128,256]{2,1,0:T(8,128)}, u32[]{:S(2)}) copy-start(f32[8,128,256]{2,1,0:T(8,128)} %get-tuple-element.177) | copy-start | bytes 3145732
Sparse Core Ops, SparseCore 0:
  438.0 162.3 all-reduce.6
  1061.0 566.8 all-reduce.4
